TPU v7x, 32 devices: a whole 2x2x4 slice. The times are simulated.
32 devices in a mesh: rep: 2 (over y), shard: 16 (over z, x, core).
Axes of the slice: x: 2, y: 2, z: 4, core: 2. Of those that a mesh axis runs over, the one named last changes fastest.
Arguments:
- tokens: bfloat16 [2, 3072, 768], P('rep', 'shard'), may hold values from -6 to 6
- segments: int32 [2, 3072], P('rep', 'shard'), may hold values from 0 to 16, never falling along the last dimension, each value on 1 to 2304 neighbouring positions
- padding: int32 [2, 3072], P('rep', 'shard'), may hold values from 0 to 1, as said below
- query_weight: float32 [768, 768], P('shard'), may hold values from -0.21875 to 0.21875
- key_weight: float32 [768, 768], P('shard'), may hold values from -0.21875 to 0.21875
- value_weight: float32 [768, 768], P('shard'), may hold values from -0.21875 to 0.21875
- query_bias: float32 [768], P('shard'), may hold values from -3 to 3
- value_bias: float32 [768], P('shard'), may hold values from -3 to 3
- out_weight: float32 [768, 768], P('shard'), may hold values from -0.875 to 0.875
- out_bias: float32 [768], P('shard'), may hold values from -3 to 3
- middle_gain: float32 [768], P('shard'), may hold values from 0.5 to 1.5
- middle_shift: float32 [768], P('shard'), may hold values from -3 to 3
- up_weight: float32 [768, 3072], P('shard'), may hold values from -0.21875 to 0.21875
- up_bias: float32 [3072], P('shard'), may hold values from -3 to 3
- down_weight: float32 [3072, 768], P('shard'), may hold values from -0.109375 to 0.109375
- down_bias: float32 [768], P('shard'), may hold values from -3 to 3
- final_gain: float32 [768], P('shard'), may hold values from 0.5 to 1.5
- final_shift: float32 [768], P('shard'), may hold values from -3 to 3
- cotangent: bfloat16 [2, 3072, 768], P('rep', 'shard'), may hold values from -6 to 6
Outputs:
- output: bfloat16 [2, 3072, 768], P('rep', 'shard')
- grad_tokens: bfloat16 [2, 3072, 768], P('rep', 'shard')
- grad_query_weight: float32 [768, 768], P('shard')
- grad_key_weight: float32 [768, 768], P('shard')
- grad_value_weight: float32 [768, 768], P('shard')
- grad_query_bias: float32 [768], P('shard')
- grad_value_bias: float32 [768], P('shard')
- grad_out_weight: float32 [768, 768], P('shard')
- grad_out_bias: float32 [768], P('shard')
- grad_middle_gain: float32 [768], P('shard')
- grad_middle_shift: float32 [768], P('shard')
- grad_up_weight: float32 [768, 3072], P('shard')
- grad_up_bias: float32 [3072], P('shard')
- grad_down_weight: float32 [3072, 768], P('shard')
- grad_down_bias: float32 [768], P('shard')
- grad_final_gain: float32 [768], P('shard')
- grad_final_shift: float32 [768], P('shard')
Inputs may be any that keep to these rules, and one draw needn't show every extreme that they name: `segments`: within each sequence the numbers never fall; every document has 1 to 2304 tokens and one has exactly 2304. Each sequence ends with a run of at least one padding token and has no other padding.
All inputs are finite; a program needn't handle non-finite values.
Results may differ from a plain program's by a relative error of at most 0.024.
Values may be sent and summed in bfloat16 or wider, within the bound.
A program may use at most 256 MiB of HBM per device.

v0:
```python
import jax
import jax.numpy as jnp
from jax import lax
from jax.sharding import PartitionSpec as P

D = 768
HEADS = 12
HEAD_DIM = 64


epsilon = 1e-12
very_low = -1e30
block_size = 512
root_half = 0.7071067811865476
inv_root_tau = 0.3989422804014327


def split_size():
    return block_size


def over_blocks(update, initial, arrays, total_rows):
    length = split_size()
    number = total_rows // length
    split = tuple((item.reshape((number, length) + item.shape[1:]) for item in arrays))

    def advance(carried, pieces):
        return (update(carried, pieces), None)

    return lax.scan(advance, initial, split)[0]


def scan_blocks(step, initial, arrays, total_rows):
    length = split_size()
    number = total_rows // length
    split = tuple((item.reshape((number, length) + item.shape[1:]) for item in arrays))
    final, produced = lax.scan(step, initial, split)
    return (final, produced.reshape((total_rows,) + produced.shape[2:]))


def guarded_update(update):

    def run_update(carried, pieces):
        return update(carried, pieces)

    return run_update


def guarded_step(step):

    def run_step(carried, pieces):
        return step(carried, pieces)

    return run_step


def norm_forward(value, gain, shift):
    center = value - jnp.mean(value, axis=-1, keepdims=True)
    spread = jnp.mean(center * center, axis=-1, keepdims=True)
    scale = lax.rsqrt(spread + epsilon)
    normal = center * scale
    return (normal * gain + shift, normal, scale)


def norm_backward(upstream, normal, scale, gain):
    inner = upstream * gain
    return scale * (
        inner
        - jnp.mean(inner, axis=-1, keepdims=True)
        - normal * jnp.mean(inner * normal, axis=-1, keepdims=True)
    )


def gelu_slope(hidden):
    return 0.5 * (1.0 + lax.erf(hidden * root_half)) + hidden * inv_root_tau * jnp.exp(
        -0.5 * hidden * hidden
    )


def score_grads(
    queries, query_codes, log_rows, delta_rows, dctx_rows, key_rows, value_rows, key_codes
):
    raw_scores = (
        jnp.einsum("qhd,khd->hqk", queries, key_rows, preferred_element_type=jnp.float32) * 0.125
    )
    allowed = (query_codes[:, None] == key_codes[None, :])[None]
    chances = jnp.where(allowed, jnp.exp(raw_scores - log_rows[:, :, None]), 0.0)
    d_chance = jnp.einsum("qhd,khd->hqk", dctx_rows, value_rows, preferred_element_type=jnp.float32)
    d_score = (chances * (d_chance - delta_rows[:, :, None])).astype(jnp.bfloat16)
    return (chances, d_score)


def forward_update(queries, codes_here):

    def update(carried, pieces):
        running_top, running_total, context_sum = carried
        key_rows, value_rows, key_codes = pieces
        raw_scores = (
            jnp.einsum("qhd,khd->hqk", queries, key_rows, preferred_element_type=jnp.float32)
            * 0.125
        )
        allowed = (codes_here[:, None] == key_codes[None, :])[None]
        masked = jnp.where(allowed, raw_scores, very_low)
        new_top = jnp.maximum(running_top, jnp.max(masked, axis=2))
        rescale = jnp.exp(running_top - new_top)
        weights = jnp.where(allowed, jnp.exp(masked - new_top[:, :, None]), 0.0)
        new_total = running_total * rescale + jnp.sum(weights, axis=2)
        added = jnp.einsum(
            "hqk,khd->qhd",
            weights.astype(jnp.bfloat16),
            value_rows,
            preferred_element_type=jnp.float32,
        )
        return (new_top, new_total, context_sum * rescale.T[:, :, None] + added)

    return guarded_update(update)


def shards(
    tokens,
    segments,
    padding,
    query_weight,
    key_weight,
    value_weight,
    query_bias,
    value_bias,
    out_weight,
    out_bias,
    middle_gain,
    middle_shift,
    up_weight,
    up_bias,
    down_weight,
    down_bias,
    final_gain,
    final_shift,
    cotangent,
):
    w_query, w_key, w_value, w_out, b_query, b_value, b_out, gain_mid, shift_mid = (
        lax.all_gather(query_weight.astype(jnp.bfloat16), "shard", axis=0, tiled=True),
        lax.all_gather(key_weight.astype(jnp.bfloat16), "shard", axis=0, tiled=True),
        lax.all_gather(value_weight.astype(jnp.bfloat16), "shard", axis=0, tiled=True),
        lax.all_gather(out_weight.astype(jnp.bfloat16), "shard", axis=0, tiled=True),
        lax.all_gather(query_bias.astype(jnp.bfloat16), "shard", axis=0, tiled=True),
        lax.all_gather(value_bias.astype(jnp.bfloat16), "shard", axis=0, tiled=True),
        lax.all_gather(out_bias.astype(jnp.bfloat16), "shard", axis=0, tiled=True),
        lax.all_gather(middle_gain.astype(jnp.bfloat16), "shard", axis=0, tiled=True),
        lax.all_gather(middle_shift.astype(jnp.bfloat16), "shard", axis=0, tiled=True),
    )
    w_up, b_up, w_down, b_down, gain_end, shift_end = (
        lax.all_gather(up_weight.astype(jnp.bfloat16), "shard", axis=0, tiled=True),
        lax.all_gather(up_bias.astype(jnp.bfloat16), "shard", axis=0, tiled=True),
        lax.all_gather(down_weight.astype(jnp.bfloat16), "shard", axis=0, tiled=True),
        lax.all_gather(down_bias.astype(jnp.bfloat16), "shard", axis=0, tiled=True),
        lax.all_gather(final_gain.astype(jnp.bfloat16), "shard", axis=0, tiled=True),
        lax.all_gather(final_shift.astype(jnp.bfloat16), "shard", axis=0, tiled=True),
    )
    own_tokens = tokens[0]
    here_rows = own_tokens.shape[0]
    own_codes = 2 * segments[0] + padding[0]
    all_codes = lax.all_gather(own_codes, "shard", axis=0, tiled=True)
    queries_flat = (
        jnp.dot(own_tokens, w_query, preferred_element_type=jnp.float32)
        + b_query.astype(jnp.float32)
    ).astype(jnp.bfloat16)
    keys_flat = jnp.dot(own_tokens, w_key, preferred_element_type=jnp.float32).astype(jnp.bfloat16)
    values_flat = (
        jnp.dot(own_tokens, w_value, preferred_element_type=jnp.float32)
        + b_value.astype(jnp.float32)
    ).astype(jnp.bfloat16)
    keys_all, values_all = (
        lax.all_gather(keys_flat, "shard", axis=0, tiled=True),
        lax.all_gather(values_flat, "shard", axis=0, tiled=True),
    )
    seq_rows = keys_all.shape[0]
    queries = queries_flat.reshape(here_rows, HEADS, HEAD_DIM)
    key_heads = keys_all.reshape(seq_rows, HEADS, HEAD_DIM)
    value_heads = values_all.reshape(seq_rows, HEADS, HEAD_DIM)
    start_state = (
        jnp.full((HEADS, here_rows), very_low, jnp.float32),
        jnp.zeros((HEADS, here_rows), jnp.float32),
        jnp.zeros((here_rows, HEADS, HEAD_DIM), jnp.float32),
    )
    best_score, total_weight, context_sum = over_blocks(
        forward_update(queries, own_codes),
        start_state,
        (key_heads, value_heads, all_codes),
        seq_rows,
    )
    log_total = best_score + jnp.log(total_weight)
    context = (context_sum / total_weight.T[:, :, None]).reshape(here_rows, D)
    context_low = context.astype(jnp.bfloat16)
    branch = jnp.dot(context_low, w_out, preferred_element_type=jnp.float32) + b_out.astype(
        jnp.float32
    )
    middle, normal_mid, scale_mid = norm_forward(
        own_tokens.astype(jnp.float32) + branch,
        gain_mid.astype(jnp.float32),
        shift_mid.astype(jnp.float32),
    )
    middle_low = middle.astype(jnp.bfloat16)
    hidden = jnp.dot(middle_low, w_up, preferred_element_type=jnp.float32) + b_up.astype(
        jnp.float32
    )
    active_low = jax.nn.gelu(hidden, approximate=False).astype(jnp.bfloat16)
    feed = jnp.dot(active_low, w_down, preferred_element_type=jnp.float32) + b_down.astype(
        jnp.float32
    )
    result, normal_end, scale_end = norm_forward(
        middle + feed, gain_end.astype(jnp.float32), shift_end.astype(jnp.float32)
    )
    output = result.astype(jnp.bfloat16)[None]
    upstream = cotangent[0].astype(jnp.float32)
    grad_gain_end = jnp.sum(upstream * normal_end, axis=0)
    grad_shift_end = jnp.sum(upstream, axis=0)
    d_second = norm_backward(upstream, normal_end, scale_end, gain_end.astype(jnp.float32))
    feed_low = d_second.astype(jnp.bfloat16)
    grad_down = lax.psum_scatter(
        jnp.einsum("tf,td->fd", active_low, feed_low, preferred_element_type=jnp.float32).astype(
            jnp.bfloat16
        ),
        "shard",
        scatter_dimension=0,
        tiled=True,
    )
    d_active = jnp.einsum("td,fd->tf", feed_low, w_down, preferred_element_type=jnp.float32)
    up_low = (d_active * gelu_slope(hidden)).astype(jnp.bfloat16)
    grad_up = lax.psum_scatter(
        jnp.einsum("td,tf->df", middle_low, up_low, preferred_element_type=jnp.float32).astype(
            jnp.bfloat16
        ),
        "shard",
        scatter_dimension=0,
        tiled=True,
    )
    d_middle = jnp.einsum("tf,df->td", up_low, w_up, preferred_element_type=jnp.float32) + d_second
    grad_gain_mid = jnp.sum(d_middle * normal_mid, axis=0)
    grad_shift_mid = jnp.sum(d_middle, axis=0)
    d_first = norm_backward(d_middle, normal_mid, scale_mid, gain_mid.astype(jnp.float32))
    branch_low = d_first.astype(jnp.bfloat16)
    dctx_low = jnp.einsum(
        "te,de->td", branch_low, w_out, preferred_element_type=jnp.float32
    ).astype(jnp.bfloat16)
    dctx_heads = dctx_low.reshape(here_rows, HEADS, HEAD_DIM)
    delta = jnp.sum(
        dctx_heads.astype(jnp.float32) * context.reshape(here_rows, HEADS, HEAD_DIM), axis=2
    ).T
    empty_heads = jnp.zeros((here_rows, HEADS, HEAD_DIM), jnp.float32)

    def key_step(carried, pieces):
        key_rows, value_rows, key_codes = pieces
        chances, d_score = score_grads(
            queries, own_codes, log_total, delta, dctx_heads, key_rows, value_rows, key_codes
        )
        block_rows = key_rows.shape[0]
        query_part = (
            carried
            + jnp.einsum("hqk,khd->qhd", d_score, key_rows, preferred_element_type=jnp.float32)
            * 0.125
        )
        d_key = (
            jnp.einsum("hqk,qhd->khd", d_score, queries, preferred_element_type=jnp.float32) * 0.125
        )
        d_value = jnp.einsum(
            "hqk,qhd->khd",
            chances.astype(jnp.bfloat16),
            dctx_heads,
            preferred_element_type=jnp.float32,
        )
        return (
            query_part,
            jnp.concatenate([d_key.reshape(block_rows, D), d_value.reshape(block_rows, D)], axis=1),
        )

    d_query, key_value_terms = scan_blocks(
        guarded_step(key_step), empty_heads, (key_heads, value_heads, all_codes), seq_rows
    )
    summed_kv = lax.psum_scatter(
        key_value_terms.astype(jnp.bfloat16), "shard", scatter_dimension=0, tiled=True
    ).astype(jnp.float32)
    key_grad = summed_kv[:, :D]
    value_grad = summed_kv[:, D:]
    query_low = d_query.reshape(here_rows, D).astype(jnp.bfloat16)
    key_low = key_grad.astype(jnp.bfloat16)
    value_low = value_grad.astype(jnp.bfloat16)
    mixer_part = lax.psum_scatter(
        jnp.concatenate(
            [
                jnp.einsum("td,te->de", own_tokens, query_low, preferred_element_type=jnp.float32),
                jnp.einsum("td,te->de", own_tokens, key_low, preferred_element_type=jnp.float32),
                jnp.einsum("td,te->de", own_tokens, value_low, preferred_element_type=jnp.float32),
                jnp.einsum(
                    "td,te->de", context_low, branch_low, preferred_element_type=jnp.float32
                ),
            ],
            axis=1,
        ).astype(jnp.bfloat16),
        "shard",
        scatter_dimension=0,
        tiled=True,
    )
    grad_input = jnp.einsum("te,de->td", query_low, w_query, preferred_element_type=jnp.float32)
    grad_input = grad_input + jnp.einsum(
        "te,de->td", key_low, w_key, preferred_element_type=jnp.float32
    )
    grad_input = grad_input + jnp.einsum(
        "te,de->td", value_low, w_value, preferred_element_type=jnp.float32
    )
    grad_tokens = (grad_input + d_first).astype(jnp.bfloat16)[None]
    vectors = jnp.stack(
        [
            jnp.sum(query_low.astype(jnp.float32), axis=0),
            jnp.sum(value_low.astype(jnp.float32), axis=0),
            jnp.sum(branch_low.astype(jnp.float32), axis=0),
            grad_gain_mid,
            grad_shift_mid,
            jnp.sum(feed_low.astype(jnp.float32), axis=0),
            grad_gain_end,
            grad_shift_end,
        ]
    )
    vector_part, up_bias_part = (
        lax.psum_scatter(
            vectors.astype(jnp.bfloat16), "shard", scatter_dimension=1, tiled=True
        ).astype(jnp.float32),
        lax.psum_scatter(
            jnp.sum(up_low.astype(jnp.float32), axis=0).astype(jnp.bfloat16),
            "shard",
            scatter_dimension=0,
            tiled=True,
        ).astype(jnp.float32),
    )
    mixer_total, up_total, down_total, vector_total, up_bias_total = (
        lax.psum(mixer_part, "rep").astype(jnp.float32),
        lax.psum(grad_up, "rep").astype(jnp.float32),
        lax.psum(grad_down, "rep").astype(jnp.float32),
        lax.psum(vector_part.astype(jnp.bfloat16), "rep").astype(jnp.float32),
        lax.psum(up_bias_part.astype(jnp.bfloat16), "rep").astype(jnp.float32),
    )
    return (
        output,
        grad_tokens,
        mixer_total[:, 0:D],
        mixer_total[:, D : 2 * D],
        mixer_total[:, 2 * D : 3 * D],
        vector_total[0],
        vector_total[1],
        mixer_total[:, 3 * D : 4 * D],
        vector_total[2],
        vector_total[3],
        vector_total[4],
        up_total,
        up_bias_total,
        down_total,
        vector_total[5],
        vector_total[6],
        vector_total[7],
    )


def solution(mesh):
    in_specs = (
        P("rep", "shard", None),
        P("rep", "shard"),
        P("rep", "shard"),
        P("shard", None),
        P("shard", None),
        P("shard", None),
        P("shard"),
        P("shard"),
        P("shard", None),
        P("shard"),
        P("shard"),
        P("shard"),
        P("shard", None),
        P("shard"),
        P("shard", None),
        P("shard"),
        P("shard"),
        P("shard"),
        P("rep", "shard", None),
    )
    out_specs = (
        P("rep", "shard", None),
        P("rep", "shard", None),
        P("shard", None),
        P("shard", None),
        P("shard", None),
        P("shard"),
        P("shard"),
        P("shard", None),
        P("shard"),
        P("shard"),
        P("shard"),
        P("shard", None),
        P("shard"),
        P("shard", None),
        P("shard"),
        P("shard"),
        P("shard"),
    )
    return jax.shard_map(shards, mesh=mesh, in_specs=in_specs, out_specs=out_specs, check_vma=False)
```

profile of v0, /device:TPU:3, one launch (start us, length us, event | category | flops | bytes accessed | tf_op | source)
XLA Modules:
  0.0 956.5 jit_solution(7064987100216604116)
XLA Ops:
  12.3 37.8 %all-gather.10.cloned.1.call-done = bf16[768,768]{1,0:T(8,128)(2,1)} async-done(((bf16[48,768]{1,0:T(8,128)(2,1)}), bf16[768,768]{1,0:T(8,128)(2,1)}) %all-gather.10.cloned.1.call-update) | async-done | bytes 1179664 | tf_op jit(solution)/shard_map/all_gather | solution.py:142
  56.4 51.6 %all-reduce.12 = (bf16[768]{0:T(1024)(128)(2,1)S(1)}, bf16[768]{0:T(1024)(128)(2,1)S(1)}, bf16[3072]{0:T(1024)(128)(2,1)S(1)}, bf16[768]{0:T(1024)(128)(2,1)S(1)...) all-reduce(bf16[768]{0:T(1024)(128)(2,1)S(1)} %dynamic-update-slice, ...), channel_id=1, replica_groups=mesh['rep'=2,'shard'=16] {'shard'}, use_global_device_ids=true, to_apply=%add.1 | all-reduce | flops 8448 | bytes 33792
  113.3 58.9 %all-reduce = s32[3072]{0:T(1024)S(1)} all-reduce(s32[3072]{0:T(1024)S(1)} %dynamic-update-slice), channel_id=2, replica_groups=mesh['rep'=2,'shard'=16] {'shard'}, use_global_device_ids=true, to_apply=%add | all-reduce | flops 3072 | bytes 24576
  174.7 10.7 %all-gather.12.cloned.1.call-done = bf16[3072,768]{1,0:T(8,128)(2,1)} async-done(((bf16[192,768]{1,0:T(8,128)(2,1)}), bf16[3072,768]{1,0:T(8,128)(2,1)}) %all-gather.12.cloned.1.call-update) | async-done | bytes 4718608 | tf_op jit(solution)/shard_map/all_gather | solution.py:173
  185.4 15.1 %reshape.236 = bf16[6,512,12,64]{3,2,1,0:T(8,128)(2,1)} reshape(bf16[3072,768]{1,0:T(8,128)(2,1)} %all-gather.12.cloned.1.call-done) | data formatting | bytes 9437184 | tf_op jit(solution)/shard_map/reshape;reshape | solution.py:25
  200.5 13.6 %copy.64 = bf16[6,512,12,64]{1,3,2,0:T(8,128)(2,1)} copy(bf16[6,512,12,64]{3,2,1,0:T(8,128)(2,1)} %reshape.236) | data formatting | bytes 9437184
  214.0 25.8 %all-gather.18.cloned.1.call-done = bf16[3072,768]{1,0:T(8,128)(2,1)} async-done(((bf16[192,768]{1,0:T(8,128)(2,1)}), bf16[3072,768]{1,0:T(8,128)(2,1)}) %all-gather.18.cloned.1.call-update) | async-done | bytes 4718608 | tf_op jit(solution)/shard_map/all_gather | solution.py:174
  239.9 15.0 %reshape.237 = bf16[6,512,12,64]{3,2,1,0:T(8,128)(2,1)} reshape(bf16[3072,768]{1,0:T(8,128)(2,1)} %all-gather.18.cloned.1.call-done) | data formatting | bytes 9437184 | tf_op jit(solution)/shard_map/reshape;reshape | solution.py:25
  254.9 13.6 %copy.65 = bf16[6,512,12,64]{1,3,2,0:T(8,128)(2,1)} copy(bf16[6,512,12,64]{3,2,1,0:T(8,128)(2,1)} %reshape.237) | data formatting | bytes 9437184
  268.4 44.5 %while.28 = (s32[]{:T(128)}, f32[12,192]{1,0:T(8,128)S(1)}, f32[12,192]{1,0:T(8,128)S(1)}, f32[192,12,64]{0,2,1:T(8,128)S(1)}, s32[192]{0:T(256)S(1)}, /*index=5...) while((s32[]{:T(128)}, f32[12,192]{1,0:T(8,128)S(1)}, ...), condition=%wide.region_3.4_spmd.clone, body=%wide.region_0.3_spmd.clone.sunk | while | flops 317879808 | bytes 17750924 | solution.py:30
  315.9 18.6 %all-gather.22.cloned.1.call-done = bf16[768,3072]{1,0:T(8,128)(2,1)} async-done(((bf16[48,3072]{1,0:T(8,128)(2,1)}), bf16[768,3072]{1,0:T(8,128)(2,1)}) %all-gather.22.cloned.1.call-update) | async-done | bytes 4718608 | tf_op jit(solution)/shard_map/all_gather | solution.py:152
  334.5 8.9 fusion.49
  343.4 45.7 %all-gather.24.cloned.1.call-done = bf16[3072,768]{1,0:T(8,128)(2,1)} async-done(((bf16[192,768]{1,0:T(8,128)(2,1)}), bf16[3072,768]{1,0:T(8,128)(2,1)}) %all-gather.24.cloned.1.call-update) | async-done | bytes 4718608 | tf_op jit(solution)/shard_map/all_gather | solution.py:154
  389.0 4.0 fusion.101
  403.6 79.0 %while.29 = (s32[]{:T(128)}, f32[192,12,64]{0,2,1:T(8,128)S(1)}, bf16[6,512,1536]{2,1,0:T(8,128)(2,1)}, bf16[6,512,12,64]{1,3,2,0:T(8,128)(2,1)}, s32[192]{0:T(2...) while((s32[]{:T(128)}, f32[192,12,64]{0,2,1:T(8,128)S(1)}, ...), condition=%wide.region_14.15_spmd.clone, body=%wide.region_13.14_spmd.clone.sunk | while | flops 771244032 | bytes 44384276 | solution.py:37
  485.6 107.1 %reduce-scatter.10.cloned.1.call-done = bf16[192,1536]{1,0:T(8,128)(2,1)} async-done(((bf16[3072,1536]{1,0:T(8,128)(2,1)}), bf16[192,1536]{1,0:T(8,128)(2,1)}) %reduce-scatter.10.cloned.1.call-update) | async-done | bytes 589840 | tf_op jit(solution)/shard_map/reduce_scatter | solution.py:279
  598.3 6.6 copy.74
  620.0 26.6 %all-reduce.11 = (bf16[768]{0:T(1024)(128)(2,1)S(1)}, bf16[3072]{0:T(1024)(128)(2,1)S(1)}) all-reduce(bf16[768]{0:T(1024)(128)(2,1)S(1)} %dynamic-update-slice.9, bf16[3072]{0:T(1024)(128)(2,1)} %get-tuple-element.398), channel_id=1, replica_groups=mesh['rep'=2,'shard'=16] {'shard'}, use_global_device_ids=true, to_apply=%add.9 | all-reduce | flops 3840 | bytes 15360
  647.1 32.3 %reduce-scatter.16.cloned.1.call-done = bf16[48,3072]{1,0:T(8,128)(2,1)} async-done(((bf16[768,3072]{1,0:T(8,128)(2,1)}), bf16[48,3072]{1,0:T(8,128)(2,1)}) %reduce-scatter.16.cloned.1.call-update) | async-done | bytes 294928
  681.6 76.5 %reduce-scatter.12.cloned.1.call-done = bf16[48,3072]{1,0:T(8,128)(2,1)} async-done(((bf16[768,3072]{1,0:T(8,128)(2,1)}), bf16[48,3072]{1,0:T(8,128)(2,1)}) %reduce-scatter.12.cloned.1.call-update) | async-done | bytes 294928 | tf_op jit(solution)/shard_map/reduce_scatter | solution.py:229
  758.1 78.6 %reduce-scatter.14.cloned.1.call-done = bf16[192,768]{1,0:T(8,128)(2,1)} async-done(((bf16[3072,768]{1,0:T(8,128)(2,1)}), bf16[192,768]{1,0:T(8,128)(2,1)}) %reduce-scatter.14.cloned.1.call-update) | async-done | bytes 294928 | tf_op jit(solution)/shard_map/reduce_scatter | solution.py:219
  840.7 51.6 %reduce-scatter.18.cloned.1.call-done = bf16[48,8]{1,0:T(8,128)(2,1)} async-done(((bf16[768,8]{1,0:T(8,128)(2,1)}), bf16[48,8]{1,0:T(8,128)(2,1)}) %reduce-scatter.18.cloned.1.call-update) | async-done | bytes 784
  893.1 3.8 all-reduce.13
  898.0 44.9 %all-reduce.17.cloned.1.call-done = (bf16[48,3072]{0,1:T(8,128)(2,1)}, bf16[48,3072]{1,0:T(8,128)(2,1)}, bf16[192,768]{1,0:T(8,128)(2,1)}) async-done(((bf16[48,3072]{0,1:T(8,128)(2,1)}, bf16[48,3072]{1,0:T(8,128)(2,1)}, bf16[192,768]{1,0:T(8,128)(2,1)}), (bf16[48,3072]{0,1:T(8,128)(2,1)}, bf16[48,3072]{1,0:T(8,128)(2,1)}, bf16[192,768]{1,0:T(8,128)(2,1)})) %all-reduce.17.cloned.1.call-update) | async-done | bytes 884752 | tf_op jit(solution)/shard_map/psum | solution.py:335
  (418 shorter events, 191.7 us)
Async XLA Ops:
  7.2 100.8 %copy-start.2 = (bf16[1,192,768]{2,1,0:T(8,128)(2,1)S(1)}, bf16[1,192,768]{2,1,0:T(8,128)(2,1)}, u32[]{:S(2)}) copy-start(bf16[1,192,768]{2,1,0:T(8,128)(2,1)} %param.23) | copy-start | bytes 884740
  7.3 42.7 %all-gather.10.cloned.1.call-start = ((), (), s32[]{:S(2)}) async-start(), calls=%async_computation.5 | async-start | bytes 1253376 | tf_op jit(solution)/shard_map/all_gather | solution.py:142
  9.0 99.0 %all-gather.16.cloned.1.call-start = ((), (), s32[]{:S(2)}) async-start(), calls=%async_computation.8 | async-start | bytes 1253376 | tf_op jit(solution)/shard_map/all_gather | solution.py:143
  10.6 99.9 %copy-start.30 = (f32[48,768]{1,0:T(8,128)S(1)}, f32[48,768]{1,0:T(8,128)}, u32[]{:S(2)}) copy-start(f32[48,768]{1,0:T(8,128)} %param.31) | copy-start | bytes 442372
  10.6 162.2 %all-gather.14.cloned.1.call-start = ((), (), s32[]{:S(2)}) async-start(), calls=%async_computation.7 | async-start | bytes 1253376 | tf_op jit(solution)/shard_map/all_gather | solution.py:141
  12.2 99.0 %copy-start.28 = (f32[48,3072]{1,0:T(8,128)S(1)}, f32[48,3072]{1,0:T(8,128)}, u32[]{:S(2)}) copy-start(f32[48,3072]{1,0:T(8,128)} %param.35) | copy-start | bytes 1769476
  12.2 173.2 %all-gather.12.cloned.1.call-start = ((), (), s32[]{:S(2)}) async-start(), calls=%async_computation.6 | async-start | bytes 5013504 | tf_op jit(solution)/shard_map/all_gather | solution.py:173
  52.5 187.3 %all-gather.18.cloned.1.call-start = ((), (), s32[]{:S(2)}) async-start(), calls=%async_computation.9 | async-start | bytes 5013504 | tf_op jit(solution)/shard_map/all_gather | solution.py:174
  110.4 202.7 %all-gather.20.cloned.1.call-start = ((), (), s32[]{:S(2)}) async-start(), calls=%async_computation.10 | async-start | bytes 1253376 | tf_op jit(solution)/shard_map/all_gather | solution.py:144
  111.1 223.3 %all-gather.22.cloned.1.call-start = ((), (), s32[]{:S(2)}) async-start(), calls=%async_computation.11 | async-start | bytes 5013504 | tf_op jit(solution)/shard_map/all_gather | solution.py:152
  112.0 277.1 %all-gather.24.cloned.1.call-start = ((), (), s32[]{:S(2)}) async-start(), calls=%async_computation.12 | async-start | bytes 5013504 | tf_op jit(solution)/shard_map/all_gather | solution.py:154
  112.8 479.9 %reduce-scatter.10.cloned.1.call-start = ((), (), s32[]{:S(2)}) async-start(), calls=%async_computation.13 | async-start | bytes 10027008 | tf_op jit(solution)/shard_map/reduce_scatter | solution.py:279
  315.0 85.4 %copy-start.4 = (f32[192,768]{1,0:T(8,128)}, f32[192,768]{1,0:T(8,128)S(1)}, u32[]{:S(2)}) copy-start(f32[192,768]{1,0:T(8,128)S(1)} %get-tuple-element.393) | copy-start | bytes 1769476
  315.0 85.4 %copy-start.31 = (f32[192]{0:T(256)}, f32[192]{0:T(256)S(1)}, u32[]{:S(2)}) copy-start(f32[192]{0:T(256)S(1)} %broadcast_multiply_fusion.5) | copy-start | bytes 2308
  315.3 85.2 %copy-start.35 = (f32[192]{0:T(256)}, f32[192]{0:T(256)S(1)}, u32[]{:S(2)}) copy-start(f32[192]{0:T(256)S(1)} %add_rsqrt_fusion.1) | copy-start | bytes 2308
  482.6 196.8 %reduce-scatter.16.cloned.1.call-start = ((), (), s32[]{:S(2)}) async-start(), calls=%async_computation.16 | async-start | bytes 5013504
  605.0 153.1 %reduce-scatter.12.cloned.1.call-start = ((), (), s32[]{:S(2)}) async-start(), calls=%async_computation.14 | async-start | bytes 5013504 | tf_op jit(solution)/shard_map/reduce_scatter | solution.py:229
  610.1 226.6 %reduce-scatter.14.cloned.1.call-start = ((), (), s32[]{:S(2)}) async-start(), calls=%async_computation.15 | async-start | bytes 5013504 | tf_op jit(solution)/shard_map/reduce_scatter | solution.py:219
  615.4 276.9 %reduce-scatter.18.cloned.1.call-start = ((), (), s32[]{:S(2)}) async-start(), calls=%async_computation.17 | async-start | bytes 208896
  618.5 218.2 %copy-start.7 = (f32[192,768]{1,0:T(8,128)S(1)}, f32[192,768]{1,0:T(8,128)}, u32[]{:S(2)}) copy-start(f32[192,768]{1,0:T(8,128)} %copy-done.6) | copy-start | bytes 1769476
  618.5 218.2 %copy-start.34 = (f32[192]{0:T(256)S(1)}, f32[192]{0:T(256)}, u32[]{:S(2)}) copy-start(f32[192]{0:T(256)} %copy-done.33) | copy-start | bytes 2308
  618.5 218.2 %copy-start.38 = (f32[192]{0:T(256)S(1)}, f32[192]{0:T(256)}, u32[]{:S(2)}) copy-start(f32[192]{0:T(256)} %copy-done.37) | copy-start | bytes 2308
  618.5 324.4 %all-reduce.17.cloned.1.call-start = ((), (), s32[]{:S(2)}) async-start(), calls=%async_computation.18 | async-start | bytes 2752512 | tf_op jit(solution)/shard_map/psum | solution.py:335
  620.0 217.7 %copy-start.23 = (f32[192,768]{1,0:T(8,128)S(1)}, f32[192,768]{1,0:T(8,128)}, u32[]{:S(2)}) copy-start(f32[192,768]{1,0:T(8,128)} %fusion.103) | copy-start | bytes 1769476
  (72 other events, 713.9 us)
Sparse Core Ops, SparseCore 0:
  11.0 39.0 all-gather.9
  52.9 37.3 all-gather.15
  93.1 37.1 all-gather.13
  133.0 52.3 all-gather.11
  188.1 51.6 all-gather.17
  242.6 36.8 all-gather.19
  282.3 52.0 all-gather.21
  337.3 51.6 all-gather.23
  482.7 109.9 reduce-scatter.9
  605.1 74.3 reduce-scatter.15
  683.3 74.7 reduce-scatter.11
  761.8 74.8 reduce-scatter.13
  840.2 52.1 reduce-scatter.17
  894.6 48.2 all-reduce.16
where the time goes:
time: 963 us; the launch traced here: 956 us
  waiting for transfers between devices  530 us (55%)
  blocking collectives  141 us (15%)
  matrix products  129 us (13%)
  local copies, waits for them, and re-layouts  107 us (11%)
  other arithmetic  31.2 us (3%)
  between operations  16.8 us (2%)
    unnamed x3, blocking collectives  137 us
    reduce_scatter x1, waiting for transfers between devices, shards(): lax.psum_scatter(key_value_terms.astype(jnp.bfloat16), 'shard', scatter_d...  107 us
    unnamed x16, waiting for transfers between devices  84.1 us
    reduce_scatter x1, waiting for transfers between devices, shards(): lax.psum_scatter(jnp.einsum('tf,td->fd', active_low, feed_low, preferred_...  78.6 us
    reduce_scatter x1, waiting for transfers between devices, shards(): lax.psum_scatter(jnp.einsum('td,tf->df', middle_low, up_low, preferred_el...  76.5 us
    unnamed x148, local copies, waits for them, and re-layouts  49.3 us
    all_gather x1, waiting for transfers between devices, shards(): lax.all_gather(down_weight.astype(jnp.bfloat16), 'shard', axis=0, tiled=T...  45.7 us
    psum x1, waiting for transfers between devices, shards(): lax.psum(mixer_part, 'rep').astype(jnp.float32)  44.9 us
  transfers between devices with their start and end apart: 14, of which 11 were waited for; matrix products, arithmetic and copies ran while one was open for 16% of the time, Pallas kernels for 0%

commit v1 on v0

v1 whole, which is shorter than its diff:
```python
import functools

import jax
import jax.numpy as jnp
from jax import lax
from jax.experimental import pallas as pl
from jax.experimental.pallas import tpu as pltpu
from jax.sharding import PartitionSpec as P

D = 768
HEADS = 12
HEAD_DIM = 64
PLANE = 4
GROUP_HEADS = HEADS // PLANE
GROUP_DIM = GROUP_HEADS * HEAD_DIM
FF = 3072
GROUP_FF = FF // PLANE

epsilon = 1e-12
very_low = -1e30
root_half = 0.7071067811865476
inv_root_tau = 0.3989422804014327
bf16 = jnp.bfloat16
f32 = jnp.float32
MESH = pl.DeviceIdType.MESH
VMEM_SPEC = pl.BlockSpec(memory_space=pltpu.VMEM)
ANY_SPEC = pl.BlockSpec(memory_space=pl.ANY)
VMEM_BYTES = 60000 * 1024


def struct(shape, dtype=bf16):
    return jax.ShapeDtypeStruct(shape, dtype)


def comm_call(body, name, ident, inputs, out_shapes, out_specs, scratch):
    return pl.pallas_call(
        body,
        name=name,
        out_shape=out_shapes,
        in_specs=[VMEM_SPEC] * len(inputs),
        out_specs=out_specs,
        scratch_shapes=scratch,
        compiler_params=pltpu.CompilerParams(
            collective_id=ident, has_side_effects=True, vmem_limit_bytes=VMEM_BYTES
        ),
    )(*inputs)


def greet(peers):
    barrier = pltpu.get_barrier_semaphore()
    for peer in peers:
        pl.semaphore_signal(barrier, inc=1, device_id=peer, device_id_type=MESH)
    pl.semaphore_wait(barrier, len(peers))


def remote(src, dst, send_sem, recv_sem, peer):
    return pltpu.make_async_remote_copy(
        src_ref=src,
        dst_ref=dst,
        send_sem=send_sem,
        recv_sem=recv_sem,
        device_id=peer,
        device_id_type=MESH,
    )


def plane_peer(me, mask):
    group = lax.rem(me, PLANE)
    core = lax.rem(group, 2)
    column = lax.div(group, 2)
    if mask & 1:
        core = 1 - core
    if mask & 2:
        column = 1 - column
    return me - group + 2 * column + core


def plane_slot(me, mask):
    return lax.rem(plane_peer(me, mask), PLANE)


def plane_gather(value, ident):
    rows, cols = value.shape

    def body(x_ref, out_ref, send, recv, local):
        me = lax.axis_index("shard")
        peers = [{"shard": plane_peer(me, mask)} for mask in (1, 2)]
        greet(peers)
        mine, far = lax.rem(me, PLANE), plane_slot(me, 2)
        own = pltpu.make_async_copy(x_ref, out_ref.at[mine], local)
        own.start()
        across = remote(x_ref, out_ref.at[mine], send.at[0], recv.at[0], peers[1])
        across.start()
        beside = remote(x_ref, out_ref.at[mine], send.at[1], recv.at[1], peers[0])
        beside.start()
        across.wait_recv()
        relay = remote(out_ref.at[far], out_ref.at[far], send.at[2], recv.at[2], peers[0])
        relay.start()
        beside.wait_recv()
        relay.wait_recv()
        across.wait_send()
        beside.wait_send()
        relay.wait_send()
        own.wait()

    return comm_call(
        body,
        "plane_gather",
        ident,
        [value],
        struct((PLANE, rows, cols), value.dtype),
        VMEM_SPEC,
        [
            pltpu.SemaphoreType.DMA((3,)),
            pltpu.SemaphoreType.DMA((3,)),
            pltpu.SemaphoreType.DMA,
        ],
    )


def plane_sum(parts, ident):
    _, rows, cols = parts.shape

    def body(p_ref, out_ref, near, held, far_in, send, recv):
        me = lax.axis_index("shard")
        peers = [{"shard": plane_peer(me, mask)} for mask in (1, 2)]
        greet(peers)
        first = remote(
            p_ref.at[plane_slot(me, 3)], near.at[0], send.at[0], recv.at[0], peers[0]
        )
        first.start()
        second = remote(
            p_ref.at[plane_slot(me, 1)], near.at[1], send.at[1], recv.at[1], peers[0]
        )
        second.start()
        first.wait_recv()
        held[...] = (p_ref[plane_slot(me, 2)].astype(f32) + near[0].astype(f32)).astype(bf16)
        third = remote(held, far_in, send.at[2], recv.at[2], peers[1])
        third.start()
        second.wait_recv()
        out_ref[...] = p_ref[lax.rem(me, PLANE)].astype(f32) + near[1].astype(f32)
        third.wait_recv()
        out_ref[...] += far_in[...].astype(f32)
        first.wait_send()
        second.wait_send()
        third.wait_send()

    return comm_call(
        body,
        "plane_sum",
        ident,
        [parts],
        struct((rows, cols), f32),
        VMEM_SPEC,
        [
            pltpu.VMEM((2, rows, cols), bf16),
            pltpu.VMEM((rows, cols), bf16),
            pltpu.VMEM((rows, cols), bf16),
            pltpu.SemaphoreType.DMA((3,)),
            pltpu.SemaphoreType.DMA((3,)),
        ],
    )


def others(me, count):
    return [{"shard": lax.rem(me + step, count)} for step in range(1, count)]


def gather_weights(count, tokens, qkv, up, out_w, down, small, ident):
    planes = count // PLANE
    rows = qkv.shape[1]
    block = down.shape[0]

    def body(x_ref, qkv_ref, up_ref, wo_ref, down_ref, small_ref, *rest):
        x_out, qkv_out, up_out, wo_out, down_out, small_out = rest[:6]
        send, recv, local, send_wo, recv_wo = rest[6:]
        me = lax.axis_index("shard")
        group, plane = lax.rem(me, PLANE), lax.div(me, PLANE)
        greet(others(me, count))
        owns = [
            (x_ref, x_out.at[group]),
            (qkv_ref.at[group], qkv_out.at[me]),
            (up_ref.at[group], up_out.at[me]),
            (down_ref, down_out.at[plane]),
            (small_ref, small_out.at[me]),
        ]
        started = []
        for index, (src, dst) in enumerate(owns):
            copy = pltpu.make_async_copy(src, dst, local.at[index])
            copy.start()
            started.append(copy)
        sent = []

        def push(src, dst, peer):
            index = len(sent)
            copy = remote(src, dst, send.at[index], recv.at[index], {"shard": peer})
            copy.start()
            sent.append(copy)

        for mask in (2, 1, 3):
            push(x_ref, x_out.at[group], plane_peer(me, mask))
        for src, dst in ((small_ref, small_out), (qkv_ref, qkv_out), (up_ref, up_out)):
            for step in range(1, count):
                peer = lax.rem(me + step, count)
                piece = src if src is small_ref else src.at[lax.rem(peer, PLANE)]
                push(piece, dst.at[me], peer)
        for step in range(1, planes):
            push(down_ref, down_out.at[plane], lax.rem(me + PLANE * step, count))
        target, place = lax.div(me, planes), lax.rem(me, planes)

        def wo_copy(source, index):
            peer = PLANE * index + target
            return peer, remote(
                wo_ref, wo_out.at[place], send_wo.at[index], recv_wo.at[source], {"shard": peer}
            )

        for index in range(planes):
            peer, copy = wo_copy(place, index)
            pl.when(peer != me)(copy.start)
        keep = pltpu.make_async_copy(wo_ref, wo_out.at[place], local.at[5])
        pl.when(target == group)(keep.start)
        for copy in sent:
            copy.wait_recv()
        for index in range(planes):
            pl.when(group * planes + index != me)(wo_copy(index, index)[1].wait_recv)
        for index in range(planes):
            peer, copy = wo_copy(place, index)
            pl.when(peer != me)(copy.wait_send)
        pl.when(target == group)(keep.wait)
        for copy in sent:
            copy.wait_send()
        for copy in started:
            copy.wait()

    total = 3 + 3 * (count - 1) + planes - 1
    return comm_call(
        body,
        "gather_weights",
        ident,
        [tokens, qkv, up, out_w, down, small],
        [
            struct((PLANE,) + tokens.shape),
            struct((count, rows, qkv.shape[2])),
            struct((count, rows, up.shape[2])),
            struct((planes,) + out_w.shape),
            struct((planes, block, D)),
            struct((count,) + small.shape),
        ],
        [ANY_SPEC] * 6,
        [
            pltpu.SemaphoreType.DMA((total,)),
            pltpu.SemaphoreType.DMA((total,)),
            pltpu.SemaphoreType.DMA((6,)),
            pltpu.SemaphoreType.DMA((planes,)),
            pltpu.SemaphoreType.DMA((planes,)),
        ],
    )


def gather_planes(count, value, ident):
    planes = count // PLANE

    def body(x_ref, out_ref, send, recv, local):
        me = lax.axis_index("shard")
        plane = lax.div(me, PLANE)
        peers = [{"shard": lax.rem(me + PLANE * s, count)} for s in range(1, planes)]
        greet(peers)
        own = pltpu.make_async_copy(x_ref, out_ref.at[plane], local)
        own.start()
        sent = []
        for index, peer in enumerate(peers):
            copy = remote(x_ref, out_ref.at[plane], send.at[index], recv.at[index], peer)
            copy.start()
            sent.append(copy)
        for copy in sent:
            copy.wait_recv()
        for copy in sent:
            copy.wait_send()
        own.wait()

    return comm_call(
        body,
        "gather_planes",
        ident,
        [value],
        struct((planes,) + value.shape),
        ANY_SPEC,
        [
            pltpu.SemaphoreType.DMA((planes,)),
            pltpu.SemaphoreType.DMA((planes,)),
            pltpu.SemaphoreType.DMA,
        ],
    )


def sum_planes(count, parts, ident):
    planes, rows, cols = parts.shape

    def body(p_ref, out_ref, held, send, recv):
        me = lax.axis_index("shard")
        plane = lax.div(me, PLANE)
        peers = [lax.rem(me + PLANE * s, count) for s in range(1, planes)]
        greet([{"shard": peer} for peer in peers])
        sent = []
        for index, peer in enumerate(peers):
            copy = remote(
                p_ref.at[lax.div(peer, PLANE)],
                held.at[index],
                send.at[index],
                recv.at[index],
                {"shard": peer},
            )
            copy.start()
            sent.append(copy)
        for copy in sent:
            copy.wait_recv()
        total = p_ref[plane].astype(f32)
        for index in range(planes - 1):
            total = total + held[index].astype(f32)
        out_ref[...] = total.astype(bf16)
        for copy in sent:
            copy.wait_send()

    return comm_call(
        body,
        "sum_planes",
        ident,
        [parts],
        struct((rows, cols)),
        VMEM_SPEC,
        [
            pltpu.VMEM((planes - 1, rows, cols), bf16),
            pltpu.SemaphoreType.DMA((planes,)),
            pltpu.SemaphoreType.DMA((planes,)),
        ],
    )


def reduce_grads(count, copies, qkv, up, out_w, down, small, ident):
    planes = count // PLANE
    rows = qkv.shape[1]
    block = down.shape[1]
    arrays = [qkv, up, out_w, small]

    def body(qkv_ref, up_ref, wo_ref, small_ref, down_ref, *rest):
        outs, (qkv_in, up_in, wo_in, small_in, down_in) = rest[:5], rest[5:10]
        halves, gets = rest[10:15], rest[15:20]
        send, recv, send_rep, recv_rep, send_wo, recv_wo = rest[20:]
        me = lax.axis_index("shard")
        rep = lax.axis_index("rep")
        plane = lax.div(me, PLANE)
        across = [{"rep": lax.rem(rep + step, copies)} for step in range(1, copies)]
        greet(others(me, count) + across)
        sent = []

        def push(src, dst, peer):
            index = len(sent)
            copy = remote(src, dst, send.at[index], recv.at[index], {"shard": peer})
            copy.start()
            sent.append(copy)

        pairs = [(qkv_ref, qkv_in), (up_ref, up_in), (small_ref, small_in)]
        group = lax.rem(me, PLANE)
        target, place = lax.div(me, planes), lax.rem(me, planes)
        for src, held in pairs:
            for step in range(1, count):
                peer = lax.rem(me + step, count)
                push(src.at[peer], held.at[me], peer)
        for step in range(1, planes):
            peer = lax.rem(me + PLANE * step, count)
            push(down_ref.at[lax.div(peer, PLANE)], down_in.at[plane], peer)
        for src, held in pairs:
            held[me] = src[me]
        down_in[plane] = down_ref[plane]

        def wo_copy(source, index):
            peer = group * planes + index
            return peer, remote(
                wo_ref.at[index],
                wo_in.at[plane],
                send_wo.at[index],
                recv_wo.at[source],
                {"shard": peer},
            )

        for index in range(planes):
            peer, copy = wo_copy(plane, index)
            pl.when(peer != me)(copy.start)

        @pl.when(target == group)
        def _():
            wo_in[plane] = wo_ref[place]

        for copy in sent:
            copy.wait_recv()
        for index in range(planes):
            pl.when(PLANE * index + target != me)(wo_copy(index, index)[1].wait_recv)
        for index in range(planes):
            peer, copy = wo_copy(plane, index)
            pl.when(peer != me)(copy.wait_send)
        for half, held in zip(halves[:2], (qkv_in, up_in)):
            for lane in range(PLANE):
                total = held[lane].astype(f32)
                for other in range(1, planes):
                    total = total + held[other * PLANE + lane].astype(f32)
                half[lane] = total.astype(bf16)
        for half, held, number in (
            (halves[2], wo_in, planes),
            (halves[3], small_in, count),
            (halves[4], down_in, planes),
        ):
            total = held[0].astype(f32)
            for other in range(1, number):
                total = total + held[other].astype(f32)
            half[...] = total.astype(bf16)
        passed = []
        for index, peer in enumerate(across):
            for place, (half, got) in enumerate(zip(halves, gets)):
                copy = remote(
                    half,
                    got.at[index],
                    send_rep.at[5 * index + place],
                    recv_rep.at[5 * index + place],
                    peer,
                )
                copy.start()
                passed.append(copy)
        for copy in passed:
            copy.wait_recv()
        for out, half, got in zip(outs, halves, gets):
            total = half[...].astype(f32)
            for index in range(copies - 1):
                total = total + got[index].astype(f32)
            out[...] = total
        for copy in sent + passed:
            copy.wait_send()

    totals = 3 * (count - 1) + planes - 1
    shapes = [
        (PLANE, rows, qkv.shape[2]),
        (PLANE, rows, up.shape[2]),
        (rows, D),
        small.shape[1:],
        (block, D),
    ]
    return comm_call(
        body,
        "reduce_grads",
        ident,
        arrays + [down],
        [struct(shape, f32) for shape in shapes],
        [VMEM_SPEC] * 5,
        [pltpu.VMEM(item.shape, bf16) for item in arrays + [down]]
        + [pltpu.VMEM(shape, bf16) for shape in shapes]
        + [pltpu.VMEM((copies - 1,) + shape, bf16) for shape in shapes]
        + [
            pltpu.SemaphoreType.DMA((totals,)),
            pltpu.SemaphoreType.DMA((totals,)),
            pltpu.SemaphoreType.DMA((5 * (copies - 1),)),
            pltpu.SemaphoreType.DMA((5 * (copies - 1),)),
            pltpu.SemaphoreType.DMA((planes,)),
            pltpu.SemaphoreType.DMA((planes,)),
        ],
    )


def norm_forward(value, gain, shift):
    center = value - jnp.mean(value, axis=-1, keepdims=True)
    spread = jnp.mean(center * center, axis=-1, keepdims=True)
    scale = lax.rsqrt(spread + epsilon)
    normal = center * scale
    return (normal * gain + shift, normal, scale)


def norm_backward(upstream, normal, scale, gain):
    inner = upstream * gain
    return scale * (
        inner
        - jnp.mean(inner, axis=-1, keepdims=True)
        - normal * jnp.mean(inner * normal, axis=-1, keepdims=True)
    )


def gelu_slope(hidden):
    return 0.5 * (1.0 + lax.erf(hidden * root_half)) + hidden * inv_root_tau * jnp.exp(
        -0.5 * hidden * hidden
    )


def dot(left, right):
    return jnp.dot(left, right, preferred_element_type=f32)


def dot_left(left, right):
    return lax.dot_general(left, right, (((0,), (0,)), ((), ())), preferred_element_type=f32)


def dot_right(left, right):
    return lax.dot_general(left, right, (((1,), (1,)), ((), ())), preferred_element_type=f32)


def heads_of(value):
    return value.reshape(value.shape[0], GROUP_HEADS, HEAD_DIM).transpose(1, 0, 2)


def flat_of(value):
    return value.transpose(1, 0, 2).reshape(value.shape[1], GROUP_DIM)


def attend_forward(queries, keys, values, own_codes, all_codes):
    def step(carried, pieces):
        top, total, summed = carried
        key_rows, value_rows, key_codes = pieces
        raw = jnp.einsum("hqd,khd->hqk", queries, key_rows, preferred_element_type=f32) * 0.125
        allowed = (own_codes[:, None] == key_codes[None, :])[None]
        masked = jnp.where(allowed, raw, very_low)
        new_top = jnp.maximum(top, jnp.max(masked, axis=2))
        rescale = jnp.exp(top - new_top)
        weights = jnp.where(allowed, jnp.exp(masked - new_top[:, :, None]), 0.0)
        added = jnp.einsum(
            "hqk,khd->hqd", weights.astype(bf16), value_rows, preferred_element_type=f32
        )
        return (
            new_top,
            total * rescale + jnp.sum(weights, axis=2),
            summed * rescale[:, :, None] + added,
        ), None

    rows = queries.shape[1]
    start = (
        jnp.full((GROUP_HEADS, rows), very_low, f32),
        jnp.zeros((GROUP_HEADS, rows), f32),
        jnp.zeros((GROUP_HEADS, rows, HEAD_DIM), f32),
    )
    (top, total, summed), _ = lax.scan(step, start, (keys, values, all_codes))
    return summed / total[:, :, None], top + jnp.log(total)


def attend_backward(queries, keys, values, own_codes, all_codes, logs, delta, upstream):
    def step(carried, pieces):
        key_rows, value_rows, key_codes = pieces
        raw = jnp.einsum("hqd,khd->hqk", queries, key_rows, preferred_element_type=f32) * 0.125
        allowed = (own_codes[:, None] == key_codes[None, :])[None]
        chances = jnp.where(allowed, jnp.exp(raw - logs[:, :, None]), 0.0)
        d_chance = jnp.einsum("hqd,khd->hqk", upstream, value_rows, preferred_element_type=f32)
        d_score = (chances * (d_chance - delta[:, :, None])).astype(bf16)
        carried = carried + jnp.einsum(
            "hqk,khd->hqd", d_score, key_rows, preferred_element_type=f32
        )
        d_key = jnp.einsum("hqk,hqd->khd", d_score, queries, preferred_element_type=f32) * 0.125
        d_value = jnp.einsum(
            "hqk,hqd->khd", chances.astype(bf16), upstream, preferred_element_type=f32
        )
        size = key_rows.shape[0]
        return carried, jnp.concatenate(
            [d_key.reshape(size, GROUP_DIM), d_value.reshape(size, GROUP_DIM)], axis=1
        ).astype(bf16)

    start = jnp.zeros(queries.shape, f32)
    d_query, d_pair = lax.scan(step, start, (keys, values, all_codes))
    return d_query * 0.125, d_pair


def shards(count, copies, *arrays):
    (
        tokens,
        segments,
        padding,
        query_weight,
        key_weight,
        value_weight,
        query_bias,
        value_bias,
        out_weight,
        out_bias,
        middle_gain,
        middle_shift,
        up_weight,
        up_bias,
        down_weight,
        down_bias,
        final_gain,
        final_shift,
        cotangent,
    ) = arrays
    planes = count // PLANE
    rows = query_weight.shape[0]
    block = down_weight.shape[0]
    x_own = tokens[0]
    here = x_own.shape[0]
    wide = PLANE * here
    me = lax.axis_index("shard")
    group = lax.rem(me, PLANE)
    qkv_send = jnp.concatenate(
        [
            item.astype(bf16).reshape(rows, PLANE, GROUP_DIM)
            for item in (query_weight, key_weight, value_weight)
        ],
        axis=2,
    ).transpose(1, 0, 2)
    up_send = (
        up_weight.astype(bf16)
        .reshape(rows, planes, PLANE, block)
        .transpose(2, 0, 1, 3)
        .reshape(PLANE, rows, GROUP_FF)
    )
    codes = (2 * segments[0] + padding[0]).astype(f32)
    lanes = 128 * ((max(here, block) + 127) // 128)

    def padded(value):
        return jnp.pad(value.astype(f32), (0, lanes - value.shape[0]))

    vectors = [
        query_bias,
        value_bias,
        out_bias,
        middle_gain,
        middle_shift,
        down_bias,
        final_gain,
        final_shift,
        up_bias,
        codes,
    ]
    small_send = jnp.pad(
        jnp.stack([padded(item) for item in vectors]), ((0, 6), (0, 0))
    ).astype(bf16)
    x_all, qkv_all, up_all, wo_all, down_all, small = gather_weights(
        count,
        x_own,
        qkv_send,
        up_send,
        out_weight.astype(bf16),
        down_weight.astype(bf16),
        small_send,
        0,
    )
    x_plane = x_all.reshape(wide, D)
    w_qkv = qkv_all.reshape(D, 3 * GROUP_DIM)
    w_up = up_all.reshape(D, GROUP_FF)
    w_out = wo_all.reshape(GROUP_DIM, D)
    w_down = down_all.reshape(GROUP_FF, D)
    small = small.astype(f32)
    spread = [small[:, index, :rows].reshape(D) for index in range(8)]
    b_query, b_value, b_out, gain_mid, shift_mid, b_down, gain_end, shift_end = spread
    b_up = lax.dynamic_index_in_dim(
        small[:, 8, :block].reshape(planes, PLANE, block), group, 1, keepdims=False
    ).reshape(GROUP_FF)
    all_codes = small[:, 9, :here].reshape(planes, wide)
    own_codes = lax.dynamic_index_in_dim(all_codes, lax.div(me, PLANE), 0, keepdims=False)

    def group_part(value):
        return lax.dynamic_slice(value, (group * GROUP_DIM,), (GROUP_DIM,))

    qkv_bias = jnp.concatenate(
        [group_part(b_query), jnp.zeros((GROUP_DIM,), f32), group_part(b_value)]
    )
    qkv = (dot(x_plane, w_qkv) + qkv_bias).astype(bf16)
    pairs = gather_planes(count, qkv[:, GROUP_DIM:], 1)
    queries = heads_of(qkv[:, :GROUP_DIM])
    keys = pairs[:, :, :GROUP_DIM].reshape(planes, wide, GROUP_HEADS, HEAD_DIM)
    values = pairs[:, :, GROUP_DIM:].reshape(planes, wide, GROUP_HEADS, HEAD_DIM)
    context_heads, logs = attend_forward(queries, keys, values, own_codes, all_codes)
    context_low = flat_of(context_heads).astype(bf16)

    def split(value):
        return value.reshape(PLANE, here, D)

    branch = plane_sum(split(dot(context_low, w_out).astype(bf16)), 2) + b_out
    middle, normal_mid, scale_mid = norm_forward(x_own.astype(f32) + branch, gain_mid, shift_mid)
    middle_plane = plane_gather(middle.astype(bf16), 3).reshape(wide, D)
    hidden = dot(middle_plane, w_up) + b_up
    active_low = jax.nn.gelu(hidden, approximate=False).astype(bf16)
    feed = plane_sum(split(dot(active_low, w_down).astype(bf16)), 4) + b_down
    result, normal_end, scale_end = norm_forward(middle + feed, gain_end, shift_end)
    output = result.astype(bf16)[None]
    upstream = cotangent[0].astype(f32)
    d_second = norm_backward(upstream, normal_end, scale_end, gain_end)
    feed_low = d_second.astype(bf16)
    feed_plane = plane_gather(feed_low, 5).reshape(wide, D)
    grad_down = dot_left(active_low, feed_plane).astype(bf16)
    up_low = (dot_right(feed_plane, w_down) * gelu_slope(hidden)).astype(bf16)
    grad_up = dot_left(middle_plane, up_low).astype(bf16)
    d_middle = plane_sum(split(dot_right(up_low, w_up).astype(bf16)), 6) + d_second
    d_first = norm_backward(d_middle, normal_mid, scale_mid, gain_mid)
    branch_low = d_first.astype(bf16)
    branch_plane = plane_gather(branch_low, 7).reshape(wide, D)
    grad_out = dot_left(context_low, branch_plane).astype(bf16)
    d_context = heads_of(dot_right(branch_plane, w_out).astype(bf16))
    delta = jnp.sum(d_context.astype(f32) * context_heads, axis=2)
    d_query, d_pair = attend_backward(
        queries, keys, values, own_codes, all_codes, logs, delta, d_context
    )
    pair_low = sum_planes(count, d_pair, 8)
    mixer_low = jnp.concatenate([flat_of(d_query).astype(bf16), pair_low], axis=1)
    grad_qkv = dot_left(x_plane, mixer_low).astype(bf16)
    grad_input = plane_sum(split(dot_right(mixer_low, w_qkv).astype(bf16)), 9)
    grad_tokens = (grad_input + d_first).astype(bf16)[None]
    mixer_sums = jnp.sum(mixer_low.astype(f32), axis=0)

    def from_group(value):
        return lax.dynamic_update_slice(jnp.zeros((D,), f32), value, (group * GROUP_DIM,))

    sums = [
        from_group(mixer_sums[:GROUP_DIM]),
        from_group(mixer_sums[2 * GROUP_DIM :]),
        jnp.sum(branch_low.astype(f32), axis=0),
        jnp.sum(d_middle * normal_mid, axis=0),
        jnp.sum(d_middle, axis=0),
        jnp.sum(feed_low.astype(f32), axis=0),
        jnp.sum(upstream * normal_end, axis=0),
        jnp.sum(upstream, axis=0),
    ]
    own_lane = (jnp.arange(PLANE) == group).astype(f32)
    up_sums = jnp.sum(up_low.astype(f32), axis=0).reshape(planes, 1, block)
    up_sums = (up_sums * own_lane[None, :, None]).reshape(count, 1, block)
    sums = jnp.stack([item.reshape(count, rows) for item in sums], axis=1)
    small_grads = jnp.concatenate(
        [
            jnp.pad(sums, ((0, 0), (0, 0), (0, lanes - rows))),
            jnp.pad(up_sums, ((0, 0), (0, 7), (0, lanes - block))),
        ],
        axis=1,
    ).astype(bf16)
    qkv_total, up_total, out_total, small_total, down_total = reduce_grads(
        count,
        copies,
        grad_qkv.reshape(count, rows, 3 * GROUP_DIM),
        grad_up.reshape(count, rows, GROUP_FF),
        grad_out.reshape(planes, rows, D),
        grad_down.reshape(planes, block, D),
        small_grads,
        10,
    )

    def joined(value):
        return value.transpose(1, 0, 2).reshape(rows, D)

    up_grad = (
        up_total.reshape(PLANE, rows, planes, block).transpose(1, 2, 0, 3).reshape(rows, FF)
    )
    return (
        output,
        grad_tokens,
        joined(qkv_total[:, :, :GROUP_DIM]),
        joined(qkv_total[:, :, GROUP_DIM : 2 * GROUP_DIM]),
        joined(qkv_total[:, :, 2 * GROUP_DIM :]),
        small_total[0, :rows],
        small_total[1, :rows],
        out_total,
        small_total[2, :rows],
        small_total[3, :rows],
        small_total[4, :rows],
        up_grad,
        small_total[8, :block],
        down_total,
        small_total[5, :rows],
        small_total[6, :rows],
        small_total[7, :rows],
    )


def solution(mesh):
    sheet, line = P("shard", None), P("shard")
    batch = P("rep", "shard", None)
    in_specs = (batch, P("rep", "shard"), P("rep", "shard"), sheet, sheet, sheet, line, line)
    in_specs += (sheet, line, line, line, sheet, line, sheet, line, line, line, batch)
    out_specs = (batch, batch, sheet, sheet, sheet, line, line, sheet, line, line, line)
    out_specs += (sheet, line, sheet, line, line, line)
    body = functools.partial(shards, mesh.shape["shard"], mesh.shape["rep"])
    return jax.shard_map(
        body, mesh=mesh, in_specs=in_specs, out_specs=out_specs, check_vma=False
    )
```

time: 963 us -> 592 us (0.61)
  waiting for transfers between devices: 530 us -> 0 us
  Pallas kernels: 0 us -> 405 us
  blocking collectives: 141 us -> 0 us
  local copies, waits for them, and re-layouts: 107 us -> 45.9 us
  matrix products: 129 us -> 89.9 us
  between operations: 16.8 us -> 1.85 us
  other arithmetic: 31.2 us -> 41.7 us
    pallas_call x0 -> x11, Pallas kernels: none -> 405 us  [comm_call(): pl.pallas_call(body, name=name, out_shape=out_shapes, in_specs=[VMEM_SPEC...]
    reduce_scatter x3 -> x0, waiting for transfers between devices: 262 us -> none  [the longest x1 107 us: shards(): lax.psum_scatter(key_value_terms.astype(jnp.bfloat16), 'shard', scatter_d...]
    all_gather x8 -> x0, waiting for transfers between devices: 139 us -> none  [the longest x1 45.7 us: shards(): lax.all_gather(down_weight.astype(jnp.bfloat16), 'shard', axis=0, tiled=T...]
    unnamed x3 -> x0, blocking collectives: 137 us -> none
    unnamed x16 -> x0, waiting for transfers between devices: 84.1 us -> none
    unnamed x148 -> x108, local copies, waits for them, and re-layouts: 49.3 us -> 2.41 us
    psum x1 -> x0, waiting for transfers between devices: 44.9 us -> none  [shards(): lax.psum(mixer_part, 'rep').astype(jnp.float32)]
    dot_general x60 -> x40, matrix products: 129 us -> 89.9 us  [the longest x4 14.7 us: step(): jnp.einsum('hqd,khd->hqk', upstream, value_rows, preferred_element_type=f32)]
  transfers between devices with their start and end apart: 14 -> 0, of which waited for: 11 -> 0; matrix products, arithmetic and copies ran while one was open for 16% -> 0% of each run, Pallas kernels for 0% -> 0%
where the time goes in v1:
time: 592 us; the launch traced here: 586 us
  Pallas kernels  405 us (68%)
  matrix products  89.9 us (15%)
  local copies, waits for them, and re-layouts  45.9 us (8%)
  other arithmetic  41.7 us (7%)
    pallas_call x11, Pallas kernels, comm_call(): pl.pallas_call(body, name=name, out_shape=out_shapes, in_specs=[VMEM_SPEC...  405 us
    dot_general x4, matrix products, step(): jnp.einsum('hqd,khd->hqk', upstream, value_rows, preferred_element_type=f32)  14.7 us
    dot_general x4, matrix products, dot(): return jnp.dot(left, right, preferred_element_type=f32)  14.3 us
    dot_general x4, matrix products, step(): jnp.einsum('hqk,khd->hqd', weights.astype(bf16), value_rows, preferred_el...  12.9 us
    dot_general x4, matrix products, dot_right(): lax.dot_general(left, right, (((1,), (1,)), ((), ())), preferred_element_...  11.9 us

profile of v1, /device:TPU:3, one launch (start us, length us, event | category | flops | bytes accessed | tf_op | source)
XLA Modules:
  0.0 585.6 jit_solution(14541215096538915437)
XLA Ops:
  17.8 79.3 %gather_weights.1 = (bf16[4,192,768]{2,1,0:T(8,128)(2,1)}, bf16[16,48,576]{2,1,0:T(8,128)(2,1)}, bf16[16,48,768]{2,1,0:T(8,128)(2,1)}, bf16[4,48,768]{2,1,0:T(8,...) custom-call(bf16[192,768]{1,0:T(8,128)(2,1)} %bitcast.221, ...), custom_call_target="tpu_custom_call" | custom-call | tf_op jit(solution)/shard_map/gather_weights/pallas_call | solution.py:36
  105.2 48.7 %gather_planes.1 = bf16[4,768,384]{2,1,0:T(8,128)(2,1)} custom-call(bf16[768,384]{1,0:T(8,128)(2,1)} %slice.115.x_ref), custom_call_target="tpu_custom_call" | custom-call | tf_op jit(solution)/shard_map/gather_planes/pallas_call | solution.py:36
  153.9 3.8 fusion.80
  161.4 28.2 %while.28 = (s32[]{:T(128)}, f32[3,768]{1,0:T(4,128)S(1)}, f32[3,768]{1,0:T(4,128)S(1)}, f32[3,768,64]{1,2,0:T(8,128)S(1)}, f32[768]{0:T(1024)S(1)}, /*index=5*/...) while((s32[]{:T(128)}, f32[3,768]{1,0:T(4,128)S(1)}, ...), condition=%wide.region_3.4_spmd.clone, body=%wide.region_0.3_spmd.clone.sunk | while | flops 477031680 | bytes 25817228 | solution.py:535
  165.2 3.2 fusion.137
  172.3 3.2 fusion.137
  179.3 3.2 fusion.137
  192.6 15.3 %plane_sum.4 = f32[192,768]{1,0:T(8,128)} custom-call(bf16[4,192,768]{2,1,0:T(8,128)(2,1)} %bitcast.201), custom_call_target="tpu_custom_call" | custom-call | tf_op jit(solution)/shard_map/plane_sum/pallas_call | solution.py:36
  210.3 12.6 %plane_gather.3 = bf16[4,192,768]{2,1,0:T(8,128)(2,1)} custom-call(bf16[192,768]{1,0:T(8,128)(2,1)} %fusion.63.x_ref), custom_call_target="tpu_custom_call" | custom-call | tf_op jit(solution)/shard_map/plane_gather/pallas_call | solution.py:36
  223.0 7.9 %fusion.43 = (bf16[768,768]{1,0:T(8,128)(2,1)S(1)}, f32[768,768]{1,0:T(8,128)}) fusion(f32[768]{0:T(1024)S(1)} %add.168, bf16[768,768]{1,0:T(8,128)(2,1)} %bitcast.214, bf16[768,768]{1,0:T(8,128)(2,1)S(1)} %bitcast.227), kind=kOutput, calls=%fused_computation.55 | convolution fusion | flops 944898048 | bytes 5901312 | tf_op jit(solution)/shard_map/dot_general | solution.py:491
  233.1 12.6 %plane_sum.5 = f32[192,768]{1,0:T(8,128)} custom-call(bf16[4,192,768]{2,1,0:T(8,128)(2,1)} %bitcast.220), custom_call_target="tpu_custom_call" | custom-call | tf_op jit(solution)/shard_map/plane_sum/pallas_call | solution.py:36
  253.8 12.8 %plane_gather.4 = bf16[4,192,768]{2,1,0:T(8,128)(2,1)} custom-call(bf16[192,768]{1,0:T(8,128)(2,1)} %get-tuple-element.297.x_ref), custom_call_target="tpu_custom_call" | custom-call | tf_op jit(solution)/shard_map/plane_gather/pallas_call | solution.py:36
  266.6 5.8 convert_reduce_fusion
  275.9 3.9 convolution_convert_fusion.1
  282.1 12.5 %plane_sum.6 = f32[192,768]{1,0:T(8,128)} custom-call(bf16[4,192,768]{2,1,0:T(8,128)(2,1)} %bitcast.219), custom_call_target="tpu_custom_call" | custom-call | tf_op jit(solution)/shard_map/plane_sum/pallas_call | solution.py:36
  304.2 12.7 %plane_gather.5 = bf16[4,192,768]{2,1,0:T(8,128)(2,1)} custom-call(bf16[192,768]{1,0:T(8,128)(2,1)} %get-tuple-element.299.x_ref), custom_call_target="tpu_custom_call" | custom-call | tf_op jit(solution)/shard_map/plane_gather/pallas_call | solution.py:36
  321.8 43.8 %while.29 = (s32[]{:T(128)}, f32[3,768,64]{1,2,0:T(8,128)S(1)}, bf16[4,768,384]{2,1,0:T(8,128)(2,1)}, f32[768]{0:T(1024)S(1)}, f32[4,768]{1,0:T(4,128)}, /*index...) while((s32[]{:T(128)}, f32[3,768,64]{1,2,0:T(8,128)S(1)}, ...), condition=%wide.region_14.15_spmd.clone, body=%wide.region_13.14_spmd.clone.sunk | while | flops 1152663552 | bytes 41072828 | solution.py:560
  326.0 3.7 fusion.149
  336.9 3.7 fusion.149
  347.8 3.7 fusion.149
  358.7 3.7 fusion.149
  365.6 55.3 %sum_planes.1 = bf16[768,384]{1,0:T(8,128)(2,1)} custom-call(bf16[4,768,384]{2,1,0:T(8,128)(2,1)} %get-tuple-element.145.p_ref), custom_call_target="tpu_custom_call" | custom-call | tf_op jit(solution)/shard_map/sum_planes/pallas_call | solution.py:36
  426.2 13.7 %plane_sum.7 = f32[192,768]{1,0:T(8,128)} custom-call(bf16[4,192,768]{2,1,0:T(8,128)(2,1)} %bitcast.218), custom_call_target="tpu_custom_call" | custom-call | tf_op jit(solution)/shard_map/plane_sum/pallas_call | solution.py:36
  444.2 130.0 %reduce_grads.1 = (f32[4,48,576]{2,1,0:T(8,128)}, f32[4,48,768]{2,1,0:T(8,128)}, f32[48,768]{1,0:T(8,128)}, f32[16,256]{1,0:T(8,128)}, f32[192,768]{1,0:T(8,128)}) custom-call(bf16[16,48,576]{2,1,0:T(8,128)(2,1)} %bitcast.202, bf16[16,48,768]{2,1,0:T(8,128)(2,1)} %bitcast.209, bf16[4,48,768]{2,1,0:T(8,128)(2,1)} %bitcast.207, ...), custom_call_target="tpu_custom_call" | custom-call | tf_op jit(solution)/shard_map/reduce_grads/pallas_call | solution.py:36
  (328 shorter events, 131.6 us)
Async XLA Ops:
  99.2 123.8 %copy-start.45 = (f32[768]{0:T(1024)}, f32[768]{0:T(1024)S(1)}, u32[]{:S(2)}) copy-start(f32[768]{0:T(1024)S(1)} %add.168) | copy-start | bytes 9220
  99.3 110.2 %copy-start.18 = (f32[768]{0:T(1024)}, f32[768]{0:T(1024)S(1)}, u32[]{:S(2)}) copy-start(f32[768]{0:T(1024)S(1)} %mul.216) | copy-start | bytes 9220
  99.4 110.1 %copy-start.26 = (f32[768]{0:T(1024)}, f32[768]{0:T(1024)S(1)}, u32[]{:S(2)}) copy-start(f32[768]{0:T(1024)S(1)} %add.164) | copy-start | bytes 9220
  161.4 29.6 %copy-start.7 = (bf16[4,48,768]{2,1,0:T(8,128)(2,1)S(1)}, bf16[4,48,768]{2,1,0:T(8,128)(2,1)}, u32[]{:S(2)}) copy-start(bf16[4,48,768]{2,1,0:T(8,128)(2,1)} %get-tuple-element.140) | copy-start | bytes 884740
  189.6 19.6 %copy-start.15 = (f32[4,768]{1,0:T(4,128)}, f32[4,768]{1,0:T(4,128)S(1)}, u32[]{:S(2)}) copy-start(f32[4,768]{1,0:T(4,128)S(1)} %get-tuple-element.568) | copy-start | bytes 36868
  189.6 18.2 %copy-start.10 = (bf16[1,192,768]{2,1,0:T(8,128)(2,1)S(1)}, bf16[1,192,768]{2,1,0:T(8,128)(2,1)}, u32[]{:S(2)}) copy-start(bf16[1,192,768]{2,1,0:T(8,128)(2,1)} %param.23) | copy-start | bytes 884740
  207.8 15.2 %copy-start.47 = (bf16[16,48,768]{2,1,0:T(8,128)(2,1)S(1)}, bf16[16,48,768]{2,1,0:T(8,128)(2,1)}, u32[]{:S(2)}) copy-start(bf16[16,48,768]{2,1,0:T(8,128)(2,1)} %get-tuple-element.141) | copy-start | bytes 3538948
  209.2 36.5 %copy-start.24 = (f32[192]{0:T(256)}, f32[192]{0:T(256)S(1)}, u32[]{:S(2)}) copy-start(f32[192]{0:T(256)S(1)} %broadcast_multiply_fusion.5) | copy-start | bytes 2308
  209.4 36.3 %copy-start.34 = (f32[192]{0:T(256)}, f32[192]{0:T(256)S(1)}, u32[]{:S(2)}) copy-start(f32[192]{0:T(256)S(1)} %add_rsqrt_fusion.1) | copy-start | bytes 2308
  279.8 14.8 %copy-start.22 = (f32[768]{0:T(1024)S(1)}, f32[768]{0:T(1024)}, u32[]{:S(2)}) copy-start(f32[768]{0:T(1024)} %mul.225) | copy-start | bytes 9220
  279.8 14.8 %copy-start.25 = (f32[192]{0:T(256)S(1)}, f32[192]{0:T(256)}, u32[]{:S(2)}) copy-start(f32[192]{0:T(256)} %copy-done.24) | copy-start | bytes 2308
  279.8 14.8 %copy-start.35 = (f32[192]{0:T(256)S(1)}, f32[192]{0:T(256)}, u32[]{:S(2)}) copy-start(f32[192]{0:T(256)} %copy-done.34) | copy-start | bytes 2308
  297.6 19.3 %copy-start.2 = (bf16[3,768,64]{1,2,0:T(8,128)(2,1)S(1)}, bf16[3,768,64]{1,2,0:T(8,128)(2,1)}, u32[]{:S(2)}) copy-start(bf16[3,768,64]{1,2,0:T(8,128)(2,1)} %copy-done.1) | copy-start | bytes 884740
  297.6 21.7 %copy-start.8 = (bf16[4,48,768]{2,1,0:T(8,128)(2,1)S(1)}, bf16[4,48,768]{2,1,0:T(8,128)(2,1)}, u32[]{:S(2)}) copy-start(bf16[4,48,768]{2,1,0:T(8,128)(2,1)} %get-tuple-element.140) | copy-start | bytes 884740
  304.2 16.9 %copy-start.5 = (f32[3,768,64]{1,2,0:T(8,128)S(1)}, f32[3,768,64]{1,2,0:T(8,128)}, u32[]{:S(2)}) copy-start(f32[3,768,64]{1,2,0:T(8,128)} %copy-done.4) | copy-start | bytes 1769476
  365.6 55.5 %copy-start.46 = (bf16[4,192,768]{2,1,0:T(8,128)(2,1)S(1)}, bf16[4,192,768]{2,1,0:T(8,128)(2,1)}, u32[]{:S(2)}) copy-start(bf16[4,192,768]{2,1,0:T(8,128)(2,1)} %get-tuple-element.136) | copy-start | bytes 3538948
  424.0 15.9 %copy-start.3 = (f32[192,768]{1,0:T(8,128)S(1)}, f32[192,768]{1,0:T(8,128)}, u32[]{:S(2)}) copy-start(f32[192,768]{1,0:T(8,128)} %get-tuple-element.300) | copy-start | bytes 1769476
  426.1 15.9 %copy-start.28 = (bf16[16,1,48]{2,1,0:T(2,128)(2,1)S(1)}, bf16[16,1,48]{2,1,0:T(2,128)(2,1)}, u32[]{:S(2)}) copy-start(bf16[16,1,48]{2,1,0:T(2,128)(2,1)} %stack_reshape.47) | copy-start | bytes 4612
  426.1 15.9 %copy-start.29 = (bf16[16,1,48]{2,1,0:T(2,128)(2,1)S(1)}, bf16[16,1,48]{2,1,0:T(2,128)(2,1)}, u32[]{:S(2)}) copy-start(bf16[16,1,48]{2,1,0:T(2,128)(2,1)} %stack_reshape.46) | copy-start | bytes 4612
  426.1 15.9 %copy-start.30 = (bf16[16,1,48]{2,1,0:T(2,128)(2,1)S(1)}, bf16[16,1,48]{2,1,0:T(2,128)(2,1)}, u32[]{:S(2)}) copy-start(bf16[16,1,48]{2,1,0:T(2,128)(2,1)} %stack_reshape.45) | copy-start | bytes 4612
  426.1 15.9 %copy-start.31 = (bf16[16,1,48]{2,1,0:T(2,128)(2,1)S(1)}, bf16[16,1,48]{2,1,0:T(2,128)(2,1)}, u32[]{:S(2)}) copy-start(bf16[16,1,48]{2,1,0:T(2,128)(2,1)} %stack_reshape.42) | copy-start | bytes 4612
  426.1 16.0 %copy-start.32 = (bf16[16,1,48]{2,1,0:T(2,128)(2,1)S(1)}, bf16[16,1,48]{2,1,0:T(2,128)(2,1)}, u32[]{:S(2)}) copy-start(bf16[16,1,48]{2,1,0:T(2,128)(2,1)} %stack_reshape.43) | copy-start | bytes 4612
  426.2 16.0 %copy-start.33 = (bf16[16,1,48]{2,1,0:T(2,128)(2,1)S(1)}, bf16[16,1,48]{2,1,0:T(2,128)(2,1)}, u32[]{:S(2)}) copy-start(bf16[16,1,48]{2,1,0:T(2,128)(2,1)} %stack_reshape.44) | copy-start | bytes 4612
  426.2 16.1 %copy-start.23 = (bf16[16,1,192]{2,1,0:T(2,128)(2,1)S(1)}, bf16[16,1,192]{2,1,0:T(2,128)(2,1)}, u32[]{:S(2)}) copy-start(bf16[16,1,192]{2,1,0:T(2,128)(2,1)} %multiply_convert_fusion.1) | copy-start | bytes 18436
  (33 other events, 253.7 us)

commit v2 on v1

--- a/solution.py
+++ b/solution.py
@@ -166,17 +166,20 @@
     return [{"shard": lax.rem(me + step, count)} for step in range(1, count)]
 
 
-def gather_weights(count, tokens, qkv, up, out_w, down, small, ident):
+def gather_weights(count, copies, tokens, qkv, up, out_w, down, small, ident):
     planes = count // PLANE
     rows = qkv.shape[1]
     block = down.shape[0]
 
     def body(x_ref, qkv_ref, up_ref, wo_ref, down_ref, small_ref, *rest):
         x_out, qkv_out, up_out, wo_out, down_out, small_out = rest[:6]
-        send, recv, local, send_wo, recv_wo = rest[6:]
+        send, recv, local, send_wo, recv_wo, send_unit, recv_unit = rest[6:]
         me = lax.axis_index("shard")
         group, plane = lax.rem(me, PLANE), lax.div(me, PLANE)
-        greet(others(me, count))
+        across = [
+            {"rep": lax.rem(lax.axis_index("rep") + step, copies)} for step in range(1, copies)
+        ]
+        greet(others(me, count) + across)
         owns = [
             (x_ref, x_out.at[group]),
             (qkv_ref.at[group], qkv_out.at[me]),
@@ -199,13 +202,62 @@
 
         for mask in (2, 1, 3):
             push(x_ref, x_out.at[group], plane_peer(me, mask))
-        for src, dst in ((small_ref, small_out), (qkv_ref, qkv_out), (up_ref, up_out)):
-            for step in range(1, count):
-                peer = lax.rem(me + step, count)
-                piece = src if src is small_ref else src.at[lax.rem(peer, PLANE)]
-                push(piece, dst.at[me], peer)
-        for step in range(1, planes):
-            push(down_ref, down_out.at[plane], lax.rem(me + PLANE * step, count))
+        for step in range(1, count):
+            push(small_ref, small_out.at[me], lax.rem(me + step, count))
+        rep = lax.axis_index("rep")
+        split = copies == 2
+        units = []
+        for step in range(planes):
+            for lane in range(PLANE):
+                if step or lane:
+                    units.append((qkv_ref, qkv_out, step, lane))
+        for step in range(planes):
+            for lane in range(PLANE):
+                if step or lane:
+                    units.append((up_ref, up_out, step, lane))
+            if step:
+                units.append((down_ref, down_out, step, 0))
+
+        def unit_copy(index):
+            src, dst, step, lane = units[index]
+            goal = lax.rem(plane + step, planes)
+            goal_group = lax.rem(group + lane, PLANE)
+            piece, slot = (src, plane) if src is down_ref else (src.at[goal_group], me)
+            return remote(
+                piece,
+                dst.at[slot],
+                send_unit.at[index],
+                recv_unit.at[index],
+                {"shard": goal * PLANE + goal_group},
+            )
+
+        def unit_relay(index):
+            src, dst, step, lane = units[index]
+            origin = lax.rem(plane + planes - step, planes)
+            origin_group = lax.rem(group + PLANE - lane, PLANE)
+            slot = origin if src is down_ref else origin * PLANE + origin_group
+            return remote(
+                dst.at[slot],
+                dst.at[slot],
+                send_unit.at[index],
+                recv_unit.at[index],
+                {"rep": lax.rem(rep + 1, copies)},
+            )
+
+        def carried(index, mine):
+            step = units[index][2]
+            if not split or step == 0:
+                return None
+            return (rep == step % 2) if mine else (rep != step % 2)
+
+        def guarded(test, action):
+            if test is None:
+                action()
+            else:
+                pl.when(test)(action)
+
+        for index in range(len(units)):
+            guarded(carried(index, True), unit_copy(index).start)
         target, place = lax.div(me, planes), lax.rem(me, planes)
 
         def wo_copy(source, index):
@@ -219,6 +271,22 @@
             pl.when(peer != me)(copy.start)
         keep = pltpu.make_async_copy(wo_ref, wo_out.at[place], local.at[5])
         pl.when(target == group)(keep.start)
+        for index, (_, _, step, _) in enumerate(units):
+            if split and step:
+
+                @pl.when(rep == step % 2)
+                def _(index=index):
+                    unit_relay(index).wait_recv()
+                    unit_copy(index).wait_send()
+                    unit_relay(index).start()
+
+            else:
+                unit_copy(index).wait_recv()
+                unit_copy(index).wait_send()
+        for index, (_, _, step, _) in enumerate(units):
+            if split and step:
+                pl.when(rep != step % 2)(unit_relay(index).wait_recv)
+                pl.when(rep == step % 2)(unit_relay(index).wait_send)
         for copy in sent:
             copy.wait_recv()
         for index in range(planes):
@@ -232,7 +300,8 @@
         for copy in started:
             copy.wait()
 
-    total = 3 + 3 * (count - 1) + planes - 1
+    total = 3 + count - 1
+    number = 2 * (count - 1) + planes - 1
     return comm_call(
         body,
         "gather_weights",
@@ -253,6 +322,8 @@
             pltpu.SemaphoreType.DMA((6,)),
             pltpu.SemaphoreType.DMA((planes,)),
             pltpu.SemaphoreType.DMA((planes,)),
+            pltpu.SemaphoreType.DMA((number,)),
+            pltpu.SemaphoreType.DMA((number,)),
         ],
     )
 
@@ -263,19 +334,54 @@
     def body(x_ref, out_ref, send, recv, local):
         me = lax.axis_index("shard")
         plane = lax.div(me, PLANE)
-        peers = [{"shard": lax.rem(me + PLANE * s, count)} for s in range(1, planes)]
-        greet(peers)
+        greet([{"shard": lax.rem(me + PLANE * s, count)} for s in range(1, planes)])
         own = pltpu.make_async_copy(x_ref, out_ref.at[plane], local)
         own.start()
-        sent = []
-        for index, peer in enumerate(peers):
-            copy = remote(x_ref, out_ref.at[plane], send.at[index], recv.at[index], peer)
-            copy.start()
-            sent.append(copy)
-        for copy in sent:
-            copy.wait_recv()
-        for copy in sent:
-            copy.wait_send()
+
+        def hop(way, source, src):
+            peer = me + PLANE if way == 0 else me - PLANE
+            return remote(
+                src,
+                out_ref.at[source],
+                send.at[way, source],
+                recv.at[way, source],
+                {"shard": lax.rem(peer + count, count)},
+            )
+
+        @pl.when(plane < planes - 1)
+        def _():
+            hop(0, plane, x_ref).start()
+
+        @pl.when(plane > 0)
+        def _():
+            hop(1, plane, x_ref).start()
+
+        for step in range(1, planes):
+            for way, source in ((0, plane - step), (1, plane + step)):
+                onward = plane < planes - 1 if way == 0 else plane > 0
+
+                @pl.when((source >= 0) & (source < planes))
+                def _(way=way, source=source, onward=onward):
+                    copy = hop(way, source, out_ref.at[source])
+                    copy.wait_recv()
+                    pl.when(onward)(copy.start)
+
+        @pl.when(plane < planes - 1)
+        def _():
+            hop(0, plane, x_ref).wait_send()
+
+        @pl.when(plane > 0)
+        def _():
+            hop(1, plane, x_ref).wait_send()
+
+        for step in range(1, planes):
+            for way, source in ((0, plane - step), (1, plane + step)):
+                onward = plane < planes - 1 if way == 0 else plane > 0
+
+                @pl.when((source >= 0) & (source < planes) & onward)
+                def _(way=way, source=source):
+                    hop(way, source, out_ref.at[source]).wait_send()
+
         own.wait()
 
     return comm_call(
@@ -286,8 +392,8 @@
         struct((planes,) + value.shape),
         ANY_SPEC,
         [
-            pltpu.SemaphoreType.DMA((planes,)),
-            pltpu.SemaphoreType.DMA((planes,)),
+            pltpu.SemaphoreType.DMA((2, planes)),
+            pltpu.SemaphoreType.DMA((2, planes)),
             pltpu.SemaphoreType.DMA,
         ],
     )
@@ -296,30 +402,55 @@
 def sum_planes(count, parts, ident):
     planes, rows, cols = parts.shape
 
-    def body(p_ref, out_ref, held, send, recv):
+    def body(p_ref, out_ref, held, staged, send, recv):
         me = lax.axis_index("shard")
         plane = lax.div(me, PLANE)
-        peers = [lax.rem(me + PLANE * s, count) for s in range(1, planes)]
-        greet([{"shard": peer} for peer in peers])
-        sent = []
-        for index, peer in enumerate(peers):
-            copy = remote(
-                p_ref.at[lax.div(peer, PLANE)],
-                held.at[index],
-                send.at[index],
-                recv.at[index],
-                {"shard": peer},
+        greet([{"shard": lax.rem(me + PLANE * s, count)} for s in range(1, planes)])
+
+        def hop(way, goal, src):
+            peer = me + PLANE if way == 0 else me - PLANE
+            return remote(
+                src,
+                held.at[way, goal],
+                send.at[goal],
+                recv.at[way, goal],
+                {"shard": lax.rem(peer + count, count)},
             )
-            copy.start()
-            sent.append(copy)
-        for copy in sent:
-            copy.wait_recv()
-        total = p_ref[plane].astype(f32)
-        for index in range(planes - 1):
-            total = total + held[index].astype(f32)
-        out_ref[...] = total.astype(bf16)
-        for copy in sent:
-            copy.wait_send()
+
+        for step in range(planes - 1):
+            for way, goal in ((0, planes - 1 - step), (1, step)):
+                ahead = goal > plane if way == 0 else goal < plane
+                first = plane == 0 if way == 0 else plane == planes - 1
+
+                @pl.when(ahead & first)
+                def _(way=way, goal=goal):
+                    hop(way, goal, p_ref.at[goal]).start()
+
+                @pl.when(ahead & jnp.logical_not(first))
+                def _(way=way, goal=goal):
+                    copy = hop(way, goal, staged.at[goal])
+                    copy.wait_recv()
+                    total = p_ref[goal].astype(f32) + held[way, goal].astype(f32)
+                    staged[goal] = total.astype(bf16)
+                    copy.start()
+
+        out_ref[...] = p_ref[plane]
+
+        @pl.when(plane > 0)
+        def _():
+            hop(0, plane, staged.at[plane]).wait_recv()
+            out_ref[...] = (out_ref[...].astype(f32) + held[0, plane].astype(f32)).astype(bf16)
+
+        @pl.when(plane < planes - 1)
+        def _():
+            hop(1, plane, staged.at[plane]).wait_recv()
+            out_ref[...] = (out_ref[...].astype(f32) + held[1, plane].astype(f32)).astype(bf16)
+
+        for goal in range(planes):
+
+            @pl.when(goal != plane)
+            def _(goal=goal):
+                hop(0, goal, staged.at[goal]).wait_send()
 
     return comm_call(
         body,
@@ -329,9 +460,10 @@
         struct((rows, cols)),
         VMEM_SPEC,
         [
-            pltpu.VMEM((planes - 1, rows, cols), bf16),
+            pltpu.VMEM((2, planes, rows, cols), bf16),
+            pltpu.VMEM((planes, rows, cols), bf16),
             pltpu.SemaphoreType.DMA((planes,)),
-            pltpu.SemaphoreType.DMA((planes,)),
+            pltpu.SemaphoreType.DMA((2, planes)),
         ],
     )
 
@@ -627,6 +759,7 @@
     ).astype(bf16)
     x_all, qkv_all, up_all, wo_all, down_all, small = gather_weights(
         count,
+        copies,
         x_own,
         qkv_send,
         up_send,

time: 592 us -> 573 us (0.968); the launches traced: 586 us -> 573 us
  Pallas kernels: 405 us -> 393 us
    pallas_call x11, Pallas kernels: 405 us -> 393 us  [comm_call(): pl.pallas_call(body, name=name, out_shape=out_shapes, in_specs=[VMEM_SPEC...]
where the time goes in v2:
time: 573 us
  Pallas kernels  393 us (69%)
  matrix products  89.9 us (16%)
  local copies, waits for them, and re-layouts  45.6 us (8%)
  other arithmetic  41.7 us (7%)
    pallas_call x11, Pallas kernels, comm_call(): pl.pallas_call(body, name=name, out_shape=out_shapes, in_specs=[VMEM_SPEC...  393 us
    dot_general x4, matrix products, step(): jnp.einsum('hqd,khd->hqk', upstream, value_rows, preferred_element_type=f32)  14.7 us
    dot_general x4, matrix products, dot(): return jnp.dot(left, right, preferred_element_type=f32)  14.3 us
    dot_general x4, matrix products, step(): jnp.einsum('hqk,khd->hqd', weights.astype(bf16), value_rows, preferred_el...  12.9 us
    dot_general x4, matrix products, dot_right(): lax.dot_general(left, right, (((1,), (1,)), ((), ())), preferred_element_...  12 us

profile of v2, /device:TPU:3, one launch (start us, length us, event | category | flops | bytes accessed | tf_op | source)
XLA Modules:
  0.0 573.0 jit_solution(14357953845404334768)
XLA Ops:
  17.8 71.9 %gather_weights.1 = (bf16[4,192,768]{2,1,0:T(8,128)(2,1)}, bf16[16,48,576]{2,1,0:T(8,128)(2,1)}, bf16[16,48,768]{2,1,0:T(8,128)(2,1)}, bf16[4,48,768]{2,1,0:T(8,...) custom-call(bf16[192,768]{1,0:T(8,128)(2,1)} %bitcast.221, ...), custom_call_target="tpu_custom_call" | custom-call | tf_op jit(solution)/shard_map/gather_weights/pallas_call | solution.py:36
  97.7 44.7 %gather_planes.1 = bf16[4,768,384]{2,1,0:T(8,128)(2,1)} custom-call(bf16[768,384]{1,0:T(8,128)(2,1)} %slice.115.x_ref), custom_call_target="tpu_custom_call" | custom-call | tf_op jit(solution)/shard_map/gather_planes/pallas_call | solution.py:36
  142.4 3.8 fusion.80
  149.6 28.1 %while.28 = (s32[]{:T(128)}, f32[3,768]{1,0:T(4,128)S(1)}, f32[3,768]{1,0:T(4,128)S(1)}, f32[3,768,64]{1,2,0:T(8,128)S(1)}, f32[768]{0:T(1024)S(1)}, /*index=5*/...) while((s32[]{:T(128)}, f32[3,768]{1,0:T(4,128)S(1)}, ...), condition=%wide.region_3.4_spmd.clone, body=%wide.region_0.3_spmd.clone.sunk | while | flops 477031680 | bytes 25817228 | solution.py:667
  153.4 3.2 fusion.137
  160.4 3.2 fusion.137
  174.5 3.2 fusion.137
  180.7 13.4 %plane_sum.4 = f32[192,768]{1,0:T(8,128)} custom-call(bf16[4,192,768]{2,1,0:T(8,128)(2,1)} %bitcast.201), custom_call_target="tpu_custom_call" | custom-call | tf_op jit(solution)/shard_map/plane_sum/pallas_call | solution.py:36
  196.6 12.6 %plane_gather.3 = bf16[4,192,768]{2,1,0:T(8,128)(2,1)} custom-call(bf16[192,768]{1,0:T(8,128)(2,1)} %fusion.63.x_ref), custom_call_target="tpu_custom_call" | custom-call | tf_op jit(solution)/shard_map/plane_gather/pallas_call | solution.py:36
  209.3 7.9 %fusion.43 = (bf16[768,768]{1,0:T(8,128)(2,1)S(1)}, f32[768,768]{1,0:T(8,128)}) fusion(f32[768]{0:T(1024)S(1)} %add.168, bf16[768,768]{1,0:T(8,128)(2,1)} %bitcast.214, bf16[768,768]{1,0:T(8,128)(2,1)S(1)} %bitcast.227), kind=kOutput, calls=%fused_computation.55 | convolution fusion | flops 944898048 | bytes 5901312 | tf_op jit(solution)/shard_map/dot_general | solution.py:623
  219.4 12.6 %plane_sum.5 = f32[192,768]{1,0:T(8,128)} custom-call(bf16[4,192,768]{2,1,0:T(8,128)(2,1)} %bitcast.220), custom_call_target="tpu_custom_call" | custom-call | tf_op jit(solution)/shard_map/plane_sum/pallas_call | solution.py:36
  240.0 25.4 %plane_gather.4 = bf16[4,192,768]{2,1,0:T(8,128)(2,1)} custom-call(bf16[192,768]{1,0:T(8,128)(2,1)} %get-tuple-element.297.x_ref), custom_call_target="tpu_custom_call" | custom-call | tf_op jit(solution)/shard_map/plane_gather/pallas_call | solution.py:36
  265.4 5.8 %convert_reduce_fusion = (f32[768]{0:T(1024)}, bf16[768,768]{1,0:T(8,128)(2,1)}) fusion(f32[768,768]{1,0:T(8,128)} %get-tuple-element.323, f32[768]{0:T(1024)} %copy-done.45, bf16[768,768]{1,0:T(8,128)(2,1)} %bitcast.216, bf16[768,768]{1,0:T(8,128)(2,1)} %bitcast.229), kind=kOutput, calls=%fused_computation.61 | convolution fusion | flops 913636608 | bytes 5904384 | tf_op jit(solution)/shard_map/dot_general | solution.py:631
  274.7 3.9 convolution_convert_fusion.1
  280.9 12.5 %plane_sum.6 = f32[192,768]{1,0:T(8,128)} custom-call(bf16[4,192,768]{2,1,0:T(8,128)(2,1)} %bitcast.219), custom_call_target="tpu_custom_call" | custom-call | tf_op jit(solution)/shard_map/plane_sum/pallas_call | solution.py:36
  303.0 12.7 %plane_gather.5 = bf16[4,192,768]{2,1,0:T(8,128)(2,1)} custom-call(bf16[192,768]{1,0:T(8,128)(2,1)} %get-tuple-element.299.x_ref), custom_call_target="tpu_custom_call" | custom-call | tf_op jit(solution)/shard_map/plane_gather/pallas_call | solution.py:36
  320.7 43.6 %while.29 = (s32[]{:T(128)}, f32[3,768,64]{1,2,0:T(8,128)S(1)}, bf16[4,768,384]{2,1,0:T(8,128)(2,1)}, f32[768]{0:T(1024)S(1)}, f32[4,768]{1,0:T(4,128)}, /*index...) while((s32[]{:T(128)}, f32[3,768,64]{1,2,0:T(8,128)S(1)}, ...), condition=%wide.region_14.15_spmd.clone, body=%wide.region_13.14_spmd.clone.sunk | while | flops 1152663552 | bytes 41072828 | solution.py:692
  324.6 3.7 fusion.149
  335.5 3.7 fusion.149
  346.4 3.7 fusion.149
  357.3 3.7 fusion.149
  364.3 52.4 %sum_planes.1 = bf16[768,384]{1,0:T(8,128)(2,1)} custom-call(bf16[4,768,384]{2,1,0:T(8,128)(2,1)} %get-tuple-element.145.p_ref), custom_call_target="tpu_custom_call" | custom-call | tf_op jit(solution)/shard_map/sum_planes/pallas_call | solution.py:36
  422.0 17.8 %plane_sum.7 = f32[192,768]{1,0:T(8,128)} custom-call(bf16[4,192,768]{2,1,0:T(8,128)(2,1)} %bitcast.218), custom_call_target="tpu_custom_call" | custom-call | tf_op jit(solution)/shard_map/plane_sum/pallas_call | solution.py:36
  444.2 117.5 %reduce_grads.1 = (f32[4,48,576]{2,1,0:T(8,128)}, f32[4,48,768]{2,1,0:T(8,128)}, f32[48,768]{1,0:T(8,128)}, f32[16,256]{1,0:T(8,128)}, f32[192,768]{1,0:T(8,128)}) custom-call(bf16[16,48,576]{2,1,0:T(8,128)(2,1)} %bitcast.202, bf16[16,48,768]{2,1,0:T(8,128)(2,1)} %bitcast.209, bf16[4,48,768]{2,1,0:T(8,128)(2,1)} %bitcast.207, ...), custom_call_target="tpu_custom_call" | custom-call | tf_op jit(solution)/shard_map/reduce_grads/pallas_call | solution.py:36
  (328 shorter events, 131.3 us)
Async XLA Ops:
  91.7 117.5 %copy-start.45 = (f32[768]{0:T(1024)}, f32[768]{0:T(1024)S(1)}, u32[]{:S(2)}) copy-start(f32[768]{0:T(1024)S(1)} %add.168) | copy-start | bytes 9220
  91.8 103.9 %copy-start.18 = (f32[768]{0:T(1024)}, f32[768]{0:T(1024)S(1)}, u32[]{:S(2)}) copy-start(f32[768]{0:T(1024)S(1)} %mul.216) | copy-start | bytes 9220
  91.9 103.8 %copy-start.26 = (f32[768]{0:T(1024)}, f32[768]{0:T(1024)S(1)}, u32[]{:S(2)}) copy-start(f32[768]{0:T(1024)S(1)} %add.164) | copy-start | bytes 9220
  149.6 29.6 %copy-start.7 = (bf16[4,48,768]{2,1,0:T(8,128)(2,1)S(1)}, bf16[4,48,768]{2,1,0:T(8,128)(2,1)}, u32[]{:S(2)}) copy-start(bf16[4,48,768]{2,1,0:T(8,128)(2,1)} %get-tuple-element.140) | copy-start | bytes 884740
  177.8 17.6 %copy-start.15 = (f32[4,768]{1,0:T(4,128)}, f32[4,768]{1,0:T(4,128)S(1)}, u32[]{:S(2)}) copy-start(f32[4,768]{1,0:T(4,128)S(1)} %get-tuple-element.568) | copy-start | bytes 36868
  177.8 16.3 %copy-start.10 = (bf16[1,192,768]{2,1,0:T(8,128)(2,1)S(1)}, bf16[1,192,768]{2,1,0:T(8,128)(2,1)}, u32[]{:S(2)}) copy-start(bf16[1,192,768]{2,1,0:T(8,128)(2,1)} %param.23) | copy-start | bytes 884740
  194.1 15.2 %copy-start.47 = (bf16[16,48,768]{2,1,0:T(8,128)(2,1)S(1)}, bf16[16,48,768]{2,1,0:T(8,128)(2,1)}, u32[]{:S(2)}) copy-start(bf16[16,48,768]{2,1,0:T(8,128)(2,1)} %get-tuple-element.141) | copy-start | bytes 3538948
  195.4 36.5 %copy-start.24 = (f32[192]{0:T(256)}, f32[192]{0:T(256)S(1)}, u32[]{:S(2)}) copy-start(f32[192]{0:T(256)S(1)} %broadcast_multiply_fusion.5) | copy-start | bytes 2308
  195.7 36.3 %copy-start.34 = (f32[192]{0:T(256)}, f32[192]{0:T(256)S(1)}, u32[]{:S(2)}) copy-start(f32[192]{0:T(256)S(1)} %add_rsqrt_fusion.1) | copy-start | bytes 2308
  278.6 14.8 %copy-start.22 = (f32[768]{0:T(1024)S(1)}, f32[768]{0:T(1024)}, u32[]{:S(2)}) copy-start(f32[768]{0:T(1024)} %mul.225) | copy-start | bytes 9220
  278.6 14.8 %copy-start.25 = (f32[192]{0:T(256)S(1)}, f32[192]{0:T(256)}, u32[]{:S(2)}) copy-start(f32[192]{0:T(256)} %copy-done.24) | copy-start | bytes 2308
  278.6 14.8 %copy-start.35 = (f32[192]{0:T(256)S(1)}, f32[192]{0:T(256)}, u32[]{:S(2)}) copy-start(f32[192]{0:T(256)} %copy-done.34) | copy-start | bytes 2308
  296.4 19.3 %copy-start.2 = (bf16[3,768,64]{1,2,0:T(8,128)(2,1)S(1)}, bf16[3,768,64]{1,2,0:T(8,128)(2,1)}, u32[]{:S(2)}) copy-start(bf16[3,768,64]{1,2,0:T(8,128)(2,1)} %copy-done.1) | copy-start | bytes 884740
  296.4 21.7 %copy-start.8 = (bf16[4,48,768]{2,1,0:T(8,128)(2,1)S(1)}, bf16[4,48,768]{2,1,0:T(8,128)(2,1)}, u32[]{:S(2)}) copy-start(bf16[4,48,768]{2,1,0:T(8,128)(2,1)} %get-tuple-element.140) | copy-start | bytes 884740
  303.0 16.9 %copy-start.5 = (f32[3,768,64]{1,2,0:T(8,128)S(1)}, f32[3,768,64]{1,2,0:T(8,128)}, u32[]{:S(2)}) copy-start(f32[3,768,64]{1,2,0:T(8,128)} %copy-done.4) | copy-start | bytes 1769476
  364.3 52.7 %copy-start.46 = (bf16[4,192,768]{2,1,0:T(8,128)(2,1)S(1)}, bf16[4,192,768]{2,1,0:T(8,128)(2,1)}, u32[]{:S(2)}) copy-start(bf16[4,192,768]{2,1,0:T(8,128)(2,1)} %get-tuple-element.136) | copy-start | bytes 3538948
  419.8 20.0 %copy-start.3 = (f32[192,768]{1,0:T(8,128)S(1)}, f32[192,768]{1,0:T(8,128)}, u32[]{:S(2)}) copy-start(f32[192,768]{1,0:T(8,128)} %get-tuple-element.300) | copy-start | bytes 1769476
  421.9 20.0 %copy-start.28 = (bf16[16,1,48]{2,1,0:T(2,128)(2,1)S(1)}, bf16[16,1,48]{2,1,0:T(2,128)(2,1)}, u32[]{:S(2)}) copy-start(bf16[16,1,48]{2,1,0:T(2,128)(2,1)} %stack_reshape.47) | copy-start | bytes 4612
  421.9 20.1 %copy-start.29 = (bf16[16,1,48]{2,1,0:T(2,128)(2,1)S(1)}, bf16[16,1,48]{2,1,0:T(2,128)(2,1)}, u32[]{:S(2)}) copy-start(bf16[16,1,48]{2,1,0:T(2,128)(2,1)} %stack_reshape.46) | copy-start | bytes 4612
  421.9 20.1 %copy-start.30 = (bf16[16,1,48]{2,1,0:T(2,128)(2,1)S(1)}, bf16[16,1,48]{2,1,0:T(2,128)(2,1)}, u32[]{:S(2)}) copy-start(bf16[16,1,48]{2,1,0:T(2,128)(2,1)} %stack_reshape.45) | copy-start | bytes 4612
  421.9 20.1 %copy-start.31 = (bf16[16,1,48]{2,1,0:T(2,128)(2,1)S(1)}, bf16[16,1,48]{2,1,0:T(2,128)(2,1)}, u32[]{:S(2)}) copy-start(bf16[16,1,48]{2,1,0:T(2,128)(2,1)} %stack_reshape.42) | copy-start | bytes 4612
  421.9 20.1 %copy-start.32 = (bf16[16,1,48]{2,1,0:T(2,128)(2,1)S(1)}, bf16[16,1,48]{2,1,0:T(2,128)(2,1)}, u32[]{:S(2)}) copy-start(bf16[16,1,48]{2,1,0:T(2,128)(2,1)} %stack_reshape.43) | copy-start | bytes 4612
  422.0 20.1 %copy-start.33 = (bf16[16,1,48]{2,1,0:T(2,128)(2,1)S(1)}, bf16[16,1,48]{2,1,0:T(2,128)(2,1)}, u32[]{:S(2)}) copy-start(bf16[16,1,48]{2,1,0:T(2,128)(2,1)} %stack_reshape.44) | copy-start | bytes 4612
  422.0 20.2 %copy-start.23 = (bf16[16,1,192]{2,1,0:T(2,128)(2,1)S(1)}, bf16[16,1,192]{2,1,0:T(2,128)(2,1)}, u32[]{:S(2)}) copy-start(bf16[16,1,192]{2,1,0:T(2,128)(2,1)} %multiply_convert_fusion.1) | copy-start | bytes 18436
  (33 other events, 253.6 us)

commit v3 on v2

--- a/solution.py
+++ b/solution.py
@@ -26,6 +26,7 @@
 VMEM_SPEC = pl.BlockSpec(memory_space=pltpu.VMEM)
 ANY_SPEC = pl.BlockSpec(memory_space=pl.ANY)
 VMEM_BYTES = 60000 * 1024
+MODEL_BYTES = 100_000_000
 
 
 def struct(shape, dtype=bf16):
@@ -40,6 +41,7 @@
         in_specs=[VMEM_SPEC] * len(inputs),
         out_specs=out_specs,
         scratch_shapes=scratch,
+        cost_estimate=pl.CostEstimate(flops=0, bytes_accessed=MODEL_BYTES, transcendentals=0),
         compiler_params=pltpu.CompilerParams(
             collective_id=ident, has_side_effects=True, vmem_limit_bytes=VMEM_BYTES
         ),
@@ -166,14 +168,13 @@
     return [{"shard": lax.rem(me + step, count)} for step in range(1, count)]
 
 
-def gather_weights(count, copies, tokens, qkv, up, out_w, down, small, ident):
+def gather_weights(count, copies, tokens, qkv, up, out_w, small, ident):
     planes = count // PLANE
     rows = qkv.shape[1]
-    block = down.shape[0]
-
-    def body(x_ref, qkv_ref, up_ref, wo_ref, down_ref, small_ref, *rest):
-        x_out, qkv_out, up_out, wo_out, down_out, small_out = rest[:6]
-        send, recv, local, send_wo, recv_wo, send_unit, recv_unit = rest[6:]
+
+    def body(x_ref, qkv_ref, up_ref, wo_ref, small_ref, *rest):
+        x_out, qkv_out, up_out, wo_out, small_out = rest[:5]
+        send, recv, local, send_wo, recv_wo, send_unit, recv_unit = rest[5:]
         me = lax.axis_index("shard")
         group, plane = lax.rem(me, PLANE), lax.div(me, PLANE)
         across = [
@@ -183,8 +184,7 @@
         owns = [
             (x_ref, x_out.at[group]),
             (qkv_ref.at[group], qkv_out.at[me]),
-            (up_ref.at[group], up_out.at[me]),
-            (down_ref, down_out.at[plane]),
+            (up_ref.at[group], up_out.at[group]),
             (small_ref, small_out.at[me]),
         ]
         started = []
@@ -211,20 +211,16 @@
             for lane in range(PLANE):
                 if step or lane:
                     units.append((qkv_ref, qkv_out, step, lane))
-        for step in range(planes):
-            for lane in range(PLANE):
-                if step or lane:
-                    units.append((up_ref, up_out, step, lane))
-            if step:
-                units.append((down_ref, down_out, step, 0))
+        for lane in range(1, PLANE):
+            units.append((up_ref, up_out, 0, lane))
 
         def unit_copy(index):
             src, dst, step, lane = units[index]
             goal = lax.rem(plane + step, planes)
             goal_group = lax.rem(group + lane, PLANE)
-            piece, slot = (src, plane) if src is down_ref else (src.at[goal_group], me)
+            slot = group if src is up_ref else me
             return remote(
-                piece,
+                src.at[goal_group],
                 dst.at[slot],
                 send_unit.at[index],
                 recv_unit.at[index],
@@ -235,7 +231,7 @@
             src, dst, step, lane = units[index]
             origin = lax.rem(plane + planes - step, planes)
             origin_group = lax.rem(group + PLANE - lane, PLANE)
-            slot = origin if src is down_ref else origin * PLANE + origin_group
+            slot = origin_group if src is up_ref else origin * PLANE + origin_group
             return remote(
                 dst.at[slot],
                 dst.at[slot],
@@ -301,21 +297,20 @@
             copy.wait()
 
     total = 3 + count - 1
-    number = 2 * (count - 1) + planes - 1
+    number = count - 1 + PLANE - 1
     return comm_call(
         body,
         "gather_weights",
         ident,
-        [tokens, qkv, up, out_w, down, small],
+        [tokens, qkv, up, out_w, small],
         [
             struct((PLANE,) + tokens.shape),
             struct((count, rows, qkv.shape[2])),
-            struct((count, rows, up.shape[2])),
+            struct((PLANE, rows, up.shape[2])),
             struct((planes,) + out_w.shape),
-            struct((planes, block, D)),
             struct((count,) + small.shape),
         ],
-        [ANY_SPEC] * 6,
+        [ANY_SPEC] * 5,
         [
             pltpu.SemaphoreType.DMA((total,)),
             pltpu.SemaphoreType.DMA((total,)),
@@ -471,13 +466,13 @@
 def reduce_grads(count, copies, qkv, up, out_w, down, small, ident):
     planes = count // PLANE
     rows = qkv.shape[1]
-    block = down.shape[1]
+    block = down.shape[0]
     arrays = [qkv, up, out_w, small]
 
     def body(qkv_ref, up_ref, wo_ref, small_ref, down_ref, *rest):
-        outs, (qkv_in, up_in, wo_in, small_in, down_in) = rest[:5], rest[5:10]
-        halves, gets = rest[10:15], rest[15:20]
-        send, recv, send_rep, recv_rep, send_wo, recv_wo = rest[20:]
+        outs, (qkv_in, up_in, wo_in, small_in) = rest[:5], rest[5:9]
+        halves, gets = [rest[9], up_in, rest[10], rest[11], down_ref], rest[12:17]
+        send, recv, send_rep, recv_rep, send_wo, recv_wo = rest[17:]
         me = lax.axis_index("shard")
         rep = lax.axis_index("rep")
         plane = lax.div(me, PLANE)
@@ -491,19 +486,19 @@
             copy.start()
             sent.append(copy)
 
-        pairs = [(qkv_ref, qkv_in), (up_ref, up_in), (small_ref, small_in)]
+        pairs = [(qkv_ref, qkv_in), (small_ref, small_in)]
         group = lax.rem(me, PLANE)
         target, place = lax.div(me, planes), lax.rem(me, planes)
         for src, held in pairs:
             for step in range(1, count):
                 peer = lax.rem(me + step, count)
                 push(src.at[peer], held.at[me], peer)
-        for step in range(1, planes):
-            peer = lax.rem(me + PLANE * step, count)
-            push(down_ref.at[lax.div(peer, PLANE)], down_in.at[plane], peer)
+        for lane in range(1, PLANE):
+            goal = lax.rem(group + lane, PLANE)
+            push(up_ref.at[goal], up_in.at[group], plane * PLANE + goal)
+        up_in[group] = up_ref[group]
         for src, held in pairs:
             held[me] = src[me]
-        down_in[plane] = down_ref[plane]
 
         def wo_copy(source, index):
             peer = group * planes + index
@@ -530,7 +525,7 @@
         for index in range(planes):
             peer, copy = wo_copy(plane, index)
             pl.when(peer != me)(copy.wait_send)
-        for half, held in zip(halves[:2], (qkv_in, up_in)):
+        for half, held in zip(halves[:1], (qkv_in,)):
             for lane in range(PLANE):
                 total = held[lane].astype(f32)
                 for other in range(1, planes):
@@ -539,7 +534,6 @@
         for half, held, number in (
             (halves[2], wo_in, planes),
             (halves[3], small_in, count),
-            (halves[4], down_in, planes),
         ):
             total = held[0].astype(f32)
             for other in range(1, number):
@@ -567,7 +561,7 @@
         for copy in sent + passed:
             copy.wait_send()
 
-    totals = 3 * (count - 1) + planes - 1
+    totals = 2 * (count - 1) + PLANE - 1
     shapes = [
         (PLANE, rows, qkv.shape[2]),
         (PLANE, rows, up.shape[2]),
@@ -582,8 +576,8 @@
         arrays + [down],
         [struct(shape, f32) for shape in shapes],
         [VMEM_SPEC] * 5,
-        [pltpu.VMEM(item.shape, bf16) for item in arrays + [down]]
-        + [pltpu.VMEM(shape, bf16) for shape in shapes]
+        [pltpu.VMEM(item.shape, bf16) for item in arrays]
+        + [pltpu.VMEM(shapes[index], bf16) for index in (0, 2, 3)]
         + [pltpu.VMEM((copies - 1,) + shape, bf16) for shape in shapes]
         + [
             pltpu.SemaphoreType.DMA((totals,)),
@@ -757,22 +751,24 @@
     small_send = jnp.pad(
         jnp.stack([padded(item) for item in vectors]), ((0, 6), (0, 0))
     ).astype(bf16)
-    x_all, qkv_all, up_all, wo_all, down_all, small = gather_weights(
+    x_all, qkv_all, up_all, wo_all, small = gather_weights(
         count,
         copies,
         x_own,
         qkv_send,
         up_send,
         out_weight.astype(bf16),
-        down_weight.astype(bf16),
         small_send,
         0,
     )
     x_plane = x_all.reshape(wide, D)
     w_qkv = qkv_all.reshape(D, 3 * GROUP_DIM)
-    w_up = up_all.reshape(D, GROUP_FF)
+    lines = [[start + PLANE * step for step in range(planes)] for start in range(PLANE)]
+    strip = jnp.concatenate([up_all.reshape(PLANE * rows, D), down_weight.astype(bf16)], axis=0)
+    strips = lax.all_gather(strip, "shard", axis_index_groups=lines, axis=0)
+    w_up = strips[:, : PLANE * rows].reshape(D, GROUP_FF)
     w_out = wo_all.reshape(GROUP_DIM, D)
-    w_down = down_all.reshape(GROUP_FF, D)
+    w_down = strips[:, PLANE * rows :].reshape(GROUP_FF, D)
     small = small.astype(f32)
     spread = [small[:, index, :rows].reshape(D) for index in range(8)]
     b_query, b_value, b_out, gain_mid, shift_mid, b_down, gain_end, shift_end = spread
@@ -814,6 +810,18 @@
     grad_down = dot_left(active_low, feed_plane).astype(bf16)
     up_low = (dot_right(feed_plane, w_down) * gelu_slope(hidden)).astype(bf16)
     grad_up = dot_left(middle_plane, up_low).astype(bf16)
+    strip_grads = lax.psum_scatter(
+        jnp.concatenate(
+            [
+                grad_up.reshape(planes, PLANE * rows, GROUP_FF),
+                grad_down.reshape(planes, block, D),
+            ],
+            axis=1,
+        ),
+        "shard",
+        axis_index_groups=lines,
+        scatter_dimension=0,
+    )
     d_middle = plane_sum(split(dot_right(up_low, w_up).astype(bf16)), 6) + d_second
     d_first = norm_backward(d_middle, normal_mid, scale_mid, gain_mid)
     branch_low = d_first.astype(bf16)
@@ -859,9 +867,9 @@
         count,
         copies,
         grad_qkv.reshape(count, rows, 3 * GROUP_DIM),
-        grad_up.reshape(count, rows, GROUP_FF),
+        strip_grads[: PLANE * rows].reshape(PLANE, rows, GROUP_FF),
         grad_out.reshape(planes, rows, D),
-        grad_down.reshape(planes, block, D),
+        strip_grads[PLANE * rows :],
         small_grads,
         10,
     )

time: 573 us -> 553 us (0.965); the launches traced: 573 us -> 546 us
  Pallas kernels: 393 us -> 340 us
  between operations: 1.81 us -> 15.3 us
  local copies, waits for them, and re-layouts: 45.6 us -> 56 us
    pallas_call x11, Pallas kernels: 393 us -> 340 us  [comm_call(): pl.pallas_call(body, name=name, out_shape=out_shapes, in_specs=[VMEM_SPEC...]
  transfers between devices with their start and end apart: 0 -> 2, of which waited for: 0 -> 0; matrix products, arithmetic and copies ran while one was open for 0% -> 23% of each run, Pallas kernels for 0% -> 35%
where the time goes in v3:
time: 553 us; the launch traced here: 546 us
  Pallas kernels  340 us (61%)
  matrix products  90.1 us (16%)
  local copies, waits for them, and re-layouts  56 us (10%)
  other arithmetic  44.4 us (8%)
  between operations  15.3 us (3%)
    pallas_call x11, Pallas kernels, comm_call(): pl.pallas_call(body, name=name, out_shape=out_shapes, in_specs=[VMEM_SPEC...  340 us
    dot_general x4, matrix products, step(): jnp.einsum('hqd,khd->hqk', upstream, value_rows, preferred_element_type=f32)  14.8 us
    dot_general x4, matrix products, dot(): return jnp.dot(left, right, preferred_element_type=f32)  14.4 us
    dot_general x4, matrix products, step(): jnp.einsum('hqk,khd->hqd', weights.astype(bf16), value_rows, preferred_el...  13 us
  transfers between devices with their start and end apart: 2, of which 0 were waited for; matrix products, arithmetic and copies ran while one was open for 23% of the time, Pallas kernels for 35%

profile of v3, /device:TPU:3, one launch (start us, length us, event | category | flops | bytes accessed | tf_op | source)
XLA Modules:
  0.0 546.3 jit_solution(736890292765106412)
XLA Ops:
  22.3 46.3 %gather_weights.1 = (bf16[4,192,768]{2,1,0:T(8,128)(2,1)}, bf16[16,48,576]{2,1,0:T(8,128)(2,1)}, bf16[4,48,768]{2,1,0:T(8,128)(2,1)}, bf16[4,48,768]{2,1,0:T(8,128)(2,1)}, bf16[16,16,256]{2,1,0:T(8,128)(2,1)}) custom-call(bf16[192,768]{1,0:T(8,128)(2,1)} %bitcast.213, bf16[4,48,576]{2,1,0:T(8,128)(2,1)} %maximum_bitcast_fusion.qkv_ref, ...), custom_call_target="tpu_custom_call" | custom-call | bytes 100000000 | tf_op jit(solution)/shard_map/gather_weights/pallas_call | solution.py:37
  76.5 80.3 %gather_planes.1 = bf16[4,768,384]{2,1,0:T(8,128)(2,1)} custom-call(bf16[768,384]{1,0:T(8,128)(2,1)} %slice.136.x_ref), custom_call_target="tpu_custom_call" | custom-call | bytes 100000000 | tf_op jit(solution)/shard_map/gather_planes/pallas_call | solution.py:37
  156.7 3.8 fusion.81
  164.6 34.3 %while.28 = (s32[]{:T(128)}, f32[3,768]{1,0:T(4,128)S(1)}, f32[3,768]{1,0:T(4,128)S(1)}, f32[3,768,64]{1,2,0:T(8,128)}, f32[768]{0:T(1024)S(1)}, /*index=5*/f32[...) while((s32[]{:T(128)}, f32[3,768]{1,0:T(4,128)S(1)}, ...), condition=%wide.region_3.4_spmd.clone, body=%wide.region_0.3_spmd.clone.sunk | while | flops 477031680 | bytes 30535876 | solution.py:661
  169.2 3.2 fusion.138
  177.7 3.2 fusion.138
  186.3 3.2 fusion.138
  206.4 12.8 %plane_sum.4 = f32[192,768]{1,0:T(8,128)} custom-call(bf16[4,192,768]{2,1,0:T(8,128)(2,1)} %bitcast.206), custom_call_target="tpu_custom_call" | custom-call | bytes 100000000 | tf_op jit(solution)/shard_map/plane_sum/pallas_call | solution.py:37
  221.6 12.6 %plane_gather.3 = bf16[4,192,768]{2,1,0:T(8,128)(2,1)} custom-call(bf16[192,768]{1,0:T(8,128)(2,1)} %fusion.63.x_ref), custom_call_target="tpu_custom_call" | custom-call | bytes 100000000 | tf_op jit(solution)/shard_map/plane_gather/pallas_call | solution.py:37
  236.8 7.4 %fusion.43 = (bf16[768,768]{1,0:T(8,128)(2,1)S(1)}, f32[768,768]{1,0:T(8,128)}) fusion(f32[768]{0:T(1024)S(1)} %add.170, bf16[768,768]{1,0:T(8,128)(2,1)S(1)} %bitcast.218, bf16[768,768]{1,0:T(8,128)(2,1)S(1)} %bitcast.228), kind=kOutput, calls=%fused_computation.55 | convolution fusion | flops 944898048 | bytes 5901312 | tf_op jit(solution)/shard_map/dot_general | solution.py:617
  246.4 12.5 %plane_sum.5 = f32[192,768]{1,0:T(8,128)} custom-call(bf16[4,192,768]{2,1,0:T(8,128)(2,1)} %bitcast.224), custom_call_target="tpu_custom_call" | custom-call | bytes 100000000 | tf_op jit(solution)/shard_map/plane_sum/pallas_call | solution.py:37
  263.0 12.9 %plane_gather.4 = bf16[4,192,768]{2,1,0:T(8,128)(2,1)} custom-call(bf16[192,768]{1,0:T(8,128)(2,1)} %get-tuple-element.295.x_ref), custom_call_target="tpu_custom_call" | custom-call | bytes 100000000 | tf_op jit(solution)/shard_map/plane_gather/pallas_call | solution.py:37
  275.9 3.9 convolution_convert_fusion
  287.0 12.5 %plane_sum.6 = f32[192,768]{1,0:T(8,128)} custom-call(bf16[4,192,768]{2,1,0:T(8,128)(2,1)} %bitcast.222), custom_call_target="tpu_custom_call" | custom-call | bytes 100000000 | tf_op jit(solution)/shard_map/plane_sum/pallas_call | solution.py:37
  307.0 12.7 %plane_gather.5 = bf16[4,192,768]{2,1,0:T(8,128)(2,1)} custom-call(bf16[192,768]{1,0:T(8,128)(2,1)} %get-tuple-element.297.x_ref), custom_call_target="tpu_custom_call" | custom-call | bytes 100000000 | tf_op jit(solution)/shard_map/plane_gather/pallas_call | solution.py:37
  322.3 46.5 %while.29 = (s32[]{:T(128)}, f32[3,768,64]{1,2,0:T(8,128)S(1)}, bf16[4,768,384]{2,1,0:T(8,128)(2,1)}, f32[768]{0:T(1024)S(1)}, f32[4,768]{1,0:T(4,128)}, /*index...) while((s32[]{:T(128)}, f32[3,768,64]{1,2,0:T(8,128)S(1)}, ...), condition=%wide.region_14.15_spmd.clone, body=%wide.region_13.14_spmd.clone.sunk | while | flops 1152663552 | bytes 41039008 | solution.py:686
  326.9 3.7 fusion.150
  338.6 3.7 fusion.150
  350.2 3.7 fusion.150
  361.8 3.7 fusion.150
  375.0 52.6 %sum_planes.1 = bf16[768,384]{1,0:T(8,128)(2,1)} custom-call(bf16[4,768,384]{2,1,0:T(8,128)(2,1)} %get-tuple-element.143.p_ref), custom_call_target="tpu_custom_call" | custom-call | bytes 100000000 | tf_op jit(solution)/shard_map/sum_planes/pallas_call | solution.py:37
  427.8 3.3 convolution_convert_fusion.5
  431.0 17.7 %plane_sum.7 = f32[192,768]{1,0:T(8,128)} custom-call(bf16[4,192,768]{2,1,0:T(8,128)(2,1)} %bitcast.223), custom_call_target="tpu_custom_call" | custom-call | bytes 100000000 | tf_op jit(solution)/shard_map/plane_sum/pallas_call | solution.py:37
  460.8 67.2 %reduce_grads.1 = (f32[4,48,576]{2,1,0:T(8,128)}, f32[4,48,768]{2,1,0:T(8,128)}, f32[48,768]{1,0:T(8,128)}, f32[16,256]{1,0:T(8,128)}, f32[192,768]{1,0:T(8,128)}) custom-call(bf16[16,48,576]{2,1,0:T(8,128)(2,1)} %bitcast.207, bf16[4,48,768]{2,1,0:T(8,128)(2,1)} %bitcast.234, bf16[4,48,768]{2,1,0:T(8,128)(2,1)} %bitcast.225, ...), custom_call_target="tpu_custom_call" | custom-call | bytes 100000000 | tf_op jit(solution)/shard_map/reduce_grads/pallas_call | solution.py:37
  (334 shorter events, 147.7 us)
Async XLA Ops:
  7.2 227.6 %all-gather.3.cloned.1.call-start = ((), (), s32[]{:S(2)}) async-start(), calls=%async_computation.2 | async-start | bytes 2949120 | tf_op jit(solution)/shard_map/all_gather | solution.py:768
  70.5 388.3 %reduce-scatter.2.cloned.1.call-start = ((), (), s32[]{:S(2)}) async-start(), calls=%async_computation.1 | async-start | bytes 2949120 | tf_op jit(solution)/shard_map/reduce_scatter | solution.py:813
  164.6 34.9 %copy-start.1 = (bf16[1,192,768]{2,1,0:T(8,128)(2,1)S(1)}, bf16[1,192,768]{2,1,0:T(8,128)(2,1)}, u32[]{:S(2)}) copy-start(bf16[1,192,768]{2,1,0:T(8,128)(2,1)} %param.41) | copy-start | bytes 884740
  199.6 19.6 %copy-start.10 = (bf16[1,192,768]{2,1,0:T(8,128)(2,1)S(1)}, bf16[1,192,768]{2,1,0:T(8,128)(2,1)}, u32[]{:S(2)}) copy-start(bf16[1,192,768]{2,1,0:T(8,128)(2,1)} %param.23) | copy-start | bytes 884740
  201.1 35.7 %copy-start.43 = (f32[768]{0:T(1024)}, f32[768]{0:T(1024)S(1)}, u32[]{:S(2)}) copy-start(f32[768]{0:T(1024)S(1)} %add.170) | copy-start | bytes 9220
  201.1 19.5 %copy-start.24 = (f32[768]{0:T(1024)}, f32[768]{0:T(1024)S(1)}, u32[]{:S(2)}) copy-start(f32[768]{0:T(1024)S(1)} %mul.216) | copy-start | bytes 9220
  201.2 19.5 %copy-start.31 = (f32[768]{0:T(1024)}, f32[768]{0:T(1024)S(1)}, u32[]{:S(2)}) copy-start(f32[768]{0:T(1024)S(1)} %add.166) | copy-start | bytes 9220
  220.4 16.3 %copy-start.28 = (f32[192]{0:T(256)}, f32[192]{0:T(256)S(1)}, u32[]{:S(2)}) copy-start(f32[192]{0:T(256)S(1)} %broadcast_multiply_fusion.5) | copy-start | bytes 2308
  220.7 16.1 %copy-start.33 = (f32[192]{0:T(256)}, f32[192]{0:T(256)S(1)}, u32[]{:S(2)}) copy-start(f32[192]{0:T(256)S(1)} %add_rsqrt_fusion.1) | copy-start | bytes 2308
  244.2 14.7 %copy-start.25 = (f32[768]{0:T(1024)S(1)}, f32[768]{0:T(1024)}, u32[]{:S(2)}) copy-start(f32[768]{0:T(1024)} %copy-done.24) | copy-start | bytes 9220
  244.2 14.7 %copy-start.29 = (f32[192]{0:T(256)S(1)}, f32[192]{0:T(256)}, u32[]{:S(2)}) copy-start(f32[192]{0:T(256)} %copy-done.28) | copy-start | bytes 2308
  244.2 14.7 %copy-start.32 = (f32[768]{0:T(1024)S(1)}, f32[768]{0:T(1024)}, u32[]{:S(2)}) copy-start(f32[768]{0:T(1024)} %copy-done.31) | copy-start | bytes 9220
  244.2 14.7 %copy-start.34 = (f32[192]{0:T(256)S(1)}, f32[192]{0:T(256)}, u32[]{:S(2)}) copy-start(f32[192]{0:T(256)} %copy-done.33) | copy-start | bytes 2308
  244.3 14.7 %copy-start.38 = (f32[768]{0:T(1024)S(1)}, f32[768]{0:T(1024)}, u32[]{:S(2)}) copy-start(f32[768]{0:T(1024)} %add.173) | copy-start | bytes 9220
  260.3 19.5 %copy-start.36 = (f32[192]{0:T(256)}, f32[192]{0:T(256)S(1)}, u32[]{:S(2)}) copy-start(f32[192]{0:T(256)S(1)} %broadcast_multiply_fusion.4) | copy-start | bytes 2308
  260.5 19.2 %copy-start.37 = (f32[192]{0:T(256)}, f32[192]{0:T(256)S(1)}, u32[]{:S(2)}) copy-start(f32[192]{0:T(256)S(1)} %add_rsqrt_fusion) | copy-start | bytes 2308
  261.4 18.4 %copy-start.39 = (f32[192]{0:T(256)}, f32[192]{0:T(256)S(1)}, u32[]{:S(2)}) copy-start(f32[192]{0:T(256)S(1)} %get-tuple-element.328) | copy-start | bytes 2308
  261.4 18.4 %copy-start.40 = (f32[192]{0:T(256)}, f32[192]{0:T(256)S(1)}, u32[]{:S(2)}) copy-start(f32[192]{0:T(256)S(1)} %get-tuple-element.329) | copy-start | bytes 2308
  284.9 14.7 %copy-start.18 = (bf16[768,768]{1,0:T(8,128)(2,1)S(1)}, bf16[768,768]{1,0:T(8,128)(2,1)}, u32[]{:S(2)}) copy-start(bf16[768,768]{1,0:T(8,128)(2,1)} %convolution_convert_fusion) | copy-start | bytes 3538948
  305.3 16.2 %copy-start.7 = (f32[3,768,64]{1,2,0:T(8,128)S(1)}, f32[3,768,64]{1,2,0:T(8,128)}, u32[]{:S(2)}) copy-start(f32[3,768,64]{1,2,0:T(8,128)} %get-tuple-element.137) | copy-start | bytes 1769476
  322.3 46.5 %copy-start.41 = (bf16[768]{0:T(1024)(128)(2,1)S(1)}, bf16[768]{0:T(1024)(128)(2,1)}, u32[]{:S(2)}) copy-start(bf16[768]{0:T(1024)(128)(2,1)} %get-tuple-element.237) | copy-start | bytes 4612
  322.3 47.2 %copy-start.42 = (bf16[768]{0:T(1024)(128)(2,1)S(1)}, bf16[768]{0:T(1024)(128)(2,1)}, u32[]{:S(2)}) copy-start(bf16[768]{0:T(1024)(128)(2,1)} %get-tuple-element.294) | copy-start | bytes 4612
  368.8 59.0 %copy-start.46 = (bf16[16,48,576]{2,1,0:T(8,128)(2,1)S(1)}, bf16[16,48,576]{2,1,0:T(8,128)(2,1)}, u32[]{:S(2)}) copy-start(bf16[16,48,576]{2,1,0:T(8,128)(2,1)} %get-tuple-element.136) | copy-start | bytes 2654212
  427.8 20.9 %copy-start.9 = (bf16[768,384]{1,0:T(8,128)(2,1)S(1)}, bf16[768,384]{1,0:T(8,128)(2,1)}, u32[]{:S(2)}) copy-start(bf16[768,384]{1,0:T(8,128)(2,1)} %sum_planes.1) | copy-start | bytes 1769476
  (33 other events, 142.0 us)
Sparse Core Ops, SparseCore 0:
  70.7 63.2 all-gather.2
  302.5 46.1 reduce-scatter.1

commit v4 on v3

--- a/solution.py
+++ b/solution.py
@@ -200,8 +200,13 @@
             copy.start()
             sent.append(copy)
 
-        for mask in (2, 1, 3):
+        for mask in (2, 1):
             push(x_ref, x_out.at[group], plane_peer(me, mask))
+        far = plane_slot(me, 2)
+        x_relay = remote(
+            x_out.at[far], x_out.at[far], send.at[2], recv.at[2], {"shard": plane_peer(me, 1)}
+        )
+        sent.append(x_relay)
         for step in range(1, count):
             push(small_ref, small_out.at[me], lax.rem(me + step, count))
         rep = lax.axis_index("rep")
@@ -267,6 +272,8 @@
             pl.when(peer != me)(copy.start)
         keep = pltpu.make_async_copy(wo_ref, wo_out.at[place], local.at[5])
         pl.when(target == group)(keep.start)
+        sent[0].wait_recv()
+        x_relay.start()
         for index, (_, _, step, _) in enumerate(units):
             if split and step:
 
@@ -283,7 +290,7 @@
             if split and step:
                 pl.when(rep != step % 2)(unit_relay(index).wait_recv)
                 pl.when(rep == step % 2)(unit_relay(index).wait_send)
-        for copy in sent:
+        for copy in sent[1:]:
             copy.wait_recv()
         for index in range(planes):
             pl.when(group * planes + index != me)(wo_copy(index, index)[1].wait_recv)
@@ -487,16 +494,32 @@
             sent.append(copy)
 
         pairs = [(qkv_ref, qkv_in), (small_ref, small_in)]
+        passed = []
+
+        def exchange(*places):
+            for index, peer in enumerate(across):
+                for place in places:
+                    copy = remote(
+                        halves[place],
+                        gets[place].at[index],
+                        send_rep.at[5 * index + place],
+                        recv_rep.at[5 * index + place],
+                        peer,
+                    )
+                    copy.start()
+                    passed.append(copy)
+
+        exchange(4)
         group = lax.rem(me, PLANE)
         target, place = lax.div(me, planes), lax.rem(me, planes)
+        for lane in range(1, PLANE):
+            goal = lax.rem(group + lane, PLANE)
+            push(up_ref.at[goal], up_in.at[group], plane * PLANE + goal)
+        up_in[group] = up_ref[group]
         for src, held in pairs:
             for step in range(1, count):
                 peer = lax.rem(me + step, count)
                 push(src.at[peer], held.at[me], peer)
-        for lane in range(1, PLANE):
-            goal = lax.rem(group + lane, PLANE)
-            push(up_ref.at[goal], up_in.at[group], plane * PLANE + goal)
-        up_in[group] = up_ref[group]
         for src, held in pairs:
             held[me] = src[me]
 
@@ -518,13 +541,21 @@
         def _():
             wo_in[plane] = wo_ref[place]
 
-        for copy in sent:
+        for copy in sent[: PLANE - 1]:
             copy.wait_recv()
+        exchange(1)
         for index in range(planes):
             pl.when(PLANE * index + target != me)(wo_copy(index, index)[1].wait_recv)
         for index in range(planes):
             peer, copy = wo_copy(plane, index)
             pl.when(peer != me)(copy.wait_send)
+        total = wo_in[0].astype(f32)
+        for other in range(1, planes):
+            total = total + wo_in[other].astype(f32)
+        halves[2][...] = total.astype(bf16)
+        exchange(2)
+        for copy in sent[PLANE - 1 :]:
+            copy.wait_recv()
         for half, held in zip(halves[:1], (qkv_in,)):
             for lane in range(PLANE):
                 total = held[lane].astype(f32)
@@ -532,25 +563,13 @@
                     total = total + held[other * PLANE + lane].astype(f32)
                 half[lane] = total.astype(bf16)
         for half, held, number in (
-            (halves[2], wo_in, planes),
             (halves[3], small_in, count),
         ):
             total = held[0].astype(f32)
             for other in range(1, number):
                 total = total + held[other].astype(f32)
             half[...] = total.astype(bf16)
-        passed = []
-        for index, peer in enumerate(across):
-            for place, (half, got) in enumerate(zip(halves, gets)):
-                copy = remote(
-                    half,
-                    got.at[index],
-                    send_rep.at[5 * index + place],
-                    recv_rep.at[5 * index + place],
-                    peer,
-                )
-                copy.start()
-                passed.append(copy)
+        exchange(0, 3)
         for copy in passed:
             copy.wait_recv()
         for out, half, got in zip(outs, halves, gets):
@@ -765,10 +784,7 @@
     w_qkv = qkv_all.reshape(D, 3 * GROUP_DIM)
     lines = [[start + PLANE * step for step in range(planes)] for start in range(PLANE)]
     strip = jnp.concatenate([up_all.reshape(PLANE * rows, D), down_weight.astype(bf16)], axis=0)
-    strips = lax.all_gather(strip, "shard", axis_index_groups=lines, axis=0)
-    w_up = strips[:, : PLANE * rows].reshape(D, GROUP_FF)
     w_out = wo_all.reshape(GROUP_DIM, D)
-    w_down = strips[:, PLANE * rows :].reshape(GROUP_FF, D)
     small = small.astype(f32)
     spread = [small[:, index, :rows].reshape(D) for index in range(8)]
     b_query, b_value, b_out, gain_mid, shift_mid, b_down, gain_end, shift_end = spread
@@ -786,6 +802,10 @@
     )
     qkv = (dot(x_plane, w_qkv) + qkv_bias).astype(bf16)
     pairs = gather_planes(count, qkv[:, GROUP_DIM:], 1)
+    strip, pairs = lax.optimization_barrier((strip, pairs))
+    strips = lax.all_gather(strip, "shard", axis_index_groups=lines, axis=0)
+    w_up = strips[:, : PLANE * rows].reshape(D, GROUP_FF)
+    w_down = strips[:, PLANE * rows :].reshape(GROUP_FF, D)
     queries = heads_of(qkv[:, :GROUP_DIM])
     keys = pairs[:, :, :GROUP_DIM].reshape(planes, wide, GROUP_HEADS, HEAD_DIM)
     values = pairs[:, :, GROUP_DIM:].reshape(planes, wide, GROUP_HEADS, HEAD_DIM)

time: 553 us -> 496 us (0.90)
  Pallas kernels: 340 us -> 283 us
    pallas_call x11, Pallas kernels: 340 us -> 283 us  [comm_call(): pl.pallas_call(body, name=name, out_shape=out_shapes, in_specs=[VMEM_SPEC...]
  transfers between devices with their start and end apart: 2 -> 2, of which waited for: 0 -> 0; matrix products, arithmetic and copies ran while one was open for 23% -> 25% of each run, Pallas kernels for 35% -> 22%
where the time goes in v4:
time: 496 us; the launch traced here: 489 us
  Pallas kernels  283 us (57%)
  matrix products  90.4 us (18%)
  local copies, waits for them, and re-layouts  55.7 us (11%)
  other arithmetic  43.3 us (9%)
  between operations  15.3 us (3%)
    pallas_call x11, Pallas kernels, comm_call(): pl.pallas_call(body, name=name, out_shape=out_shapes, in_specs=[VMEM_SPEC...  283 us
    dot_general x4, matrix products, step(): jnp.einsum('hqd,khd->hqk', upstream, value_rows, preferred_element_type=f32)  14.8 us
    dot_general x4, matrix products, dot(): return jnp.dot(left, right, preferred_element_type=f32)  14.8 us
    dot_general x4, matrix products, step(): jnp.einsum('hqk,khd->hqd', weights.astype(bf16), value_rows, preferred_el...  13 us
    dot_general x8, matrix products, step(): jnp.einsum('hqd,khd->hqk', queries, key_rows, preferred_element_type=f32)  10.5 us
    dot_general x4, matrix products, dot_right(): lax.dot_general(left, right, (((1,), (1,)), ((), ())), preferred_element_...  10 us
  transfers between devices with their start and end apart: 2, of which 0 were waited for; matrix products, arithmetic and copies ran while one was open for 25% of the time, Pallas kernels for 22%

profile of v4, /device:TPU:3, one launch (start us, length us, event | category | flops | bytes accessed | tf_op | source)
XLA Modules:
  0.0 488.5 jit_solution(6250516900133121532)
XLA Ops:
  22.3 38.4 %gather_weights.1 = (bf16[4,192,768]{2,1,0:T(8,128)(2,1)}, bf16[16,48,576]{2,1,0:T(8,128)(2,1)}, bf16[4,48,768]{2,1,0:T(8,128)(2,1)}, bf16[4,48,768]{2,1,0:T(8,128)(2,1)}, bf16[16,16,256]{2,1,0:T(8,128)(2,1)}) custom-call(bf16[192,768]{1,0:T(8,128)(2,1)} %bitcast.213, bf16[4,48,576]{2,1,0:T(8,128)(2,1)} %maximum_bitcast_fusion.qkv_ref, ...), custom_call_target="tpu_custom_call" | custom-call | bytes 100000000 | tf_op jit(solution)/shard_map/gather_weights/pallas_call | solution.py:37
  66.9 45.1 %gather_planes.1 = bf16[4,768,384]{2,1,0:T(8,128)(2,1)} custom-call(bf16[768,384]{1,0:T(8,128)(2,1)} %slice.136.x_ref), custom_call_target="tpu_custom_call" | custom-call | bytes 100000000 | tf_op jit(solution)/shard_map/gather_planes/pallas_call | solution.py:37
  120.6 34.3 %while.28 = (s32[]{:T(128)}, f32[3,768]{1,0:T(4,128)S(1)}, f32[3,768]{1,0:T(4,128)S(1)}, f32[3,768,64]{1,2,0:T(8,128)}, f32[768]{0:T(1024)S(1)}, /*index=5*/f32[...) while((s32[]{:T(128)}, f32[3,768]{1,0:T(4,128)S(1)}, ...), condition=%wide.region_3.4_spmd.clone, body=%wide.region_0.3_spmd.clone.sunk | while | flops 477031680 | bytes 30535876 | solution.py:680
  125.1 3.2 fusion.138
  133.7 3.2 fusion.138
  142.2 3.2 fusion.138
  150.8 3.2 fusion.138
  162.4 13.3 %plane_sum.4 = f32[192,768]{1,0:T(8,128)} custom-call(bf16[4,192,768]{2,1,0:T(8,128)(2,1)} %bitcast.206), custom_call_target="tpu_custom_call" | custom-call | bytes 100000000 | tf_op jit(solution)/shard_map/plane_sum/pallas_call | solution.py:37
  178.0 12.6 %plane_gather.3 = bf16[4,192,768]{2,1,0:T(8,128)(2,1)} custom-call(bf16[192,768]{1,0:T(8,128)(2,1)} %fusion.63.x_ref), custom_call_target="tpu_custom_call" | custom-call | bytes 100000000 | tf_op jit(solution)/shard_map/plane_gather/pallas_call | solution.py:37
  193.3 7.4 %fusion.43 = (bf16[768,768]{1,0:T(8,128)(2,1)S(1)}, f32[768,768]{1,0:T(8,128)}) fusion(f32[768]{0:T(1024)S(1)} %add.170, bf16[768,768]{1,0:T(8,128)(2,1)S(1)} %bitcast.218, bf16[768,768]{1,0:T(8,128)(2,1)S(1)} %bitcast.228), kind=kOutput, calls=%fused_computation.55 | convolution fusion | flops 944898048 | bytes 5901312 | tf_op jit(solution)/shard_map/dot_general | solution.py:636
  202.8 12.5 %plane_sum.5 = f32[192,768]{1,0:T(8,128)} custom-call(bf16[4,192,768]{2,1,0:T(8,128)(2,1)} %bitcast.224), custom_call_target="tpu_custom_call" | custom-call | bytes 100000000 | tf_op jit(solution)/shard_map/plane_sum/pallas_call | solution.py:37
  219.4 12.9 %plane_gather.4 = bf16[4,192,768]{2,1,0:T(8,128)(2,1)} custom-call(bf16[192,768]{1,0:T(8,128)(2,1)} %get-tuple-element.299.x_ref), custom_call_target="tpu_custom_call" | custom-call | bytes 100000000 | tf_op jit(solution)/shard_map/plane_gather/pallas_call | solution.py:37
  232.4 3.9 convolution_convert_fusion
  243.5 12.5 %plane_sum.6 = f32[192,768]{1,0:T(8,128)} custom-call(bf16[4,192,768]{2,1,0:T(8,128)(2,1)} %bitcast.222), custom_call_target="tpu_custom_call" | custom-call | bytes 100000000 | tf_op jit(solution)/shard_map/plane_sum/pallas_call | solution.py:37
  263.5 12.7 %plane_gather.5 = bf16[4,192,768]{2,1,0:T(8,128)(2,1)} custom-call(bf16[192,768]{1,0:T(8,128)(2,1)} %get-tuple-element.301.x_ref), custom_call_target="tpu_custom_call" | custom-call | bytes 100000000 | tf_op jit(solution)/shard_map/plane_gather/pallas_call | solution.py:37
  278.8 46.5 %while.29 = (s32[]{:T(128)}, f32[3,768,64]{1,2,0:T(8,128)S(1)}, bf16[4,768,384]{2,1,0:T(8,128)(2,1)}, f32[768]{0:T(1024)S(1)}, f32[4,768]{1,0:T(4,128)}, /*index...) while((s32[]{:T(128)}, f32[3,768,64]{1,2,0:T(8,128)S(1)}, ...), condition=%wide.region_14.15_spmd.clone, body=%wide.region_13.14_spmd.clone.sunk | while | flops 1152663552 | bytes 41039008 | solution.py:705
  283.4 3.7 fusion.150
  295.0 3.7 fusion.150
  306.6 3.7 fusion.150
  318.3 3.7 fusion.150
  331.4 53.3 %sum_planes.1 = bf16[768,384]{1,0:T(8,128)(2,1)} custom-call(bf16[4,768,384]{2,1,0:T(8,128)(2,1)} %get-tuple-element.147.p_ref), custom_call_target="tpu_custom_call" | custom-call | bytes 100000000 | tf_op jit(solution)/shard_map/sum_planes/pallas_call | solution.py:37
  385.0 3.3 convolution_convert_fusion.5
  388.3 17.5 %plane_sum.7 = f32[192,768]{1,0:T(8,128)} custom-call(bf16[4,192,768]{2,1,0:T(8,128)(2,1)} %bitcast.223), custom_call_target="tpu_custom_call" | custom-call | bytes 100000000 | tf_op jit(solution)/shard_map/plane_sum/pallas_call | solution.py:37
  417.8 52.4 %reduce_grads.1 = (f32[4,48,576]{2,1,0:T(8,128)}, f32[4,48,768]{2,1,0:T(8,128)}, f32[48,768]{1,0:T(8,128)}, f32[16,256]{1,0:T(8,128)}, f32[192,768]{1,0:T(8,128)}) custom-call(bf16[16,48,576]{2,1,0:T(8,128)(2,1)} %bitcast.207, bf16[4,48,768]{2,1,0:T(8,128)(2,1)} %bitcast.234, bf16[4,48,768]{2,1,0:T(8,128)(2,1)} %bitcast.225, ...), custom_call_target="tpu_custom_call" | custom-call | bytes 100000000 | tf_op jit(solution)/shard_map/reduce_grads/pallas_call | solution.py:37
  (341 shorter events, 147.1 us)
Async XLA Ops:
  7.2 184.1 %all-gather.3.cloned.1.call-start = ((), (), s32[]{:S(2)}) async-start(), calls=%async_computation.2 | async-start | bytes 2949120 | tf_op jit(solution)/shard_map/all_gather | solution.py:806
  65.8 46.2 %copy-start.26 = (bf16[4,48,768]{2,1,0:T(8,128)(2,1)S(1)}, bf16[4,48,768]{2,1,0:T(8,128)(2,1)}, u32[]{:S(2)}) copy-start(bf16[4,48,768]{2,1,0:T(8,128)(2,1)} %get-tuple-element.137) | copy-start | bytes 884740
  66.9 46.9 %slice-start = ((bf16[768,576]{1,0:T(8,128)(2,1)}), bf16[768,192]{1,0:T(8,128)(2,1)S(1)}, s32[]{:S(2)}) async-start(bf16[768,576]{1,0:T(8,128)(2,1)} %copy-done.12), calls=%async_computation.3 | async-start | bytes 786432 | tf_op jit(solution)/shard_map/slice | solution.py:809
  112.9 303.0 %reduce-scatter.2.cloned.1.call-start = ((), (), s32[]{:S(2)}) async-start(), calls=%async_computation.1 | async-start | bytes 2949120 | tf_op jit(solution)/shard_map/reduce_scatter | solution.py:833
  120.5 34.9 %copy-start.3 = (bf16[1,192,768]{2,1,0:T(8,128)(2,1)S(1)}, bf16[1,192,768]{2,1,0:T(8,128)(2,1)}, u32[]{:S(2)}) copy-start(bf16[1,192,768]{2,1,0:T(8,128)(2,1)} %param.41) | copy-start | bytes 884740
  155.5 20.1 %copy-start.13 = (bf16[1,192,768]{2,1,0:T(8,128)(2,1)S(1)}, bf16[1,192,768]{2,1,0:T(8,128)(2,1)}, u32[]{:S(2)}) copy-start(bf16[1,192,768]{2,1,0:T(8,128)(2,1)} %param.23) | copy-start | bytes 884740
  157.0 36.2 %copy-start.47 = (f32[768]{0:T(1024)}, f32[768]{0:T(1024)S(1)}, u32[]{:S(2)}) copy-start(f32[768]{0:T(1024)S(1)} %add.170) | copy-start | bytes 9220
  157.1 20.0 %copy-start.28 = (f32[768]{0:T(1024)}, f32[768]{0:T(1024)S(1)}, u32[]{:S(2)}) copy-start(f32[768]{0:T(1024)S(1)} %mul.216) | copy-start | bytes 9220
  157.2 20.0 %copy-start.35 = (f32[768]{0:T(1024)}, f32[768]{0:T(1024)S(1)}, u32[]{:S(2)}) copy-start(f32[768]{0:T(1024)S(1)} %add.166) | copy-start | bytes 9220
  176.9 16.3 %copy-start.32 = (f32[192]{0:T(256)}, f32[192]{0:T(256)S(1)}, u32[]{:S(2)}) copy-start(f32[192]{0:T(256)S(1)} %broadcast_multiply_fusion.5) | copy-start | bytes 2308
  177.1 16.1 %copy-start.37 = (f32[192]{0:T(256)}, f32[192]{0:T(256)S(1)}, u32[]{:S(2)}) copy-start(f32[192]{0:T(256)S(1)} %add_rsqrt_fusion.1) | copy-start | bytes 2308
  200.7 14.7 %copy-start.33 = (f32[192]{0:T(256)S(1)}, f32[192]{0:T(256)}, u32[]{:S(2)}) copy-start(f32[192]{0:T(256)} %copy-done.32) | copy-start | bytes 2308
  200.7 14.7 %copy-start.36 = (f32[768]{0:T(1024)S(1)}, f32[768]{0:T(1024)}, u32[]{:S(2)}) copy-start(f32[768]{0:T(1024)} %copy-done.35) | copy-start | bytes 9220
  200.7 14.7 %copy-start.38 = (f32[192]{0:T(256)S(1)}, f32[192]{0:T(256)}, u32[]{:S(2)}) copy-start(f32[192]{0:T(256)} %copy-done.37) | copy-start | bytes 2308
  216.8 19.5 %copy-start.40 = (f32[192]{0:T(256)}, f32[192]{0:T(256)S(1)}, u32[]{:S(2)}) copy-start(f32[192]{0:T(256)S(1)} %broadcast_multiply_fusion.4) | copy-start | bytes 2308
  217.0 19.2 %copy-start.41 = (f32[192]{0:T(256)}, f32[192]{0:T(256)S(1)}, u32[]{:S(2)}) copy-start(f32[192]{0:T(256)S(1)} %add_rsqrt_fusion) | copy-start | bytes 2308
  217.9 18.4 %copy-start.43 = (f32[192]{0:T(256)}, f32[192]{0:T(256)S(1)}, u32[]{:S(2)}) copy-start(f32[192]{0:T(256)S(1)} %get-tuple-element.332) | copy-start | bytes 2308
  217.9 18.4 %copy-start.44 = (f32[192]{0:T(256)}, f32[192]{0:T(256)S(1)}, u32[]{:S(2)}) copy-start(f32[192]{0:T(256)S(1)} %get-tuple-element.333) | copy-start | bytes 2308
  241.3 14.7 %copy-start.21 = (bf16[768,768]{1,0:T(8,128)(2,1)S(1)}, bf16[768,768]{1,0:T(8,128)(2,1)}, u32[]{:S(2)}) copy-start(bf16[768,768]{1,0:T(8,128)(2,1)} %convolution_convert_fusion) | copy-start | bytes 3538948
  261.8 16.3 %copy-start.9 = (f32[3,768,64]{1,2,0:T(8,128)S(1)}, f32[3,768,64]{1,2,0:T(8,128)}, u32[]{:S(2)}) copy-start(f32[3,768,64]{1,2,0:T(8,128)} %get-tuple-element.141) | copy-start | bytes 1769476
  278.8 46.5 %copy-start.45 = (bf16[768]{0:T(1024)(128)(2,1)S(1)}, bf16[768]{0:T(1024)(128)(2,1)}, u32[]{:S(2)}) copy-start(bf16[768]{0:T(1024)(128)(2,1)} %get-tuple-element.241) | copy-start | bytes 4612
  278.8 47.2 %copy-start.46 = (bf16[768]{0:T(1024)(128)(2,1)S(1)}, bf16[768]{0:T(1024)(128)(2,1)}, u32[]{:S(2)}) copy-start(bf16[768]{0:T(1024)(128)(2,1)} %get-tuple-element.298) | copy-start | bytes 4612
  325.2 59.8 %copy-start.49 = (bf16[16,48,576]{2,1,0:T(8,128)(2,1)S(1)}, bf16[16,48,576]{2,1,0:T(8,128)(2,1)}, u32[]{:S(2)}) copy-start(bf16[16,48,576]{2,1,0:T(8,128)(2,1)} %get-tuple-element.139) | copy-start | bytes 2654212
  385.0 20.7 %copy-start.11 = (bf16[768,384]{1,0:T(8,128)(2,1)S(1)}, bf16[768,384]{1,0:T(8,128)(2,1)}, u32[]{:S(2)}) copy-start(bf16[768,384]{1,0:T(8,128)(2,1)} %sum_planes.1) | copy-start | bytes 1769476
  (37 other events, 173.4 us)
Sparse Core Ops, SparseCore 0:
  113.0 48.7 all-gather.2
  259.0 45.4 reduce-scatter.1

commit v5 on v4

--- a/solution.py
+++ b/solution.py
@@ -81,85 +81,95 @@
     return lax.rem(plane_peer(me, mask), PLANE)
 
 
-def plane_gather(value, ident):
-    rows, cols = value.shape
-
-    def body(x_ref, out_ref, send, recv, local):
+def plane_step(parts, pieces, vectors, action, out_types, ident):
+    _, rows, cols = parts.shape
+    chunks = 3 if rows % 48 == 0 else 1
+    size = rows // chunks
+    many, few = len(pieces), len(out_types)
+
+    def body(p_ref, *rest):
+        piece_refs, vector_ref = rest[:many], rest[many]
+        all_ref, sums_ref = rest[many + 1 : many + 3]
+        out_refs = rest[many + 3 : many + 3 + few]
+        near, held, far_in, low, send, recv = rest[many + 3 + few :]
         me = lax.axis_index("shard")
-        peers = [{"shard": plane_peer(me, mask)} for mask in (1, 2)]
-        greet(peers)
+        beside, across = [{"shard": plane_peer(me, mask)} for mask in (1, 2)]
         mine, far = lax.rem(me, PLANE), plane_slot(me, 2)
-        own = pltpu.make_async_copy(x_ref, out_ref.at[mine], local)
-        own.start()
-        across = remote(x_ref, out_ref.at[mine], send.at[0], recv.at[0], peers[1])
-        across.start()
-        beside = remote(x_ref, out_ref.at[mine], send.at[1], recv.at[1], peers[0])
-        beside.start()
-        across.wait_recv()
-        relay = remote(out_ref.at[far], out_ref.at[far], send.at[2], recv.at[2], peers[0])
-        relay.start()
-        beside.wait_recv()
-        relay.wait_recv()
-        across.wait_send()
-        beside.wait_send()
-        relay.wait_send()
-        own.wait()
-
+        greet([beside, across])
+        spans = [pl.ds(size * index, size) for index in range(chunks)]
+
+        def copy(kind, index):
+            span = spans[index]
+            table = {
+                0: lambda: (p_ref.at[plane_slot(me, 3), span], near.at[0, span], beside),
+                1: lambda: (p_ref.at[plane_slot(me, 1), span], near.at[1, span], beside),
+                2: lambda: (held.at[span], far_in.at[span], across),
+                3: lambda: (low.at[span], all_ref.at[mine, span], across),
+                4: lambda: (low.at[span], all_ref.at[mine, span], beside),
+                5: lambda: (all_ref.at[far, span], all_ref.at[far, span], beside),
+            }
+            src, dst, peer = table[kind]()
+            return remote(src, dst, send.at[kind, index], recv.at[kind, index], peer)
+
+        for index in range(chunks):
+            copy(0, index).start()
+        for index in range(chunks):
+            copy(1, index).start()
+        for index in range(chunks):
+            span = spans[index]
+            copy(0, index).wait_recv()
+            total = p_ref[plane_slot(me, 2), span].astype(f32) + near[0, span].astype(f32)
+            held[span] = total.astype(bf16)
+            copy(2, index).start()
+        lines = [vector_ref[index : index + 1] for index in range(len(vectors))]
+        sums = None
+        for index in range(chunks):
+            span = spans[index]
+            copy(1, index).wait_recv()
+            copy(2, index).wait_recv()
+            total = p_ref[mine, span].astype(f32) + near[1, span].astype(f32)
+            total = total + far_in[span].astype(f32)
+            result, outs, terms = action(
+                total, [item[span].astype(f32) for item in piece_refs], lines
+            )
+            low[span] = result
+            copy(3, index).start()
+            copy(4, index).start()
+            for ref, value in zip(out_refs, outs):
+                ref[span] = value.astype(ref.dtype)
+            all_ref[mine, span] = result
+            terms = [jnp.sum(item, axis=0, keepdims=True) for item in terms]
+            sums = terms if sums is None else [x + y for x, y in zip(sums, terms)]
+        sums_ref[...] = jnp.zeros(sums_ref.shape, f32)
+        for place, value in enumerate(sums):
+            sums_ref[place : place + 1] = value
+        for index in range(chunks):
+            copy(3, index).wait_recv()
+            copy(5, index).start()
+        for index in range(chunks):
+            copy(4, index).wait_recv()
+            copy(5, index).wait_recv()
+        for index in range(chunks):
+            for kind in range(6):
+                copy(kind, index).wait_send()
+
+    stack = jnp.stack(vectors)
+    shape = (rows, cols)
     return comm_call(
         body,
-        "plane_gather",
+        "plane_step",
         ident,
-        [value],
-        struct((PLANE, rows, cols), value.dtype),
-        VMEM_SPEC,
-        [
-            pltpu.SemaphoreType.DMA((3,)),
-            pltpu.SemaphoreType.DMA((3,)),
-            pltpu.SemaphoreType.DMA,
-        ],
-    )
-
-
-def plane_sum(parts, ident):
-    _, rows, cols = parts.shape
-
-    def body(p_ref, out_ref, near, held, far_in, send, recv):
-        me = lax.axis_index("shard")
-        peers = [{"shard": plane_peer(me, mask)} for mask in (1, 2)]
-        greet(peers)
-        first = remote(
-            p_ref.at[plane_slot(me, 3)], near.at[0], send.at[0], recv.at[0], peers[0]
-        )
-        first.start()
-        second = remote(
-            p_ref.at[plane_slot(me, 1)], near.at[1], send.at[1], recv.at[1], peers[0]
-        )
-        second.start()
-        first.wait_recv()
-        held[...] = (p_ref[plane_slot(me, 2)].astype(f32) + near[0].astype(f32)).astype(bf16)
-        third = remote(held, far_in, send.at[2], recv.at[2], peers[1])
-        third.start()
-        second.wait_recv()
-        out_ref[...] = p_ref[lax.rem(me, PLANE)].astype(f32) + near[1].astype(f32)
-        third.wait_recv()
-        out_ref[...] += far_in[...].astype(f32)
-        first.wait_send()
-        second.wait_send()
-        third.wait_send()
-
-    return comm_call(
-        body,
-        "plane_sum",
-        ident,
-        [parts],
-        struct((rows, cols), f32),
-        VMEM_SPEC,
+        [parts] + list(pieces) + [stack],
+        [struct((PLANE, rows, cols)), struct((8, cols), f32)]
+        + [struct(shape, item) for item in out_types],
+        [VMEM_SPEC] * (2 + few),
         [
             pltpu.VMEM((2, rows, cols), bf16),
-            pltpu.VMEM((rows, cols), bf16),
-            pltpu.VMEM((rows, cols), bf16),
-            pltpu.SemaphoreType.DMA((3,)),
-            pltpu.SemaphoreType.DMA((3,)),
+            pltpu.VMEM(shape, bf16),
+            pltpu.VMEM(shape, bf16),
+            pltpu.VMEM(shape, bf16),
+            pltpu.SemaphoreType.DMA((6, chunks)),
+            pltpu.SemaphoreType.DMA((6, chunks)),
         ],
     )
 
@@ -470,16 +480,18 @@
     )
 
 
-def reduce_grads(count, copies, qkv, up, out_w, down, small, ident):
+def reduce_grads(count, copies, qkv, up, out_w, down, small, parts, first_grad, ident):
     planes = count // PLANE
     rows = qkv.shape[1]
     block = down.shape[0]
     arrays = [qkv, up, out_w, small]
 
-    def body(qkv_ref, up_ref, wo_ref, small_ref, down_ref, *rest):
-        outs, (qkv_in, up_in, wo_in, small_in) = rest[:5], rest[5:9]
-        halves, gets = [rest[9], up_in, rest[10], rest[11], down_ref], rest[12:17]
-        send, recv, send_rep, recv_rep, send_wo, recv_wo = rest[17:]
+    def body(qkv_ref, up_ref, wo_ref, small_ref, down_ref, p_ref, first_ref, *rest):
+        outs, token_ref, rest = rest[:5], rest[5], rest[6:]
+        qkv_in, up_in, wo_in, small_in = rest[:4]
+        halves, gets = [rest[4], up_in, rest[5], rest[6], down_ref], rest[7:12]
+        near, near_sum, far_in = rest[12:15]
+        send, recv, send_rep, recv_rep, send_wo, recv_wo, send_near, recv_near = rest[15:]
         me = lax.axis_index("shard")
         rep = lax.axis_index("rep")
         plane = lax.div(me, PLANE)
@@ -495,6 +507,14 @@
 
         pairs = [(qkv_ref, qkv_in), (small_ref, small_in)]
         passed = []
+        beside, over = [{"shard": plane_peer(me, mask)} for mask in (1, 2)]
+        near_copies = [
+            remote(p_ref.at[plane_slot(me, 3)], near.at[0], send_near.at[0], recv_near.at[0], beside),
+            remote(p_ref.at[plane_slot(me, 1)], near.at[1], send_near.at[1], recv_near.at[1], beside),
+            remote(near_sum, far_in, send_near.at[2], recv_near.at[2], over),
+        ]
+        near_copies[0].start()
+        near_copies[1].start()
 
         def exchange(*places):
             for index, peer in enumerate(across):
@@ -541,6 +561,10 @@
         def _():
             wo_in[plane] = wo_ref[place]
 
+        near_copies[0].wait_recv()
+        total = p_ref[plane_slot(me, 2)].astype(f32) + near[0].astype(f32)
+        near_sum[...] = total.astype(bf16)
+        near_copies[2].start()
         for copy in sent[: PLANE - 1]:
             copy.wait_recv()
         exchange(1)
@@ -554,6 +578,11 @@
             total = total + wo_in[other].astype(f32)
         halves[2][...] = total.astype(bf16)
         exchange(2)
+        near_copies[1].wait_recv()
+        near_copies[2].wait_recv()
+        total = p_ref[lax.rem(me, PLANE)].astype(f32) + near[1].astype(f32)
+        total = total + far_in[...].astype(f32) + first_ref[...]
+        token_ref[...] = total.astype(bf16)
         for copy in sent[PLANE - 1 :]:
             copy.wait_recv()
         for half, held in zip(halves[:1], (qkv_in,)):
@@ -577,7 +606,7 @@
             for index in range(copies - 1):
                 total = total + got[index].astype(f32)
             out[...] = total
-        for copy in sent + passed:
+        for copy in sent + passed + near_copies:
             copy.wait_send()
 
     totals = 2 * (count - 1) + PLANE - 1
@@ -592,19 +621,24 @@
         body,
         "reduce_grads",
         ident,
-        arrays + [down],
-        [struct(shape, f32) for shape in shapes],
-        [VMEM_SPEC] * 5,
+        arrays + [down, parts, first_grad],
+        [struct(shape, f32) for shape in shapes] + [struct(parts.shape[1:])],
+        [VMEM_SPEC] * 6,
         [pltpu.VMEM(item.shape, bf16) for item in arrays]
         + [pltpu.VMEM(shapes[index], bf16) for index in (0, 2, 3)]
         + [pltpu.VMEM((copies - 1,) + shape, bf16) for shape in shapes]
         + [
+            pltpu.VMEM((2,) + parts.shape[1:], bf16),
+            pltpu.VMEM(parts.shape[1:], bf16),
+            pltpu.VMEM(parts.shape[1:], bf16),
             pltpu.SemaphoreType.DMA((totals,)),
             pltpu.SemaphoreType.DMA((totals,)),
             pltpu.SemaphoreType.DMA((5 * (copies - 1),)),
             pltpu.SemaphoreType.DMA((5 * (copies - 1),)),
             pltpu.SemaphoreType.DMA((planes,)),
             pltpu.SemaphoreType.DMA((planes,)),
+            pltpu.SemaphoreType.DMA((3,)),
+            pltpu.SemaphoreType.DMA((3,)),
         ],
     )
 
@@ -815,18 +849,47 @@
     def split(value):
         return value.reshape(PLANE, here, D)
 
-    branch = plane_sum(split(dot(context_low, w_out).astype(bf16)), 2) + b_out
-    middle, normal_mid, scale_mid = norm_forward(x_own.astype(f32) + branch, gain_mid, shift_mid)
-    middle_plane = plane_gather(middle.astype(bf16), 3).reshape(wide, D)
+    def enter_middle(total, pieces, lines):
+        rest = total + lines[0] + pieces[0]
+        middle, _, _ = norm_forward(rest, lines[1], lines[2])
+        return middle.astype(bf16), [rest], []
+
+    def enter_end(total, pieces, lines):
+        middle, _, _ = norm_forward(pieces[0], lines[1], lines[2])
+        result, normal, scale = norm_forward(middle + (total + lines[0]), lines[3], lines[4])
+        above = pieces[1]
+        back = norm_backward(above, normal, scale, lines[3])
+        rounded = back.astype(bf16)
+        return rounded, [result, back], [above * normal, above, rounded.astype(f32)]
+
+    def leave_middle(total, pieces, lines):
+        _, normal, scale = norm_forward(pieces[0], lines[0], lines[0])
+        above = total + pieces[1]
+        back = norm_backward(above, normal, scale, lines[0])
+        rounded = back.astype(bf16)
+        return rounded, [back], [above * normal, above, rounded.astype(f32)]
+
+    middle_all, _, rest = plane_step(
+        split(dot(context_low, w_out).astype(bf16)),
+        [x_own],
+        [b_out, gain_mid, shift_mid],
+        enter_middle,
+        [f32],
+        2,
+    )
+    middle_plane = middle_all.reshape(wide, D)
     hidden = dot(middle_plane, w_up) + b_up
     active_low = jax.nn.gelu(hidden, approximate=False).astype(bf16)
-    feed = plane_sum(split(dot(active_low, w_down).astype(bf16)), 4) + b_down
-    result, normal_end, scale_end = norm_forward(middle + feed, gain_end, shift_end)
-    output = result.astype(bf16)[None]
-    upstream = cotangent[0].astype(f32)
-    d_second = norm_backward(upstream, normal_end, scale_end, gain_end)
-    feed_low = d_second.astype(bf16)
-    feed_plane = plane_gather(feed_low, 5).reshape(wide, D)
+    feed_all, end_sums, result, d_second = plane_step(
+        split(dot(active_low, w_down).astype(bf16)),
+        [rest, cotangent[0]],
+        [b_down, gain_mid, shift_mid, gain_end, shift_end],
+        enter_end,
+        [bf16, f32],
+        3,
+    )
+    output = result[None]
+    feed_plane = feed_all.reshape(wide, D)
     grad_down = dot_left(active_low, feed_plane).astype(bf16)
     up_low = (dot_right(feed_plane, w_down) * gelu_slope(hidden)).astype(bf16)
     grad_up = dot_left(middle_plane, up_low).astype(bf16)
@@ -842,10 +905,15 @@
         axis_index_groups=lines,
         scatter_dimension=0,
     )
-    d_middle = plane_sum(split(dot_right(up_low, w_up).astype(bf16)), 6) + d_second
-    d_first = norm_backward(d_middle, normal_mid, scale_mid, gain_mid)
-    branch_low = d_first.astype(bf16)
-    branch_plane = plane_gather(branch_low, 7).reshape(wide, D)
+    branch_all, middle_sums, d_first = plane_step(
+        split(dot_right(up_low, w_up).astype(bf16)),
+        [rest, d_second],
+        [gain_mid],
+        leave_middle,
+        [f32],
+        4,
+    )
+    branch_plane = branch_all.reshape(wide, D)
     grad_out = dot_left(context_low, branch_plane).astype(bf16)
     d_context = heads_of(dot_right(branch_plane, w_out).astype(bf16))
     delta = jnp.sum(d_context.astype(f32) * context_heads, axis=2)
@@ -855,8 +923,6 @@
     pair_low = sum_planes(count, d_pair, 8)
     mixer_low = jnp.concatenate([flat_of(d_query).astype(bf16), pair_low], axis=1)
     grad_qkv = dot_left(x_plane, mixer_low).astype(bf16)
-    grad_input = plane_sum(split(dot_right(mixer_low, w_qkv).astype(bf16)), 9)
-    grad_tokens = (grad_input + d_first).astype(bf16)[None]
     mixer_sums = jnp.sum(mixer_low.astype(f32), axis=0)
 
     def from_group(value):
@@ -865,12 +931,12 @@
     sums = [
         from_group(mixer_sums[:GROUP_DIM]),
         from_group(mixer_sums[2 * GROUP_DIM :]),
-        jnp.sum(branch_low.astype(f32), axis=0),
-        jnp.sum(d_middle * normal_mid, axis=0),
-        jnp.sum(d_middle, axis=0),
-        jnp.sum(feed_low.astype(f32), axis=0),
-        jnp.sum(upstream * normal_end, axis=0),
-        jnp.sum(upstream, axis=0),
+        middle_sums[2],
+        middle_sums[0],
+        middle_sums[1],
+        end_sums[2],
+        end_sums[0],
+        end_sums[1],
     ]
     own_lane = (jnp.arange(PLANE) == group).astype(f32)
     up_sums = jnp.sum(up_low.astype(f32), axis=0).reshape(planes, 1, block)
@@ -883,7 +949,7 @@
         ],
         axis=1,
     ).astype(bf16)
-    qkv_total, up_total, out_total, small_total, down_total = reduce_grads(
+    qkv_total, up_total, out_total, small_total, down_total, grad_tokens = reduce_grads(
         count,
         copies,
         grad_qkv.reshape(count, rows, 3 * GROUP_DIM),
@@ -891,6 +957,8 @@
         grad_out.reshape(planes, rows, D),
         strip_grads[PLANE * rows :],
         small_grads,
+        split(dot_right(mixer_low, w_qkv).astype(bf16)),
+        d_first,
         10,
     )
 
@@ -902,7 +970,7 @@
     )
     return (
         output,
-        grad_tokens,
+        grad_tokens[None],
         joined(qkv_total[:, :, :GROUP_DIM]),
         joined(qkv_total[:, :, GROUP_DIM : 2 * GROUP_DIM]),
         joined(qkv_total[:, :, 2 * GROUP_DIM :]),

time: 496 us -> 446 us (0.90)
  Pallas kernels: 283 us -> 259 us
  local copies, waits for them, and re-layouts: 55.7 us -> 42.7 us
  other arithmetic: 43.3 us -> 32.2 us
    pallas_call x11 -> x7, Pallas kernels: 283 us -> 259 us  [comm_call(): pl.pallas_call(body, name=name, out_shape=out_shapes, in_specs=[VMEM_SPEC...]
    reduce_sum x9 -> x0, other arithmetic: 10 us -> none  [the longest x1 2.85 us: shards(): jnp.sum(d_middle * normal_mid, axis=0)]
    another operation x9, local copies, waits for them, and re-layouts: 8.36 us -> 0.79 us  [shards(): sums = jnp.stack([item.reshape(count, rows) for item in sums], axis=1)]
    dynamic_slice x8, local copies, waits for them, and re-layouts: 5.82 us -> 0.14 us  [attend_forward(): (top, total, summed), _ = lax.scan(step, start, (keys, values, all_codes))]
  transfers between devices with their start and end apart: 2 -> 2, of which waited for: 0 -> 0; matrix products, arithmetic and copies ran while one was open for 25% -> 22% of each run, Pallas kernels for 22% -> 17%
where the time goes in v5:
time: 446 us; the launch traced here: 441 us
  Pallas kernels  259 us (58%)
  matrix products  90.7 us (20%)
  local copies, waits for them, and re-layouts  42.7 us (10%)
  other arithmetic  32.2 us (7%)
  between operations  15 us (3%)
    pallas_call x7, Pallas kernels, comm_call(): pl.pallas_call(body, name=name, out_shape=out_shapes, in_specs=[VMEM_SPEC...  259 us
    dot_general x4, matrix products, step(): jnp.einsum('hqd,khd->hqk', upstream, value_rows, preferred_element_type=f32)  14.3 us
    dot_general x4, matrix products, dot(): return jnp.dot(left, right, preferred_element_type=f32)  13.9 us
    dot_general x4, matrix products, step(): jnp.einsum('hqk,khd->hqd', weights.astype(bf16), value_rows, preferred_el...  12.9 us
    dot_general x4, matrix products, dot_right(): lax.dot_general(left, right, (((1,), (1,)), ((), ())), preferred_element_...  10.9 us
    dot_general x4, matrix products, step(): jnp.einsum('hqk,hqd->khd', chances.astype(bf16), upstream, preferred_elem...  10.7 us
    dot_general x8, matrix products, step(): jnp.einsum('hqd,khd->hqk', queries, key_rows, preferred_element_type=f32)  10.5 us
    dot_general x4, matrix products, dot_left(): lax.dot_general(left, right, (((0,), (0,)), ((), ())), preferred_element_...  9.54 us
  transfers between devices with their start and end apart: 2, of which 0 were waited for; matrix products, arithmetic and copies ran while one was open for 22% of the time, Pallas kernels for 17%

profile of v5, /device:TPU:3, one launch (start us, length us, event | category | flops | bytes accessed | tf_op | source)
XLA Modules:
  0.0 440.6 jit_solution(11594478375465949208)
XLA Ops:
  22.3 38.4 %gather_weights.1 = (bf16[4,192,768]{2,1,0:T(8,128)(2,1)}, bf16[16,48,576]{2,1,0:T(8,128)(2,1)}, bf16[4,48,768]{2,1,0:T(8,128)(2,1)}, bf16[4,48,768]{2,1,0:T(8,128)(2,1)}, bf16[16,16,256]{2,1,0:T(8,128)(2,1)}) custom-call(bf16[192,768]{1,0:T(8,128)(2,1)} %bitcast.204, bf16[4,48,576]{2,1,0:T(8,128)(2,1)} %maximum_bitcast_fusion.qkv_ref, ...), custom_call_target="tpu_custom_call" | custom-call | bytes 100000000 | tf_op jit(solution)/shard_map/gather_weights/pallas_call | solution.py:37
  66.9 45.1 %gather_planes.1 = bf16[4,768,384]{2,1,0:T(8,128)(2,1)} custom-call(bf16[768,384]{1,0:T(8,128)(2,1)} %slice.166.x_ref), custom_call_target="tpu_custom_call" | custom-call | bytes 100000000 | tf_op jit(solution)/shard_map/gather_planes/pallas_call | solution.py:37
  119.7 31.4 %while.28 = (s32[]{:T(128)}, f32[3,768]{1,0:T(4,128)S(1)}, f32[3,768]{1,0:T(4,128)S(1)}, f32[3,768,64]{1,2,0:T(8,128)}, f32[768]{0:T(1024)S(1)}, /*index=5*/f32[...) while((s32[]{:T(128)}, f32[3,768]{1,0:T(4,128)S(1)}, ...), condition=%wide.region_3.4_spmd.clone, body=%wide.region_0.3_spmd.clone.sunk | while | flops 477031680 | bytes 30535876 | solution.py:714
  123.5 3.2 fusion.120
  131.3 3.2 fusion.120
  139.1 3.2 fusion.120
  147.0 3.2 fusion.120
  155.6 21.2 %plane_step.3 = (bf16[4,192,768]{2,1,0:T(8,128)(2,1)}, f32[8,768]{1,0:T(8,128)}, f32[192,768]{1,0:T(8,128)}) custom-call(bf16[4,192,768]{2,1,0:T(8,128)(2,1)} %bitcast.191, bf16[192,768]{1,0:T(8,128)(2,1)} %bitcast.205, f32[3,768]{1,0:T(4,128)} %pad_maximum_fusion.6.rest_1_), custom_call_target="tpu_custom_call" | custom-call | bytes 100000000 | tf_op jit(solution)/shard_map/plane_step/pallas_call | solution.py:37
  180.1 7.5 %fusion.43 = (bf16[768,768]{1,0:T(8,128)(2,1)S(1)}, f32[768,768]{1,0:T(8,128)}) fusion(f32[768]{0:T(1024)S(1)} %add.94, bf16[768,768]{1,0:T(8,128)(2,1)S(1)} %bitcast.221, bf16[768,768]{1,0:T(8,128)(2,1)S(1)} %bitcast.209), kind=kOutput, calls=%fused_computation.55 | convolution fusion | flops 944898048 | bytes 5901312 | tf_op jit(solution)/shard_map/dot_general | solution.py:670
  189.8 21.1 %plane_step.4 = (bf16[4,192,768]{2,1,0:T(8,128)(2,1)}, f32[8,768]{1,0:T(8,128)}, bf16[192,768]{1,0:T(8,128)(2,1)}, f32[192,768]{1,0:T(8,128)}) custom-call(bf16[4,192,768]{2,1,0:T(8,128)(2,1)} %bitcast.207, f32[192,768]{1,0:T(8,128)} %get-tuple-element.156.rest_0_, bf16[192,768]{1,0:T(8,128)(2,1)} %bitcast.216, f32[5,768]{1,0:T(8,128)} %stack.66.rest_2_), custom_call_target="tpu_custom_call" | custom-call | bytes 100000000 | tf_op jit(solution)/shard_map/plane_step/pallas_call | solution.py:37
  211.0 2.9 convolution_convert_fusion
  214.1 2.8 convert_reduce_fusion
  221.1 21.1 %plane_step.5 = (bf16[4,192,768]{2,1,0:T(8,128)(2,1)}, f32[8,768]{1,0:T(8,128)}, f32[192,768]{1,0:T(8,128)}) custom-call(bf16[4,192,768]{2,1,0:T(8,128)(2,1)} %bitcast.203, f32[192,768]{1,0:T(8,128)} %get-tuple-element.156.rest_0_, f32[192,768]{1,0:T(8,128)} %get-tuple-element.160.rest_1_, f32[1,768]{1,0:T(1,128)} %copy-done.22), custom_call_target="tpu_custom_call" | custom-call | bytes 100000000 | tf_op jit(solution)/shard_map/plane_step/pallas_call | solution.py:37
  248.1 44.5 %while.29 = (s32[]{:T(128)}, f32[3,768,64]{1,2,0:T(8,128)S(1)}, bf16[4,768,384]{2,1,0:T(8,128)(2,1)}, f32[768]{0:T(1024)S(1)}, f32[4,768]{1,0:T(4,128)S(1)}, /*i...) while((s32[]{:T(128)}, f32[3,768,64]{1,2,0:T(8,128)S(1)}, ...), condition=%wide.region_6.7_spmd.clone, body=%wide.region_5.6_spmd.clone.sunk | while | flops 1152663552 | bytes 41039008 | solution.py:739
  252.5 3.6 fusion.132
  260.9 2.7 fusion.133
  263.6 3.6 fusion.132
  274.6 3.6 fusion.132
  283.0 2.7 fusion.133
  285.7 3.6 fusion.132
  293.3 53.0 %sum_planes.1 = bf16[768,384]{1,0:T(8,128)(2,1)} custom-call(bf16[4,768,384]{2,1,0:T(8,128)(2,1)} %get-tuple-element.163.p_ref), custom_call_target="tpu_custom_call" | custom-call | bytes 100000000 | tf_op jit(solution)/shard_map/sum_planes/pallas_call | solution.py:37
  349.2 3.4 convolution_convert_fusion.6
  357.1 3.3 convolution_convert_fusion.5
  362.4 58.6 %reduce_grads.1 = (f32[4,48,576]{2,1,0:T(8,128)}, f32[4,48,768]{2,1,0:T(8,128)}, f32[48,768]{1,0:T(8,128)}, f32[16,256]{1,0:T(8,128)}, f32[192,768]{1,0:T(8,128)}, /*index=5*/bf16[192,768]{1,0:T(8,128)(2,1)}) custom-call(bf16[16,48,576]{2,1,0:T(8,128)(2,1)} %bitcast.192, bf16[4,48,768]{2,1,0:T(8,128)(2,1)} %bitcast.202, bf16[4,48,768]{2,1,0:T(8,128)(2,1)} %bitcast.198, ...), custom_call_target="tpu_custom_call" | custom-call | bytes 100000000 | tf_op jit(solution)/shard_map/reduce_grads/pallas_call | solution.py:37
  (285 shorter events, 113.7 us)
Async XLA Ops:
  7.2 12.5 %copy-start.14 = (f32[48,3072]{1,0:T(8,128)S(1)}, f32[48,3072]{1,0:T(8,128)}, u32[]{:S(2)}) copy-start(f32[48,3072]{1,0:T(8,128)} %param.35) | copy-start | bytes 1769476
  7.2 170.9 %all-gather.3.cloned.1.call-start = ((), (), s32[]{:S(2)}) async-start(), calls=%async_computation.2 | async-start | bytes 2949120 | tf_op jit(solution)/shard_map/all_gather | solution.py:840
  15.9 5.6 %copy-start.15 = (f32[192,768]{1,0:T(8,128)S(1)}, f32[192,768]{1,0:T(8,128)}, u32[]{:S(2)}) copy-start(f32[192,768]{1,0:T(8,128)} %param.37) | copy-start | bytes 1769476
  65.8 46.2 %copy-start.20 = (bf16[4,48,768]{2,1,0:T(8,128)(2,1)S(1)}, bf16[4,48,768]{2,1,0:T(8,128)(2,1)}, u32[]{:S(2)}) copy-start(bf16[4,48,768]{2,1,0:T(8,128)(2,1)} %get-tuple-element.147) | copy-start | bytes 884740
  66.9 46.8 %slice-start = ((bf16[768,576]{1,0:T(8,128)(2,1)}), bf16[768,192]{1,0:T(8,128)(2,1)S(1)}, s32[]{:S(2)}) async-start(bf16[768,576]{1,0:T(8,128)(2,1)} %copy-done.7), calls=%async_computation.3 | async-start | bytes 786432 | tf_op jit(solution)/shard_map/slice | solution.py:843
  112.9 247.5 %reduce-scatter.2.cloned.1.call-start = ((), (), s32[]{:S(2)}) async-start(), calls=%async_computation.1 | async-start | bytes 2949120 | tf_op jit(solution)/shard_map/reduce_scatter | solution.py:896
  119.7 34.3 %copy-start.8 = (bf16[4,48,768]{2,1,0:T(8,128)(2,1)S(1)}, bf16[4,48,768]{2,1,0:T(8,128)(2,1)}, u32[]{:S(2)}) copy-start(bf16[4,48,768]{2,1,0:T(8,128)(2,1)} %get-tuple-element.153) | copy-start | bytes 884740
  151.9 28.1 %copy-start.22 = (f32[1,768]{1,0:T(1,128)}, f32[1,768]{1,0:T(1,128)S(1)}, u32[]{:S(2)}) copy-start(f32[1,768]{1,0:T(1,128)S(1)} %stack_reshape_squeeze.46.rest_2_) | copy-start | bytes 9220
  180.0 7.6 %copy-start.9 = (bf16[4,192,768]{2,1,0:T(8,128)(2,1)}, bf16[4,192,768]{2,1,0:T(8,128)(2,1)S(1)}, u32[]{:S(2)}) copy-start(bf16[4,192,768]{2,1,0:T(8,128)(2,1)S(1)} %get-tuple-element.320) | copy-start | bytes 3538948
  180.0 7.6 %copy-start.11 = (bf16[4,192,768]{2,1,0:T(8,128)(2,1)}, bf16[4,192,768]{2,1,0:T(8,128)(2,1)S(1)}, u32[]{:S(2)}) copy-start(bf16[4,192,768]{2,1,0:T(8,128)(2,1)S(1)} %get-tuple-element.319) | copy-start | bytes 3538948
  211.0 2.9 copy-start.12
  211.0 2.9 copy-start.28
  211.0 3.1 copy-start.29
  221.1 23.7 %copy-start.5 = (f32[3,768,64]{1,2,0:T(8,128)S(1)}, f32[3,768,64]{1,2,0:T(8,128)}, u32[]{:S(2)}) copy-start(f32[3,768,64]{1,2,0:T(8,128)} %get-tuple-element.151) | copy-start | bytes 1769476
  242.2 4.3 copy-start.13
  292.5 53.8 %copy-start.24 = (f32[8,768]{1,0:T(8,128)S(1)}, f32[8,768]{1,0:T(8,128)}, u32[]{:S(2)}) copy-start(f32[8,768]{1,0:T(8,128)} %get-tuple-element.164) | copy-start | bytes 73732
  292.5 54.2 %copy-start.23 = (f32[8,768]{1,0:T(8,128)S(1)}, f32[8,768]{1,0:T(8,128)}, u32[]{:S(2)}) copy-start(f32[8,768]{1,0:T(8,128)} %get-tuple-element.165) | copy-start | bytes 73732
  349.1 6.1 %copy-start.25 = (f32[16]{0:T(128)S(1)}, f32[16]{0:T(128)}, u32[]{:S(2)}) copy-start(f32[16]{0:T(128)} %mul.138) | copy-start | bytes 196
  352.5 3.5 copy-start.2
  421.0 6.9 %copy-start.17 = (f32[4,48,768]{2,1,0:T(8,128)S(1)}, f32[4,48,768]{2,1,0:T(8,128)}, u32[]{:S(2)}) copy-start(f32[4,48,768]{2,1,0:T(8,128)} %get-tuple-element.171) | copy-start | bytes 1769476
  427.1 3.5 copy-start.18
  427.9 3.4 copy-start.19
  428.5 3.5 copy-start.21
  428.5 4.2 copy-start.16
  (16 other events, 27.9 us)
Sparse Core Ops, SparseCore 0:
  113.0 48.7 all-gather.2
  248.2 44.9 reduce-scatter.1

commit v6 on v5

--- a/solution.py
+++ b/solution.py
@@ -407,75 +407,6 @@
             pltpu.SemaphoreType.DMA((2, planes)),
             pltpu.SemaphoreType.DMA((2, planes)),
             pltpu.SemaphoreType.DMA,
-        ],
-    )
-
-
-def sum_planes(count, parts, ident):
-    planes, rows, cols = parts.shape
-
-    def body(p_ref, out_ref, held, staged, send, recv):
-        me = lax.axis_index("shard")
-        plane = lax.div(me, PLANE)
-        greet([{"shard": lax.rem(me + PLANE * s, count)} for s in range(1, planes)])
-
-        def hop(way, goal, src):
-            peer = me + PLANE if way == 0 else me - PLANE
-            return remote(
-                src,
-                held.at[way, goal],
-                send.at[goal],
-                recv.at[way, goal],
-                {"shard": lax.rem(peer + count, count)},
-            )
-
-        for step in range(planes - 1):
-            for way, goal in ((0, planes - 1 - step), (1, step)):
-                ahead = goal > plane if way == 0 else goal < plane
-                first = plane == 0 if way == 0 else plane == planes - 1
-
-                @pl.when(ahead & first)
-                def _(way=way, goal=goal):
-                    hop(way, goal, p_ref.at[goal]).start()
-
-                @pl.when(ahead & jnp.logical_not(first))
-                def _(way=way, goal=goal):
-                    copy = hop(way, goal, staged.at[goal])
-                    copy.wait_recv()
-                    total = p_ref[goal].astype(f32) + held[way, goal].astype(f32)
-                    staged[goal] = total.astype(bf16)
-                    copy.start()
-
-        out_ref[...] = p_ref[plane]
-
-        @pl.when(plane > 0)
-        def _():
-            hop(0, plane, staged.at[plane]).wait_recv()
-            out_ref[...] = (out_ref[...].astype(f32) + held[0, plane].astype(f32)).astype(bf16)
-
-        @pl.when(plane < planes - 1)
-        def _():
-            hop(1, plane, staged.at[plane]).wait_recv()
-            out_ref[...] = (out_ref[...].astype(f32) + held[1, plane].astype(f32)).astype(bf16)
-
-        for goal in range(planes):
-
-            @pl.when(goal != plane)
-            def _(goal=goal):
-                hop(0, goal, staged.at[goal]).wait_send()
-
-    return comm_call(
-        body,
-        "sum_planes",
-        ident,
-        [parts],
-        struct((rows, cols)),
-        VMEM_SPEC,
-        [
-            pltpu.VMEM((2, planes, rows, cols), bf16),
-            pltpu.VMEM((planes, rows, cols), bf16),
-            pltpu.SemaphoreType.DMA((planes,)),
-            pltpu.SemaphoreType.DMA((2, planes)),
         ],
     )
 
@@ -643,6 +574,129 @@
     )
 
 
+def pick(plane, table):
+    value = table[-1]
+    for index in range(len(table) - 1):
+        value = jnp.where(plane == index, table[index], value)
+    return value
+
+
+def attend_back(count, queries, upstream, pairs, own_row, key_cols, logs, delta, ident):
+    planes, rows, cols = pairs.shape
+    half = cols // 2
+    size = 256 if rows % 256 == 0 else rows
+    orders = []
+    for plane in range(planes):
+        goals = [goal for goal in range(planes) if goal != plane]
+        goals.sort(key=lambda goal: (-abs(goal - plane), goal))
+        orders.append(goals + [plane])
+
+    def body(q_ref, up_ref, kv_ref, row_ref, col_ref, log_ref, delta_ref, *rest):
+        dq_ref, out_ref, dq_sum, part, held, staged, send, recv = rest
+        me = lax.axis_index("shard")
+        plane = lax.div(me, PLANE)
+        greet([{"shard": lax.rem(me + PLANE * s, count)} for s in range(1, planes)])
+        dq_sum[...] = jnp.zeros(dq_sum.shape, f32)
+
+        def hop(way, goal):
+            peer = me + PLANE if way == 0 else me - PLANE
+            return remote(
+                staged.at[goal],
+                held.at[way, goal],
+                send.at[goal],
+                recv.at[way, goal],
+                {"shard": lax.rem(peer + count, count)},
+            )
+
+        def compute(goal):
+            part[...] = jnp.zeros(part.shape, f32)
+            key_codes = col_ref[goal]
+
+            def chunk(index, carry):
+                at = pl.multiple_of(index * size, size)
+                span = pl.ds(at, size)
+                allowed = key_codes == row_ref[0:1, span]
+                for head in range(GROUP_HEADS):
+                    low, high = head * HEAD_DIM, (head + 1) * HEAD_DIM
+                    q = q_ref[span, low:high]
+                    g = up_ref[span, low:high]
+                    k = kv_ref[goal, :, low:high]
+                    v = kv_ref[goal, :, half + low : half + high]
+                    raw = dot_right(k, q) * 0.125
+                    chances = jnp.where(
+                        allowed, jnp.exp(raw - log_ref[head : head + 1, span]), 0.0
+                    )
+                    d_chance = dot_right(v, g)
+                    d_score = (chances * (d_chance - delta_ref[head : head + 1, span])).astype(bf16)
+                    dq_sum[span, low:high] += dot_left(d_score, k)
+                    part[:, low:high] += dot(d_score, q) * 0.125
+                    part[:, half + low : half + high] += dot(chances.astype(bf16), g)
+                return carry
+
+            lax.fori_loop(0, rows // size, chunk, 0)
+
+        def pass_on(goal):
+            for way in (0, 1):
+                ahead = goal > plane if way == 0 else goal < plane
+                first = plane == 0 if way == 0 else plane == planes - 1
+
+                @pl.when(ahead & jnp.logical_not(first))
+                def _(way=way):
+                    copy = hop(way, goal)
+                    copy.wait_recv()
+                    total = staged[goal].astype(f32) + held[way, goal].astype(f32)
+                    staged[goal] = total.astype(bf16)
+                    copy.start()
+
+        def begin(goal):
+            for way in (0, 1):
+                ahead = goal > plane if way == 0 else goal < plane
+                first = plane == 0 if way == 0 else plane == planes - 1
+
+                @pl.when(ahead & first)
+                def _(way=way):
+                    hop(way, goal).start()
+
+        goals = [pick(plane, [order[i] for order in orders]) for i in range(planes)]
+        for index in range(planes):
+            goal = goals[index]
+            compute(goal)
+            if index < planes - 1:
+                staged[goal] = part[...].astype(bf16)
+                begin(goal)
+            if index:
+                pass_on(goals[index - 1])
+        dq_ref[...] = (dq_sum[...] * 0.125).astype(bf16)
+        for way in (0, 1):
+            behind = plane > 0 if way == 0 else plane < planes - 1
+
+            @pl.when(behind)
+            def _(way=way):
+                hop(way, plane).wait_recv()
+                part[...] += held[way, plane].astype(f32)
+
+        out_ref[...] = part[...].astype(bf16)
+        for index in range(planes - 1):
+            hop(0, goals[index]).wait_send()
+
+    return comm_call(
+        body,
+        "attend_back",
+        ident,
+        [queries, upstream, pairs, own_row, key_cols, logs, delta],
+        [struct((rows, half)), struct((rows, cols))],
+        [VMEM_SPEC] * 2,
+        [
+            pltpu.VMEM((rows, half), f32),
+            pltpu.VMEM((rows, cols), f32),
+            pltpu.VMEM((2, planes, rows, cols), bf16),
+            pltpu.VMEM((planes, rows, cols), bf16),
+            pltpu.SemaphoreType.DMA((planes,)),
+            pltpu.SemaphoreType.DMA((2, planes)),
+        ],
+    )
+
+
 def norm_forward(value, gain, shift):
     center = value - jnp.mean(value, axis=-1, keepdims=True)
     spread = jnp.mean(center * center, axis=-1, keepdims=True)
@@ -713,31 +767,6 @@
     )
     (top, total, summed), _ = lax.scan(step, start, (keys, values, all_codes))
     return summed / total[:, :, None], top + jnp.log(total)
-
-
-def attend_backward(queries, keys, values, own_codes, all_codes, logs, delta, upstream):
-    def step(carried, pieces):
-        key_rows, value_rows, key_codes = pieces
-        raw = jnp.einsum("hqd,khd->hqk", queries, key_rows, preferred_element_type=f32) * 0.125
-        allowed = (own_codes[:, None] == key_codes[None, :])[None]
-        chances = jnp.where(allowed, jnp.exp(raw - logs[:, :, None]), 0.0)
-        d_chance = jnp.einsum("hqd,khd->hqk", upstream, value_rows, preferred_element_type=f32)
-        d_score = (chances * (d_chance - delta[:, :, None])).astype(bf16)
-        carried = carried + jnp.einsum(
-            "hqk,khd->hqd", d_score, key_rows, preferred_element_type=f32
-        )
-        d_key = jnp.einsum("hqk,hqd->khd", d_score, queries, preferred_element_type=f32) * 0.125
-        d_value = jnp.einsum(
-            "hqk,hqd->khd", chances.astype(bf16), upstream, preferred_element_type=f32
-        )
-        size = key_rows.shape[0]
-        return carried, jnp.concatenate(
-            [d_key.reshape(size, GROUP_DIM), d_value.reshape(size, GROUP_DIM)], axis=1
-        ).astype(bf16)
-
-    start = jnp.zeros(queries.shape, f32)
-    d_query, d_pair = lax.scan(step, start, (keys, values, all_codes))
-    return d_query * 0.125, d_pair
 
 
 def shards(count, copies, *arrays):
@@ -915,13 +944,20 @@
     )
     branch_plane = branch_all.reshape(wide, D)
     grad_out = dot_left(context_low, branch_plane).astype(bf16)
-    d_context = heads_of(dot_right(branch_plane, w_out).astype(bf16))
-    delta = jnp.sum(d_context.astype(f32) * context_heads, axis=2)
-    d_query, d_pair = attend_backward(
-        queries, keys, values, own_codes, all_codes, logs, delta, d_context
-    )
-    pair_low = sum_planes(count, d_pair, 8)
-    mixer_low = jnp.concatenate([flat_of(d_query).astype(bf16), pair_low], axis=1)
+    d_context = dot_right(branch_plane, w_out).astype(bf16)
+    delta = jnp.sum(heads_of(d_context).astype(f32) * context_heads, axis=2)
+    query_low, pair_low = attend_back(
+        count,
+        qkv[:, :GROUP_DIM],
+        d_context,
+        pairs,
+        own_codes[None],
+        all_codes[:, :, None],
+        logs,
+        delta,
+        8,
+    )
+    mixer_low = jnp.concatenate([query_low, pair_low], axis=1)
     grad_qkv = dot_left(x_plane, mixer_low).astype(bf16)
     mixer_sums = jnp.sum(mixer_low.astype(f32), axis=0)
 

time: 446 us -> 422 us (0.946)
  matrix products: 90.7 us -> 65.5 us
  local copies, waits for them, and re-layouts: 42.7 us -> 37.4 us
  Pallas kernels: 259 us -> 264 us
    dot_general x16 -> x0, matrix products: 32.9 us -> none  [the longest x4 14.3 us: step(): jnp.einsum('hqd,khd->hqk', upstream, value_rows, preferred_element_type=f32)]
    reduce_sum x4, other arithmetic: 7.09 us -> 19.8 us  [step(): jnp.sum(weights, axis=2)]
    dot_general x8 -> x4, matrix products: 10.5 us -> 17.5 us  [step(): jnp.einsum('hqd,khd->hqk', queries, key_rows, preferred_element_type=f32)]
    another operation x15, other arithmetic: 6.81 us -> 0.16 us
    pallas_call x7, Pallas kernels: 259 us -> 264 us  [comm_call(): pl.pallas_call(body, name=name, out_shape=out_shapes, in_specs=[VMEM_SPEC...]
    dynamic_update_slice x8 -> x0, local copies, waits for them, and re-layouts: 4.77 us -> none  [attend_backward(): d_query, d_pair = lax.scan(step, start, (keys, values, all_codes))]
  transfers between devices with their start and end apart: 2 -> 2, of which waited for: 0 -> 0; matrix products, arithmetic and copies ran while one was open for 22% -> 22% of each run, Pallas kernels for 17% -> 23%
where the time goes in v6:
time: 422 us; the launch traced here: 417 us
  Pallas kernels  264 us (63%)
  matrix products  65.5 us (16%)
  local copies, waits for them, and re-layouts  37.4 us (9%)
  other arithmetic  34.3 us (8%)
  between operations  15.2 us (4%)
    pallas_call x7, Pallas kernels, comm_call(): pl.pallas_call(body, name=name, out_shape=out_shapes, in_specs=[VMEM_SPEC...  264 us
    reduce_sum x4, other arithmetic, step(): jnp.sum(weights, axis=2)  19.8 us
    dot_general x4, matrix products, step(): jnp.einsum('hqd,khd->hqk', queries, key_rows, preferred_element_type=f32)  17.5 us
    dot_general x4, matrix products, step(): jnp.einsum('hqk,khd->hqd', weights.astype(bf16), value_rows, preferred_el...  16.6 us
    dot_general x4, matrix products, dot(): return jnp.dot(left, right, preferred_element_type=f32)  13.9 us
    dot_general x4, matrix products, dot_right(): lax.dot_general(left, right, (((1,), (1,)), ((), ())), preferred_element_...  9.53 us
  transfers between devices with their start and end apart: 2, of which 0 were waited for; matrix products, arithmetic and copies ran while one was open for 22% of the time, Pallas kernels for 23%

profile of v6, /device:TPU:3, one launch (start us, length us, event | category | flops | bytes accessed | tf_op | source)
XLA Modules:
  0.0 416.9 jit_solution(3675129646726056162)
XLA Ops:
  13.5 38.4 %gather_weights.1 = (bf16[4,192,768]{2,1,0:T(8,128)(2,1)}, bf16[16,48,576]{2,1,0:T(8,128)(2,1)}, bf16[4,48,768]{2,1,0:T(8,128)(2,1)}, bf16[4,48,768]{2,1,0:T(8,128)(2,1)}, bf16[16,16,256]{2,1,0:T(8,128)(2,1)}) custom-call(bf16[192,768]{1,0:T(8,128)(2,1)} %bitcast.144, bf16[4,48,576]{2,1,0:T(8,128)(2,1)} %maximum_bitcast_fusion.qkv_ref, ...), custom_call_target="tpu_custom_call" | custom-call | bytes 100000000 | tf_op jit(solution)/shard_map/gather_weights/pallas_call | solution.py:37
  58.2 45.1 %gather_planes.1.kv_ref = bf16[4,768,384]{2,1,0:T(8,128)(2,1)} custom-call(bf16[768,384]{1,0:T(8,128)(2,1)} %slice.167.x_ref), custom_call_target="tpu_custom_call" | custom-call | bytes 100000000 | tf_op jit(solution)/shard_map/gather_planes/pallas_call | solution.py:37
  112.2 56.1 %while.15 = (s32[]{:T(128)}, f32[3,768]{1,0:T(4,128)S(1)}, f32[3,768]{1,0:T(4,128)S(1)}, f32[3,768,64]{1,2,0:T(8,128)}, f32[768]{0:T(1024)S(1)}, /*index=5*/f32[...) while((s32[]{:T(128)}, f32[3,768]{1,0:T(4,128)S(1)}, ...), condition=%wide.region_3.4_spmd.clone, body=%wide.region_0.3_spmd.clone.sunk | while | flops 477031680 | bytes 54129308 | solution.py:768
  112.6 4.4 %fusion.79 = (f32[3,768]{1,0:T(4,128)S(1)}, f32[3,768,768]{2,1,0:T(8,128)}) fusion(pred[768,768]{0,1:T(8,128)(4,1)S(1)} %broadcast_compare_fusion.2, bf16[3,768,64]{1,2,0:T(8,128)(2,1)S(1)} %get-tuple-element.309, bf16[4,768,3,64]{1,3,2,0:T(8,128)(2,1)S(1)} %get-tuple-element.308, s32[]{:T(128)} %get-tuple-element.291), kind=kOutput, calls=%fused_computation.2.clone.1 | convolution fusion | flops 231798528 | bytes 8266756 | tf_op jit(solution)/shard_map/while/body/eval_jaxpr/hqd,khd->hqk/dot_general | solution.py:747
  117.0 5.0 %fusion.80 = f32[3,768]{1,0:T(4,128)S(1)} fusion(f32[3,768,768]{2,1,0:T(8,128)} %get-tuple-element.277, f32[3,768]{1,0:T(4,128)S(1)} %select_maximum_fusion.2, pred[768,768]{0,1:T(8,128)(4,1)S(1)} %broadcast_compare_fusion.2), kind=kLoop, calls=%fused_computation.4.clone.1 | loop fusion | flops 8845056 | bytes 7686144 | tf_op jit(solution)/shard_map/while/body/eval_jaxpr/reduce_sum | solution.py:758
  122.0 4.0 fusion.82
  126.5 4.4 %fusion.79 = (f32[3,768]{1,0:T(4,128)S(1)}, f32[3,768,768]{2,1,0:T(8,128)}) fusion(pred[768,768]{0,1:T(8,128)(4,1)S(1)} %broadcast_compare_fusion.2, bf16[3,768,64]{1,2,0:T(8,128)(2,1)S(1)} %get-tuple-element.309, bf16[4,768,3,64]{1,3,2,0:T(8,128)(2,1)S(1)} %get-tuple-element.308, s32[]{:T(128)} %get-tuple-element.291), kind=kOutput, calls=%fused_computation.2.clone.1 | convolution fusion | flops 231798528 | bytes 8266756 | tf_op jit(solution)/shard_map/while/body/eval_jaxpr/hqd,khd->hqk/dot_general | solution.py:747
  130.9 5.0 %fusion.80 = f32[3,768]{1,0:T(4,128)S(1)} fusion(f32[3,768,768]{2,1,0:T(8,128)} %get-tuple-element.277, f32[3,768]{1,0:T(4,128)S(1)} %select_maximum_fusion.2, pred[768,768]{0,1:T(8,128)(4,1)S(1)} %broadcast_compare_fusion.2), kind=kLoop, calls=%fused_computation.4.clone.1 | loop fusion | flops 8845056 | bytes 7686144 | tf_op jit(solution)/shard_map/while/body/eval_jaxpr/reduce_sum | solution.py:758
  136.0 4.2 %fusion.82 = f32[3,768,64]{1,2,0:T(8,128)} fusion(f32[3,768,768]{2,1,0:T(8,128)S(1)} %copy-done, f32[3,768]{1,0:T(4,128)S(1)} %select_maximum_fusion.2, pred[768,768]{0,1:T(8,128)(4,1)S(1)} %broadcast_compare_fusion.2, f32[3,768,64]{1,2,0:T(8,128)} %get-tuple-element.294, bf16[4,768,3,64]{1,3,2,0:T(8,128)(2,1)} %get-tuple-element.310, ...), kind=kOutput, calls=%fused_computation.7.clone.1 | convolution fusion | flops 235782144 | bytes 9161217 | tf_op jit(solution)/shard_map/while/body/eval_jaxpr/hqk,khd->hqd/dot_general | solution.py:753
  140.6 4.4 %fusion.79 = (f32[3,768]{1,0:T(4,128)S(1)}, f32[3,768,768]{2,1,0:T(8,128)}) fusion(pred[768,768]{0,1:T(8,128)(4,1)S(1)} %broadcast_compare_fusion.2, bf16[3,768,64]{1,2,0:T(8,128)(2,1)S(1)} %get-tuple-element.309, bf16[4,768,3,64]{1,3,2,0:T(8,128)(2,1)S(1)} %get-tuple-element.308, s32[]{:T(128)} %get-tuple-element.291), kind=kOutput, calls=%fused_computation.2.clone.1 | convolution fusion | flops 231798528 | bytes 8266756 | tf_op jit(solution)/shard_map/while/body/eval_jaxpr/hqd,khd->hqk/dot_general | solution.py:747
  145.0 4.9 %fusion.80 = f32[3,768]{1,0:T(4,128)S(1)} fusion(f32[3,768,768]{2,1,0:T(8,128)} %get-tuple-element.277, f32[3,768]{1,0:T(4,128)S(1)} %select_maximum_fusion.2, pred[768,768]{0,1:T(8,128)(4,1)S(1)} %broadcast_compare_fusion.2), kind=kLoop, calls=%fused_computation.4.clone.1 | loop fusion | flops 8845056 | bytes 7686144 | tf_op jit(solution)/shard_map/while/body/eval_jaxpr/reduce_sum | solution.py:758
  150.1 4.2 %fusion.82 = f32[3,768,64]{1,2,0:T(8,128)} fusion(f32[3,768,768]{2,1,0:T(8,128)S(1)} %copy-done, f32[3,768]{1,0:T(4,128)S(1)} %select_maximum_fusion.2, pred[768,768]{0,1:T(8,128)(4,1)S(1)} %broadcast_compare_fusion.2, f32[3,768,64]{1,2,0:T(8,128)} %get-tuple-element.294, bf16[4,768,3,64]{1,3,2,0:T(8,128)(2,1)} %get-tuple-element.310, ...), kind=kOutput, calls=%fused_computation.7.clone.1 | convolution fusion | flops 235782144 | bytes 9161217 | tf_op jit(solution)/shard_map/while/body/eval_jaxpr/hqk,khd->hqd/dot_general | solution.py:753
  154.7 4.4 %fusion.79 = (f32[3,768]{1,0:T(4,128)S(1)}, f32[3,768,768]{2,1,0:T(8,128)}) fusion(pred[768,768]{0,1:T(8,128)(4,1)S(1)} %broadcast_compare_fusion.2, bf16[3,768,64]{1,2,0:T(8,128)(2,1)S(1)} %get-tuple-element.309, bf16[4,768,3,64]{1,3,2,0:T(8,128)(2,1)S(1)} %get-tuple-element.308, s32[]{:T(128)} %get-tuple-element.291), kind=kOutput, calls=%fused_computation.2.clone.1 | convolution fusion | flops 231798528 | bytes 8266756 | tf_op jit(solution)/shard_map/while/body/eval_jaxpr/hqd,khd->hqk/dot_general | solution.py:747
  159.1 4.9 %fusion.80 = f32[3,768]{1,0:T(4,128)S(1)} fusion(f32[3,768,768]{2,1,0:T(8,128)} %get-tuple-element.277, f32[3,768]{1,0:T(4,128)S(1)} %select_maximum_fusion.2, pred[768,768]{0,1:T(8,128)(4,1)S(1)} %broadcast_compare_fusion.2), kind=kLoop, calls=%fused_computation.4.clone.1 | loop fusion | flops 8845056 | bytes 7686144 | tf_op jit(solution)/shard_map/while/body/eval_jaxpr/reduce_sum | solution.py:758
  164.1 4.2 %fusion.82 = f32[3,768,64]{1,2,0:T(8,128)} fusion(f32[3,768,768]{2,1,0:T(8,128)S(1)} %copy-done, f32[3,768]{1,0:T(4,128)S(1)} %select_maximum_fusion.2, pred[768,768]{0,1:T(8,128)(4,1)S(1)} %broadcast_compare_fusion.2, f32[3,768,64]{1,2,0:T(8,128)} %get-tuple-element.294, bf16[4,768,3,64]{1,3,2,0:T(8,128)(2,1)} %get-tuple-element.310, ...), kind=kOutput, calls=%fused_computation.7.clone.1 | convolution fusion | flops 235782144 | bytes 9161217 | tf_op jit(solution)/shard_map/while/body/eval_jaxpr/hqk,khd->hqd/dot_general | solution.py:753
  172.3 21.3 %plane_step.3 = (bf16[4,192,768]{2,1,0:T(8,128)(2,1)}, f32[8,768]{1,0:T(8,128)}, f32[192,768]{1,0:T(8,128)}) custom-call(bf16[4,192,768]{2,1,0:T(8,128)(2,1)} %bitcast.130, bf16[192,768]{1,0:T(8,128)(2,1)} %bitcast.145, f32[3,768]{1,0:T(4,128)} %pad_maximum_fusion.5.rest_1_), custom_call_target="tpu_custom_call" | custom-call | bytes 100000000 | tf_op jit(solution)/shard_map/plane_step/pallas_call | solution.py:37
  196.2 7.6 %fusion.22 = (bf16[768,768]{1,0:T(8,128)(2,1)S(1)}, f32[768,768]{1,0:T(8,128)}) fusion(f32[768]{0:T(1024)S(1)} %add.88, bf16[768,768]{1,0:T(8,128)(2,1)S(1)} %bitcast.161, bf16[768,768]{1,0:T(8,128)(2,1)S(1)} %bitcast.148), kind=kOutput, calls=%fused_computation.29 | convolution fusion | flops 944898048 | bytes 5901312 | tf_op jit(solution)/shard_map/dot_general | solution.py:724
  205.9 21.2 %plane_step.4 = (bf16[4,192,768]{2,1,0:T(8,128)(2,1)}, f32[8,768]{1,0:T(8,128)}, bf16[192,768]{1,0:T(8,128)(2,1)}, f32[192,768]{1,0:T(8,128)}) custom-call(bf16[4,192,768]{2,1,0:T(8,128)(2,1)} %bitcast.146, f32[192,768]{1,0:T(8,128)} %get-tuple-element.100.rest_0_, bf16[192,768]{1,0:T(8,128)(2,1)} %bitcast.156, f32[5,768]{1,0:T(8,128)} %stack.66.rest_2_), custom_call_target="tpu_custom_call" | custom-call | bytes 100000000 | tf_op jit(solution)/shard_map/plane_step/pallas_call | solution.py:37
  227.2 2.9 convolution_convert_fusion
  240.5 21.0 %plane_step.5 = (bf16[4,192,768]{2,1,0:T(8,128)(2,1)}, f32[8,768]{1,0:T(8,128)}, f32[192,768]{1,0:T(8,128)}) custom-call(bf16[4,192,768]{2,1,0:T(8,128)(2,1)} %bitcast.143, f32[192,768]{1,0:T(8,128)} %get-tuple-element.100.rest_0_, f32[192,768]{1,0:T(8,128)} %get-tuple-element.103.rest_1_, f32[1,768]{1,0:T(1,128)} %copy-done.20), custom_call_target="tpu_custom_call" | custom-call | bytes 100000000 | tf_op jit(solution)/shard_map/plane_step/pallas_call | solution.py:37
  266.0 54.8 %attend_back.1 = (bf16[768,192]{1,0:T(8,128)(2,1)}, bf16[768,384]{1,0:T(8,128)(2,1)}) custom-call(bf16[768,192]{1,0:T(8,128)(2,1)} %copy-done.4, bf16[768,192]{1,0:T(8,128)(2,1)} %copy.80.up_ref, bf16[4,768,384]{2,1,0:T(8,128)(2,1)} %gather_planes.1.kv_ref, f32[1,768]{1,0:T(1,128)} %get-tuple-element.193.row_ref, ...), custom_call_target="tpu_custom_call" | custom-call | bytes 100000000 | tf_op jit(solution)/shard_map/attend_back/pallas_call | solution.py:37
  323.6 2.7 convolution_convert_fusion.6
  329.8 3.3 convolution_convert_fusion.5
  335.1 62.4 %reduce_grads.1 = (f32[4,48,576]{2,1,0:T(8,128)}, f32[4,48,768]{2,1,0:T(8,128)}, f32[48,768]{1,0:T(8,128)}, f32[16,256]{1,0:T(8,128)}, f32[192,768]{1,0:T(8,128)}, /*index=5*/bf16[192,768]{1,0:T(8,128)(2,1)}) custom-call(bf16[16,48,576]{2,1,0:T(8,128)(2,1)} %bitcast.131, bf16[4,48,768]{2,1,0:T(8,128)(2,1)} %bitcast.142, bf16[4,48,768]{2,1,0:T(8,128)(2,1)} %bitcast.138, ...), custom_call_target="tpu_custom_call" | custom-call | bytes 100000000 | tf_op jit(solution)/shard_map/reduce_grads/pallas_call | solution.py:37
  (253 shorter events, 66.8 us)
Async XLA Ops:
  7.2 187.0 %all-gather.3.cloned.1.call-start = ((), (), s32[]{:S(2)}) async-start(), calls=%async_computation.2 | async-start | bytes 2949120 | tf_op jit(solution)/shard_map/all_gather | solution.py:869
  7.3 4.5 %copy-start.32 = (f32[48]{0:T(128)S(1)}, f32[48]{0:T(128)}, u32[]{:S(2)}) copy-start(f32[48]{0:T(128)} %param.32) | copy-start | bytes 580
  7.3 4.5 %copy-start.33 = (f32[48]{0:T(128)S(1)}, f32[48]{0:T(128)}, u32[]{:S(2)}) copy-start(f32[48]{0:T(128)} %param.36) | copy-start | bytes 580
  7.4 4.5 %copy-start.34 = (f32[48]{0:T(128)S(1)}, f32[48]{0:T(128)}, u32[]{:S(2)}) copy-start(f32[48]{0:T(128)} %param.37) | copy-start | bytes 580
  7.4 4.6 %copy-start.35 = (f32[48]{0:T(128)S(1)}, f32[48]{0:T(128)}, u32[]{:S(2)}) copy-start(f32[48]{0:T(128)} %param.38) | copy-start | bytes 580
  7.4 4.6 %copy-start.27 = (f32[192]{0:T(256)S(1)}, f32[192]{0:T(256)}, u32[]{:S(2)}) copy-start(f32[192]{0:T(256)} %param.34) | copy-start | bytes 2308
  7.4 4.6 %copy-start.23 = (s32[1,192]{1,0:T(1,128)S(1)}, s32[1,192]{1,0:T(1,128)}, u32[]{:S(2)}) copy-start(s32[1,192]{1,0:T(1,128)} %param.23) | copy-start | bytes 2308
  7.4 4.6 %copy-start.24 = (s32[1,192]{1,0:T(1,128)S(1)}, s32[1,192]{1,0:T(1,128)}, u32[]{:S(2)}) copy-start(s32[1,192]{1,0:T(1,128)} %param.22) | copy-start | bytes 2308
  57.1 46.2 %copy-start.8 = (f32[192,768]{1,0:T(8,128)S(1)}, f32[192,768]{1,0:T(8,128)}, u32[]{:S(2)}) copy-start(f32[192,768]{1,0:T(8,128)} %param.35) | copy-start | bytes 1769476
  57.1 46.2 %copy-start.14 = (bf16[4,48,768]{2,1,0:T(8,128)(2,1)S(1)}, bf16[4,48,768]{2,1,0:T(8,128)(2,1)}, u32[]{:S(2)}) copy-start(bf16[4,48,768]{2,1,0:T(8,128)(2,1)} %get-tuple-element.91) | copy-start | bytes 884740
  104.2 229.0 %reduce-scatter.2.cloned.1.call-start = ((), (), s32[]{:S(2)}) async-start(), calls=%async_computation.1 | async-start | bytes 2949120 | tf_op jit(solution)/shard_map/reduce_scatter | solution.py:925
  105.4 5.9 %copy-start.4 = (bf16[768,192]{1,0:T(8,128)(2,1)}, bf16[768,192]{1,0:T(8,128)(2,1)S(1)}, u32[]{:S(2)}) copy-start(bf16[768,192]{1,0:T(8,128)(2,1)S(1)} %slice.168.q_ref) | copy-start | bytes 884740
  112.2 58.5 %copy-start.5 = (bf16[4,48,768]{2,1,0:T(8,128)(2,1)S(1)}, bf16[4,48,768]{2,1,0:T(8,128)(2,1)}, u32[]{:S(2)}) copy-start(bf16[4,48,768]{2,1,0:T(8,128)(2,1)} %get-tuple-element.97) | copy-start | bytes 884740
  117.0 5.1 %copy-start = (f32[3,768,768]{2,1,0:T(8,128)S(1)}, f32[3,768,768]{2,1,0:T(8,128)}, u32[]{:S(2)}) copy-start(f32[3,768,768]{2,1,0:T(8,128)} %get-tuple-element.277) | copy-start | bytes 21233668 | tf_op jit(solution)/shard_map/while
  130.9 5.1 %copy-start = (f32[3,768,768]{2,1,0:T(8,128)S(1)}, f32[3,768,768]{2,1,0:T(8,128)}, u32[]{:S(2)}) copy-start(f32[3,768,768]{2,1,0:T(8,128)} %get-tuple-element.277) | copy-start | bytes 21233668 | tf_op jit(solution)/shard_map/while
  145.0 5.0 %copy-start = (f32[3,768,768]{2,1,0:T(8,128)S(1)}, f32[3,768,768]{2,1,0:T(8,128)}, u32[]{:S(2)}) copy-start(f32[3,768,768]{2,1,0:T(8,128)} %get-tuple-element.277) | copy-start | bytes 21233668 | tf_op jit(solution)/shard_map/while
  159.1 5.0 %copy-start = (f32[3,768,768]{2,1,0:T(8,128)S(1)}, f32[3,768,768]{2,1,0:T(8,128)}, u32[]{:S(2)}) copy-start(f32[3,768,768]{2,1,0:T(8,128)} %get-tuple-element.277) | copy-start | bytes 21233668 | tf_op jit(solution)/shard_map/while
  168.4 27.7 %copy-start.20 = (f32[1,768]{1,0:T(1,128)}, f32[1,768]{1,0:T(1,128)S(1)}, u32[]{:S(2)}) copy-start(f32[1,768]{1,0:T(1,128)S(1)} %stack_reshape_squeeze.46.rest_2_) | copy-start | bytes 9220
  266.0 56.8 %copy-start.22 = (f32[8,768]{1,0:T(8,128)S(1)}, f32[8,768]{1,0:T(8,128)}, u32[]{:S(2)}) copy-start(f32[8,768]{1,0:T(8,128)} %get-tuple-element.108) | copy-start | bytes 73732
  266.0 57.2 %copy-start.21 = (f32[8,768]{1,0:T(8,128)S(1)}, f32[8,768]{1,0:T(8,128)}, u32[]{:S(2)}) copy-start(f32[8,768]{1,0:T(8,128)} %get-tuple-element.109) | copy-start | bytes 73732
  397.5 6.5 %copy-start.7 = (f32[4,48,576]{2,1,0:T(8,128)S(1)}, f32[4,48,576]{2,1,0:T(8,128)}, u32[]{:S(2)}) copy-start(f32[4,48,576]{2,1,0:T(8,128)} %get-tuple-element.112) | copy-start | bytes 1327108
  402.5 4.5 %copy-start.12 = (bf16[192,768]{1,0:T(8,128)(2,1)S(1)}, bf16[192,768]{1,0:T(8,128)(2,1)}, u32[]{:S(2)}) copy-start(bf16[192,768]{1,0:T(8,128)(2,1)} %get-tuple-element.101) | copy-start | bytes 884740
  402.5 5.2 %copy-start.13 = (bf16[192,768]{1,0:T(8,128)(2,1)S(1)}, bf16[192,768]{1,0:T(8,128)(2,1)}, u32[]{:S(2)}) copy-start(bf16[192,768]{1,0:T(8,128)(2,1)} %get-tuple-element.111) | copy-start | bytes 884740
  404.0 5.0 %copy-start.9 = (f32[192,768]{1,0:T(8,128)S(1)}, f32[192,768]{1,0:T(8,128)}, u32[]{:S(2)}) copy-start(f32[192,768]{1,0:T(8,128)} %get-tuple-element.343) | copy-start | bytes 1769476
  (21 other events, 64.8 us)
Sparse Core Ops, SparseCore 0:
  104.3 48.7 all-gather.2
  235.1 44.8 reduce-scatter.1
